TPU v7x, 768 devices: a whole 4x8x12 slice. The times are simulated.
768 devices in a mesh: dom: 192 (over y, z, core), sub: 4 (over x).
Axes of the slice: x: 4, y: 8, z: 12, core: 2. Of those that a mesh axis runs over, the one named last changes fastest.
Arguments:
- fine_partial: float32 [4, 165, 24576], P('sub', None, 'dom'), may hold values from -6 to 6
- upward_ops: float32 [8, 165, 165], replicated, may hold values from -0.15625 to 0.15625
- interaction_ops: float32 [188, 165, 165], P('sub'), may hold values from -0.03125 to 0.03125
- downward_ops: float32 [8, 165, 165], replicated, may hold values from -0.5 to 0.5
- fine_list: int32 [188, 24576], P('sub', 'dom'), may hold values from -1 to 24575, as said below
- mid_list: int32 [188, 3072], P('sub', 'dom'), may hold values from -1 to 3071, as said below
- top_list: int32 [188, 384], P('sub', 'dom'), may hold values from -1 to 383, as said below
- upper_list: int32 [188, 48], P('sub'), may hold values from -1 to 47, as said below
- positions: float32 [3, 1572864], P(None, ('dom', 'sub')), may hold values from -0.5 to 0.5
- leaf_cell: int32 [1572864], P(('dom', 'sub')), may hold values from 0 to 24575, as said below
Outputs:
- local_fine: float32 [165, 24576], P(None, 'dom')
- potential: float32 [1572864], P(('dom', 'sub'))
Inputs may be any that keep to these rules, and one draw needn't show every extreme that they name: `fine_list`: column t lists for each offset slot a cell of the finest level within 128 cells of t in Peano order, or -1 for an empty slot. `mid_list`: column t lists for each offset slot a cell of the middle level within 16 cells of t, or -1 for an empty slot. `top_list`: each entry is a cell of the top level, or -1 for an empty slot. `upper_list`: each entry is a cell of the upper level, or -1 for an empty slot. `leaf_cell`: A particle's leaf is one of the 128 finest cells owned by its own slab.
All inputs are finite; a program needn't handle non-finite values.
Results may differ from a plain program's by a relative error of at most 0.0003.
Values sent between devices are 32-bit elements; how exact they have to be, the bound alone decides.
No kernel may reach another device: no remote copies, remote signals or barrier semaphores. Data moves between devices by JAX's collectives and lax.ppermute only.
A program may use at most 128 MiB of HBM per device.

v0:
```python
import jax
import jax.numpy as jnp
from jax import lax
from jax.sharding import Mesh
from jax.sharding import PartitionSpec as P

ORDER = 8
DOM = ("dom_0", "dom_1", "dom_2")
DOM_SUB = ("dom_0", "dom_1", "dom_2", "sub")


precise = lax.Precision.HIGHEST


def sent_to_all(value, axis):
    copies = jnp.broadcast_to(value, (lax.axis_size(axis), *value.shape))
    return lax.all_to_all(copies, axis, split_axis=0, concat_axis=0, tiled=True)


def taken_together(value, axis):
    everything = sent_to_all(value, axis)
    return jnp.sum(everything, axis=0)


def gathered_total(value, axis):
    pieces = lax.all_gather(value, axis)
    return pieces.sum(axis=0)


def extended(block, sides, width):
    for axis, dim in sides:
        count = lax.axis_size(axis)
        forward = [(i, i + 1) for i in range(count - 1)]
        backward = [(target, source) for source, target in forward]
        low = lax.ppermute(
            lax.slice_in_dim(block, block.shape[dim] - width, None, axis=dim), axis, forward
        )
        high = lax.ppermute(lax.slice_in_dim(block, 0, width, axis=dim), axis, backward)
        block = jnp.concatenate([low, block, high], axis=dim)
    return block


def joined_along(pieces, dim):
    shape = list(pieces.shape[1:])
    shape[dim] *= pieces.shape[0]
    return jnp.moveaxis(pieces, 0, dim).reshape(shape)


def all_blocks(value, axes, sequence):
    pieces = value[None]
    for k in sequence:
        pieces = lax.all_gather(pieces, axes[k], axis=0, tiled=True)
    held = [lax.axis_size(axes[k]) for k in reversed(sequence)]
    pieces = pieces.reshape(*held, *value.shape)
    turned = sorted(range(len(sequence)), key=lambda place: sequence[len(sequence) - 1 - place])
    return pieces.transpose(*turned, *range(len(sequence), pieces.ndim)).reshape(-1, *value.shape)


def gathered_by_axis(value, axes, sequence, dim):
    return joined_along(all_blocks(value, axes, sequence), dim)


def exponents():
    entries = []
    for degree in range(ORDER + 1):
        for along_x in range(degree, -1, -1):
            for along_y in range(degree - along_x, -1, -1):
                entries.append((along_x, along_y, degree - along_x - along_y))
    return entries


def monomial_rows(coords):
    powers = [jnp.ones_like(coords)]
    for degree in range(ORDER):
        powers.append(powers[-1] * coords)
    rows = []
    for triple in exponents():
        rows.append(powers[triple[0]][0] * powers[triple[1]][1] * powers[triple[2]][2])
    return jnp.stack(rows, axis=1)


def upward(moments, upward_ops):
    parents = moments.shape[1] // 8
    grouped = moments.reshape(moments.shape[0], parents, 8)
    return jnp.einsum("oab,bpo->ap", upward_ops, grouped, precision=precise)


def downward(expansions, downward_ops):
    spread = jnp.einsum("oab,bp->apo", downward_ops, expansions, precision=precise)
    return spread.reshape(spread.shape[0], -1)


def interact_local(moments, sources, anchor, flat_ops):
    coeffs, columns = moments.shape
    cell_rows = jnp.concatenate(
        [jnp.transpose(moments), jnp.zeros((1, coeffs), jnp.float32)], axis=0
    )
    shifted = jnp.where(sources >= 0, jnp.clip(sources - anchor, 0, columns - 1), columns)
    picked = jnp.take(cell_rows, jnp.transpose(shifted), axis=0)
    stacked = picked.reshape(picked.shape[0], picked.shape[1] * picked.shape[2])
    result = jnp.dot(stacked, flat_ops, precision=precise, preferred_element_type=jnp.float32)
    return jnp.transpose(result)


def settle(portion, each_level):
    if each_level:
        return taken_together(portion, "sub")
    return portion


def shards(
    fine_partial,
    upward_ops,
    interaction_ops,
    downward_ops,
    fine_list,
    mid_list,
    top_list,
    upper_list,
    positions,
    leaf_cell,
):
    slab_cells = fine_partial.shape[2]
    mid_cells = slab_cells // 8
    top_cells = slab_cells // 64
    domain = lax.axis_index(DOM)
    coeffs = interaction_ops.shape[1]
    flat_ops = jnp.transpose(interaction_ops, (0, 2, 1)).reshape(-1, coeffs)
    fine_moments = gathered_total(fine_partial[0], "sub")
    wide_fine = extended(fine_moments, ((DOM, 1),), slab_cells)
    wide_mid = upward(wide_fine, upward_ops)
    mid_moments = wide_mid[:, mid_cells : 2 * mid_cells]
    own_top = upward(mid_moments, upward_ops)
    top_moments = gathered_by_axis(own_top, DOM, (0, 1, 2), 1)
    upper_moments = upward(top_moments, upward_ops)
    upper_span = max(1, top_cells // 8)
    upper_first = domain * top_cells // 8
    upper_sources = lax.dynamic_slice_in_dim(upper_list, upper_first, upper_span, 1)
    local_upper = settle(interact_local(upper_moments, upper_sources, 0, flat_ops), False)
    down_top = downward(local_upper, downward_ops)
    top_offset = domain * top_cells % 8
    local_top = settle(interact_local(top_moments, top_list, 0, flat_ops), False)
    local_top = local_top + lax.dynamic_slice_in_dim(down_top, top_offset, top_cells, 1)
    local_mid = settle(
        interact_local(wide_mid, mid_list, domain * mid_cells - mid_cells, flat_ops), False
    )
    local_mid = local_mid + downward(local_top, downward_ops)
    local_fine = settle(
        interact_local(wide_fine, fine_list, domain * slab_cells - slab_cells, flat_ops), False
    )
    local_fine = local_fine + downward(local_mid, downward_ops)
    local_fine = settle(local_fine, True)
    fine_rows = jnp.transpose(local_fine)
    leaves = leaf_cell - domain * slab_cells
    particles = positions.shape[1]
    block_size = min(particles, 4096)

    def evaluate(block_index):
        picked = jnp.take(fine_rows, leaves, axis=0)
        return jnp.sum(picked * monomial_rows(positions), axis=1)

    potential = lax.map(evaluate, jnp.arange(particles // block_size, dtype=jnp.int32)).reshape(-1)
    return (local_fine, potential)


def solution(mesh):
    torus = Mesh(
        mesh.devices.reshape(8, 12, 2, mesh.shape["sub"]), ("dom_0", "dom_1", "dom_2", "sub")
    )
    return jax.shard_map(
        shards,
        mesh=torus,
        in_specs=(
            P("sub", None, DOM),
            P(),
            P("sub", None, None),
            P(),
            P("sub", DOM),
            P("sub", DOM),
            P("sub", DOM),
            P("sub", None),
            P(None, DOM_SUB),
            P(DOM_SUB),
        ),
        out_specs=(P(None, DOM), P(DOM_SUB)),
        check_vma=False,
    )
```

profile of v0, /device:TPU:1, one launch (start us, length us, event | category | flops | bytes accessed | tf_op | source)
XLA Modules:
  0.0 237.7 jit_solution(7364206148183296190)
XLA Ops:
  0.7 1.0 copy.1110
  1.7 10.7 %all_gather.12 = f32[4,165,128]{2,1,0:T(8,128)S(1)} all-gather(f32[1,165,128]{2,1,0:T(8,128)S(1)} %copy.1110), channel_id=1, replica_groups=mesh['dom_0'=8,'dom_1'=12,'dom_2'=2,'sub'=4] {'sub'}, dimensions={0}, use_global_device_ids=true | all-gather | bytes 422400 | tf_op jit(solution)/shard_map/all_gather | solution.py:26
  12.5 7.4 %collective-permute-start = (f32[165,128]{0,1:T(8,128)S(1)}, f32[165,128]{0,1:T(8,128)S(1)}, u32[]{:S(2)}, u32[]{:S(2)}) collective-permute-start(f32[165,128]{0,1:T(8,128)S(1)} %copy.1112), channel_id=1, source_target_pairs={{0,4},{4,8},{8,12},{12,16},{16,20},{20,24},{24,28},{28,32},{32,36}... | collective-permute-start | bytes 253448 | tf_op jit(solution)/shard_map/ppermute | solution.py:35
  19.9 8.0 %collective-permute-start.1 = (f32[165,128]{0,1:T(8,128)S(1)}, f32[165,128]{0,1:T(8,128)S(1)}, u32[]{:S(2)}, u32[]{:S(2)}) collective-permute-start(f32[165,128]{0,1:T(8,128)S(1)} %copy.1112), channel_id=1, source_target_pairs={{4,0},{8,4},{12,8},{16,12},{20,16},{24,20},{28,24},{32,28},{36,32}... | collective-permute-start | bytes 253448 | tf_op jit(solution)/shard_map/ppermute | solution.py:38
  27.9 0.9 select_reduce_fusion
  28.9 0.6 compare_and_fusion.3
  29.5 0.8 fusion.53
  30.3 0.7 fusion.128
  31.0 0.7 fusion.160
  31.7 0.7 fusion.175
  32.4 0.7 fusion.174
  33.1 0.7 fusion.71
  33.8 0.7 fusion.100
  34.5 0.7 fusion.68
  35.2 0.7 fusion.107
  35.9 0.6 slice_bitcast_fusion.13
  36.5 0.6 slice_bitcast_fusion.7
  37.1 0.6 slice_bitcast_fusion.19
  37.8 0.6 pad_clamp_fusion.1
  38.4 9.1 %copy.1128 = f32[47,165,165]{1,0,2:T(8,128)} copy(f32[47,165,165]{1,2,0:T(8,128)} %bitcast.649) | data formatting | bytes 10236600 | tf_op jit(solution)/shard_map/transpose | solution.py:128
  47.5 8.6 %reshape.2613 = f32[7755,165]{0,1:T(8,128)} reshape(f32[47,165,165]{1,0,2:T(8,128)} %copy.1128) | data formatting | bytes 10236600 | tf_op jit(solution)/shard_map/reshape | solution.py:128
  56.1 0.6 compare_and_fusion.4
  56.8 0.6 pad_clamp_fusion.2
  57.4 0.6 compare_and_fusion.2
  58.0 0.7 reshape.2627
  58.7 0.6 compare_and_fusion
  59.6 1.4 copy.1109
  61.0 0.7 fusion.85
  61.7 0.7 fusion.104
  62.4 0.7 fusion.163
  63.1 0.7 fusion.152
  63.8 0.7 fusion.58
  64.5 0.6 slice_bitcast_fusion.1
  65.1 1.4 fusion.138
  66.5 1.3 pad_clamp_fusion.3
  67.8 0.8 fusion.40
  68.6 1.7 fusion.12
  70.3 1.4 fusion.33
  71.7 15.6 %all-gather.1 = f32[8,165,2]{1,2,0:T(2,128)S(1)} all-gather(f32[1,165,2]{1,2,0:T(2,128)S(1)} %fusion.33), channel_id=2, replica_groups=mesh['dom_0'=8,'dom_1'=12,'dom_2'=2,'sub'=4] {'dom_0'}, dimensions={0}, use_global_device_ids=true | all-gather | bytes 11880 | tf_op jit(solution)/shard_map/all_gather | solution.py:52
  87.3 22.7 %all_gather.14 = f32[96,165,2]{1,2,0:T(2,128)S(1)} all-gather(f32[8,165,2]{1,2,0:T(2,128)S(1)} %all-gather.1), channel_id=1, replica_groups=mesh['dom_0'=8,'dom_1'=12,'dom_2'=2,'sub'=4] {'dom_1'}, dimensions={0}, use_global_device_ids=true | all-gather | bytes 137280 | tf_op jit(solution)/shard_map/all_gather | solution.py:52
  110.0 14.7 %all_gather.15 = f32[192,165,2]{1,2,0:T(2,128)S(1)} all-gather(f32[96,165,2]{1,2,0:T(2,128)S(1)} %all_gather.14), channel_id=1, replica_groups=mesh['dom_0'=8,'dom_1'=12,'dom_2'=2,'sub'=4] {'dom_2'}, dimensions={0}, use_global_device_ids=true | all-gather | bytes 380160 | tf_op jit(solution)/shard_map/all_gather | solution.py:52
  124.8 0.3 reshape_reshape.3
  125.1 1.0 reshape.2612
  126.1 1.7 fusion.23
  127.8 0.7 gather_fusion.3
  128.9 6.4 %convolution_bitcast_fusion.2 = f32[165,1,1]{0,1,2:T(1,128)S(1)} fusion(f32[7755,1]{0,1:T(1,128)S(1)} %reshape.2675, f32[7755,165]{0,1:T(8,128)} %reshape.2613), kind=kOutput, calls=%fused_computation.33 | convolution fusion | flops 15354900 | bytes 5149980 | tf_op jit(solution)/shard_map/dot_general | solution.py:101
  135.3 1.5 fusion.2
  136.9 0.8 gather_fusion.2
  137.9 8.8 %fusion.32 = f32[165,2,1]{0,1,2:T(2,128)S(1)} fusion(f32[2,47,165]{2,1,0:T(8,128)S(1)} %broadcast_select_fusion.2, f32[8,165]{1,0:T(8,128)S(1)} %bitcast.657, s32[]{:T(128)S(6)} %select_n.135, f32[47,165,165]{2,1,0:T(8,128)} %param.12), kind=kOutput, calls=%fused_computation.31 | convolution fusion | flops 30710130 | bytes 5182984 | tf_op jit(solution)/shard_map/dot_general | solution.py:101
  146.7 1.5 fusion.28
  148.3 2.3 gather_fusion.1
  150.8 9.0 %fusion.27 = f32[165,16,1]{0,1,2:T(8,128)S(1)} fusion(f32[16,47,165]{2,1,0:T(8,128)S(1)} %broadcast_select_fusion.1, f32[165,2,8]{0,1,2:T(2,128)S(1)} %fusion.28, f32[47,165,165]{2,1,0:T(8,128)} %param.12), kind=kOutput, calls=%fused_computation.27 | convolution fusion | flops 245681040 | bytes 5635740 | tf_op jit(solution)/shard_map/dot_general | solution.py:101
  159.9 1.5 fusion.14
  161.7 15.4 %gather_fusion = f32[6016,165]{1,0:T(8,128)} fusion(f32[385,165]{1,0:T(8,128)S(1)} %concatenate.16, s32[6144]{0:T(1024)S(1)} %pad_clamp_fusion), kind=kCustom, calls=%fused_computation | custom fusion | bytes 7965184 | tf_op jit(solution)/shard_map/jit(_take)/gather | solution.py:99
  177.1 7.2 %reshape.2618 = f32[128,47,165]{2,1,0:T(8,128)} reshape(f32[6016,165]{1,0:T(8,128)} %gather_fusion) | data formatting | bytes 7941120 | tf_op jit(solution)/shard_map/jit(_take)/gather | solution.py:99
  184.3 4.0 %broadcast_select_fusion = f32[128,47,165]{2,1,0:T(8,128)S(1)} fusion(f32[128,47,165]{2,1,0:T(8,128)} %reshape.2618, pred[128,47]{1,0:T(8,128)(4,1)S(1)} %copy-done.27), kind=kLoop, calls=%fused_computation.7 | loop fusion | flops 992640 | bytes 7947136 | tf_op jit(solution)/shard_map/jit(_take)/select_n | solution.py:99
  188.6 11.4 %fusion.20 = f32[165,128]{1,0:T(8,128)S(1)} fusion(f32[165,128]{1,0:T(8,128)S(1)} %copy.1133, f32[128,47,165]{2,1,0:T(8,128)S(1)} %broadcast_select_fusion, f32[47,165,165]{2,1,0:T(8,128)} %param.12), kind=kOutput, calls=%fused_computation.23 | convolution fusion | flops 1965448320 | bytes 9257820 | tf_op jit(solution)/shard_map/dot_general | solution.py:101
  200.0 0.8 broadcast_in_dim.103
  200.8 3.6 %all-to-all-start = ((f32[4,165,128]{2,1,0:T(8,128)}), f32[4,165,128]{2,1,0:T(8,128)S(1)}, u32[]{:S(2)}, u32[]{:S(2)}) async-start(f32[4,165,128]{2,1,0:T(8,128)} %broadcast_in_dim.103), calls=%async_computation | async-start | bytes 688128 | tf_op jit(solution)/shard_map/all_to_all | solution.py:17
  204.4 0.8 compare_and_fusion.1
  205.6 18.4 %stack.284 = f32[2048,165]{0,1:T(8,128)S(1)} concatenate(f32[2048,1]{0,1:T(1,128)S(1)} %broadcast.99, f32[2048,1]{0,1:T(1,128)} %get-tuple-element.259, f32[2048,1]{0,1:T(1,128)} %get-tuple-element.260, f32[2048,1]{0,1:T(1,128)} %get-tuple-element.261, f32[2048,1]{0,1:T(1,128)} %get-tuple-element.245, f32[2048,1]{0,1:T(1,128)S(1)} %get-tuple-element.116, ...), dimensions={1} | concatenate | bytes 2703360 | tf_op jit(solution)/shard_map/while/body/eval_jaxpr/stack | solution.py:79
  224.1 8.6 %gather_fusion.4 = f32[2048,165]{1,0:T(8,128)} fusion(f32[128,165]{1,0:T(8,128)S(1)} %bitcast.648, s32[2048]{0:T(1024)S(1)} %fusion.44), kind=kCustom, calls=%fused_computation.4 | custom fusion | bytes 2711552 | tf_op jit(solution)/shard_map/while/body/eval_jaxpr/jit(_take)/gather | solution.py:159
  232.8 2.8 %copy.1136 = f32[2048,165]{0,1:T(8,128)} copy(f32[2048,165]{1,0:T(8,128)} %gather_fusion.4) | data formatting | bytes 2703360 | tf_op jit(solution)/shard_map/while/body/eval_jaxpr/jit(_take)/gather | solution.py:159
  235.5 2.2 multiply_reduce_fusion
  (159 shorter events, 2.0 us)
Async XLA Ops:
  0.6 134.7 %copy-start = (f32[8,165,165]{2,0,1:T(8,128)S(1)}, f32[8,165,165]{2,0,1:T(8,128)}, u32[]{:S(2)}) copy-start(f32[8,165,165]{2,0,1:T(8,128)} %param.13) | copy-start | bytes 2613604
  0.6 31.0 %copy-start.2 = (f32[3,2048]{1,0:T(4,128)S(1)}, f32[3,2048]{1,0:T(4,128)}, u32[]{:S(2)}) copy-start(f32[3,2048]{1,0:T(4,128)} %param.18) | copy-start | bytes 73732
  12.5 55.3 %collective-permute-start = (f32[165,128]{0,1:T(8,128)S(1)}, f32[165,128]{0,1:T(8,128)S(1)}, u32[]{:S(2)}, u32[]{:S(2)}) collective-permute-start(f32[165,128]{0,1:T(8,128)S(1)} %copy.1112), channel_id=1, source_target_pairs={{0,4},{4,8},{8,12},{12,16},{16,20},{20,24},{24,28},{28,32},{32,36}... | collective-permute-start | bytes 253448 | tf_op jit(solution)/shard_map/ppermute | solution.py:35
  19.9 47.9 %collective-permute-start.1 = (f32[165,128]{0,1:T(8,128)S(1)}, f32[165,128]{0,1:T(8,128)S(1)}, u32[]{:S(2)}, u32[]{:S(2)}) collective-permute-start(f32[165,128]{0,1:T(8,128)S(1)} %copy.1112), channel_id=1, source_target_pairs={{4,0},{8,4},{12,8},{16,12},{20,16},{24,20},{28,24},{32,28},{36,32}... | collective-permute-start | bytes 253448 | tf_op jit(solution)/shard_map/ppermute | solution.py:38
  31.0 34.2 %copy-start.16 = (f32[2048,1]{0,1:T(1,128)}, f32[2048,1]{0,1:T(1,128)S(1)}, u32[]{:S(2)}) copy-start(f32[2048,1]{0,1:T(1,128)S(1)} %get-tuple-element.139) | copy-start | bytes 24580
  31.0 34.2 %copy-start.18 = (f32[2048,1]{0,1:T(1,128)}, f32[2048,1]{0,1:T(1,128)S(1)}, u32[]{:S(2)}) copy-start(f32[2048,1]{0,1:T(1,128)S(1)} %get-tuple-element.141) | copy-start | bytes 24580
  31.7 30.7 %copy-start.8 = (f32[2048,1]{0,1:T(1,128)}, f32[2048,1]{0,1:T(1,128)S(1)}, u32[]{:S(2)}) copy-start(f32[2048,1]{0,1:T(1,128)S(1)} %get-tuple-element.148) | copy-start | bytes 24580
  31.7 30.7 %copy-start.22 = (f32[2048,1]{0,1:T(1,128)}, f32[2048,1]{0,1:T(1,128)S(1)}, u32[]{:S(2)}) copy-start(f32[2048,1]{0,1:T(1,128)S(1)} %get-tuple-element.151) | copy-start | bytes 24580
  31.7 33.5 %copy-start.20 = (f32[2048,1]{0,1:T(1,128)}, f32[2048,1]{0,1:T(1,128)S(1)}, u32[]{:S(2)}) copy-start(f32[2048,1]{0,1:T(1,128)S(1)} %get-tuple-element.50) | copy-start | bytes 24580
  32.4 30.0 %copy-start.10 = (f32[2048,1]{0,1:T(1,128)}, f32[2048,1]{0,1:T(1,128)S(1)}, u32[]{:S(2)}) copy-start(f32[2048,1]{0,1:T(1,128)S(1)} %get-tuple-element.88) | copy-start | bytes 24580
  32.4 30.7 %copy-start.12 = (f32[2048,1]{0,1:T(1,128)}, f32[2048,1]{0,1:T(1,128)S(1)}, u32[]{:S(2)}) copy-start(f32[2048,1]{0,1:T(1,128)S(1)} %get-tuple-element.90) | copy-start | bytes 24580
  32.4 30.7 %copy-start.14 = (f32[2048,1]{0,1:T(1,128)}, f32[2048,1]{0,1:T(1,128)S(1)}, u32[]{:S(2)}) copy-start(f32[2048,1]{0,1:T(1,128)S(1)} %get-tuple-element.92) | copy-start | bytes 24580
  33.1 30.0 %copy-start.24 = (f32[2048,1]{0,1:T(1,128)}, f32[2048,1]{0,1:T(1,128)S(1)}, u32[]{:S(2)}) copy-start(f32[2048,1]{0,1:T(1,128)S(1)} %get-tuple-element.78) | copy-start | bytes 24580
  47.5 8.6 %copy-start.63 = (s32[47,2]{0,1:T(2,128)S(1)}, s32[47,2]{0,1:T(2,128)}, u32[]{:S(2)}) copy-start(s32[47,2]{0,1:T(2,128)} %param.16) | copy-start | bytes 1132
  47.5 9.9 %copy-start.61 = (s32[47,16]{0,1:T(8,128)S(1)}, s32[47,16]{0,1:T(8,128)}, u32[]{:S(2)}) copy-start(s32[47,16]{0,1:T(8,128)} %param.15) | copy-start | bytes 9028
  47.5 11.2 %copy-start.59 = (s32[47,128]{1,0:T(8,128)S(1)}, s32[47,128]{1,0:T(8,128)}, u32[]{:S(2)}) copy-start(s32[47,128]{1,0:T(8,128)} %param.14) | copy-start | bytes 72196
  56.1 12.5 %copy-start.1 = (f32[8,165,165]{2,0,1:T(8,128)S(1)}, f32[8,165,165]{2,0,1:T(8,128)}, u32[]{:S(2)}) copy-start(f32[8,165,165]{2,0,1:T(8,128)} %param.11) | copy-start | bytes 2613604
  70.3 54.3 %copy-start.6 = (f32[48,165,1]{1,0,2:T(8,128)}, f32[48,165,1]{1,0,2:T(8,128)S(1)}, u32[]{:S(2)}) copy-start(f32[48,165,1]{1,0,2:T(8,128)S(1)} %fusion.12) | copy-start | bytes 95044
  126.1 2.5 %copy-start.64 = (pred[47]{0:T(512)(128)(4,1)S(1)}, pred[47]{0:T(512)(128)(4,1)}, u32[]{:S(2)}) copy-start(pred[47]{0:T(512)(128)(4,1)} %compare_and_fusion.3) | copy-start | bytes 145
  137.9 10.3 %copy-start.7 = (f32[48,165,1]{1,0,2:T(8,128)S(1)}, f32[48,165,1]{1,0,2:T(8,128)}, u32[]{:S(2)}) copy-start(f32[48,165,1]{1,0,2:T(8,128)} %copy-done.6) | copy-start | bytes 95044
  137.9 10.4 %copy-start.28 = (s32[1024]{0:T(1024)S(1)}, s32[1024]{0:T(1024)}, u32[]{:S(2)}) copy-start(s32[1024]{0:T(1024)} %pad_clamp_fusion.3) | copy-start | bytes 12292
  177.1 7.2 %copy-start.27 = (pred[128,47]{1,0:T(8,128)(4,1)S(1)}, pred[128,47]{1,0:T(8,128)(4,1)}, u32[]{:S(2)}) copy-start(pred[128,47]{1,0:T(8,128)(4,1)} %copy.1109) | copy-start | bytes 18052
  188.3 16.9 %copy-start.9 = (f32[2048,1]{0,1:T(1,128)S(1)}, f32[2048,1]{0,1:T(1,128)}, u32[]{:S(2)}) copy-start(f32[2048,1]{0,1:T(1,128)} %copy-done.8) | copy-start | bytes 24580
  188.3 16.9 %copy-start.11 = (f32[2048,1]{0,1:T(1,128)S(1)}, f32[2048,1]{0,1:T(1,128)}, u32[]{:S(2)}) copy-start(f32[2048,1]{0,1:T(1,128)} %copy-done.10) | copy-start | bytes 24580
  188.3 16.9 %copy-start.13 = (f32[2048,1]{0,1:T(1,128)S(1)}, f32[2048,1]{0,1:T(1,128)}, u32[]{:S(2)}) copy-start(f32[2048,1]{0,1:T(1,128)} %copy-done.12) | copy-start | bytes 24580
  188.3 16.9 %copy-start.15 = (f32[2048,1]{0,1:T(1,128)S(1)}, f32[2048,1]{0,1:T(1,128)}, u32[]{:S(2)}) copy-start(f32[2048,1]{0,1:T(1,128)} %copy-done.14) | copy-start | bytes 24580
  188.3 16.9 %copy-start.17 = (f32[2048,1]{0,1:T(1,128)S(1)}, f32[2048,1]{0,1:T(1,128)}, u32[]{:S(2)}) copy-start(f32[2048,1]{0,1:T(1,128)} %copy-done.16) | copy-start | bytes 24580
  188.3 16.9 %copy-start.19 = (f32[2048,1]{0,1:T(1,128)S(1)}, f32[2048,1]{0,1:T(1,128)}, u32[]{:S(2)}) copy-start(f32[2048,1]{0,1:T(1,128)} %copy-done.18) | copy-start | bytes 24580
  188.3 16.9 %copy-start.21 = (f32[2048,1]{0,1:T(1,128)S(1)}, f32[2048,1]{0,1:T(1,128)}, u32[]{:S(2)}) copy-start(f32[2048,1]{0,1:T(1,128)} %copy-done.20) | copy-start | bytes 24580
  188.3 16.9 %copy-start.23 = (f32[2048,1]{0,1:T(1,128)S(1)}, f32[2048,1]{0,1:T(1,128)}, u32[]{:S(2)}) copy-start(f32[2048,1]{0,1:T(1,128)} %copy-done.22) | copy-start | bytes 24580
  188.3 16.9 %copy-start.25 = (f32[2048,1]{0,1:T(1,128)S(1)}, f32[2048,1]{0,1:T(1,128)}, u32[]{:S(2)}) copy-start(f32[2048,1]{0,1:T(1,128)} %copy-done.24) | copy-start | bytes 24580
  188.3 16.9 %copy-start.26 = (f32[2048,1]{0,1:T(1,128)S(1)}, f32[2048,1]{0,1:T(1,128)}, u32[]{:S(2)}) copy-start(f32[2048,1]{0,1:T(1,128)} %get-tuple-element.82) | copy-start | bytes 24580
  188.4 16.9 %copy-start.29 = (f32[2048,1]{0,1:T(1,128)S(1)}, f32[2048,1]{0,1:T(1,128)}, u32[]{:S(2)}) copy-start(f32[2048,1]{0,1:T(1,128)} %get-tuple-element.135) | copy-start | bytes 24580
  188.4 16.9 %copy-start.30 = (f32[2048,1]{0,1:T(1,128)S(1)}, f32[2048,1]{0,1:T(1,128)}, u32[]{:S(2)}) copy-start(f32[2048,1]{0,1:T(1,128)} %get-tuple-element.136) | copy-start | bytes 24580
  188.4 16.9 %copy-start.31 = (f32[2048,1]{0,1:T(1,128)S(1)}, f32[2048,1]{0,1:T(1,128)}, u32[]{:S(2)}) copy-start(f32[2048,1]{0,1:T(1,128)} %get-tuple-element.137) | copy-start | bytes 24580
  188.4 16.9 %copy-start.32 = (f32[2048,1]{0,1:T(1,128)S(1)}, f32[2048,1]{0,1:T(1,128)}, u32[]{:S(2)}) copy-start(f32[2048,1]{0,1:T(1,128)} %get-tuple-element.138) | copy-start | bytes 24580
  188.4 16.9 %copy-start.33 = (f32[2048,1]{0,1:T(1,128)S(1)}, f32[2048,1]{0,1:T(1,128)}, u32[]{:S(2)}) copy-start(f32[2048,1]{0,1:T(1,128)} %get-tuple-element.140) | copy-start | bytes 24580
  188.4 16.9 %copy-start.34 = (f32[2048,1]{0,1:T(1,128)S(1)}, f32[2048,1]{0,1:T(1,128)}, u32[]{:S(2)}) copy-start(f32[2048,1]{0,1:T(1,128)} %get-tuple-element.142) | copy-start | bytes 24580
  188.4 16.9 %copy-start.35 = (f32[2048,1]{0,1:T(1,128)S(1)}, f32[2048,1]{0,1:T(1,128)}, u32[]{:S(2)}) copy-start(f32[2048,1]{0,1:T(1,128)} %get-tuple-element.144) | copy-start | bytes 24580
  188.4 16.9 %copy-start.36 = (f32[2048,1]{0,1:T(1,128)S(1)}, f32[2048,1]{0,1:T(1,128)}, u32[]{:S(2)}) copy-start(f32[2048,1]{0,1:T(1,128)} %get-tuple-element.192) | copy-start | bytes 24580
  188.4 16.9 %copy-start.37 = (f32[2048,1]{0,1:T(1,128)S(1)}, f32[2048,1]{0,1:T(1,128)}, u32[]{:S(2)}) copy-start(f32[2048,1]{0,1:T(1,128)} %get-tuple-element.49) | copy-start | bytes 24580
  188.4 16.9 %copy-start.38 = (f32[2048,1]{0,1:T(1,128)S(1)}, f32[2048,1]{0,1:T(1,128)}, u32[]{:S(2)}) copy-start(f32[2048,1]{0,1:T(1,128)} %get-tuple-element.145) | copy-start | bytes 24580
  188.5 16.9 %copy-start.39 = (f32[2048,1]{0,1:T(1,128)S(1)}, f32[2048,1]{0,1:T(1,128)}, u32[]{:S(2)}) copy-start(f32[2048,1]{0,1:T(1,128)} %get-tuple-element.146) | copy-start | bytes 24580
  188.5 16.9 %copy-start.40 = (f32[2048,1]{0,1:T(1,128)S(1)}, f32[2048,1]{0,1:T(1,128)}, u32[]{:S(2)}) copy-start(f32[2048,1]{0,1:T(1,128)} %get-tuple-element.147) | copy-start | bytes 24580
  188.5 16.9 %copy-start.41 = (f32[2048,1]{0,1:T(1,128)S(1)}, f32[2048,1]{0,1:T(1,128)}, u32[]{:S(2)}) copy-start(f32[2048,1]{0,1:T(1,128)} %get-tuple-element.149) | copy-start | bytes 24580
  188.5 16.9 %copy-start.42 = (f32[2048,1]{0,1:T(1,128)S(1)}, f32[2048,1]{0,1:T(1,128)}, u32[]{:S(2)}) copy-start(f32[2048,1]{0,1:T(1,128)} %get-tuple-element.150) | copy-start | bytes 24580
  188.5 16.9 %copy-start.43 = (f32[2048,1]{0,1:T(1,128)S(1)}, f32[2048,1]{0,1:T(1,128)}, u32[]{:S(2)}) copy-start(f32[2048,1]{0,1:T(1,128)} %get-tuple-element.152) | copy-start | bytes 24580
  188.5 16.9 %copy-start.44 = (f32[2048,1]{0,1:T(1,128)S(1)}, f32[2048,1]{0,1:T(1,128)}, u32[]{:S(2)}) copy-start(f32[2048,1]{0,1:T(1,128)} %get-tuple-element.233) | copy-start | bytes 24580
  188.5 16.9 %copy-start.45 = (f32[2048,1]{0,1:T(1,128)S(1)}, f32[2048,1]{0,1:T(1,128)}, u32[]{:S(2)}) copy-start(f32[2048,1]{0,1:T(1,128)} %get-tuple-element.113) | copy-start | bytes 24580
  188.5 16.9 %copy-start.46 = (f32[2048,1]{0,1:T(1,128)S(1)}, f32[2048,1]{0,1:T(1,128)}, u32[]{:S(2)}) copy-start(f32[2048,1]{0,1:T(1,128)} %get-tuple-element.114) | copy-start | bytes 24580
  188.5 16.9 %copy-start.47 = (f32[2048,1]{0,1:T(1,128)S(1)}, f32[2048,1]{0,1:T(1,128)}, u32[]{:S(2)}) copy-start(f32[2048,1]{0,1:T(1,128)} %get-tuple-element.115) | copy-start | bytes 24580
  188.5 16.9 %copy-start.48 = (f32[2048,1]{0,1:T(1,128)S(1)}, f32[2048,1]{0,1:T(1,128)}, u32[]{:S(2)}) copy-start(f32[2048,1]{0,1:T(1,128)} %get-tuple-element.117) | copy-start | bytes 24580
  188.6 16.9 %copy-start.49 = (f32[2048,1]{0,1:T(1,128)S(1)}, f32[2048,1]{0,1:T(1,128)}, u32[]{:S(2)}) copy-start(f32[2048,1]{0,1:T(1,128)} %get-tuple-element.118) | copy-start | bytes 24580
  188.6 16.9 %copy-start.50 = (f32[2048,1]{0,1:T(1,128)S(1)}, f32[2048,1]{0,1:T(1,128)}, u32[]{:S(2)}) copy-start(f32[2048,1]{0,1:T(1,128)} %get-tuple-element.119) | copy-start | bytes 24580
  188.6 16.9 %copy-start.51 = (f32[2048,1]{0,1:T(1,128)S(1)}, f32[2048,1]{0,1:T(1,128)}, u32[]{:S(2)}) copy-start(f32[2048,1]{0,1:T(1,128)} %get-tuple-element.120) | copy-start | bytes 24580
  188.6 16.9 %copy-start.52 = (f32[2048,1]{0,1:T(1,128)S(1)}, f32[2048,1]{0,1:T(1,128)}, u32[]{:S(2)}) copy-start(f32[2048,1]{0,1:T(1,128)} %get-tuple-element.121) | copy-start | bytes 24580
  188.6 16.9 %copy-start.53 = (f32[2048,1]{0,1:T(1,128)S(1)}, f32[2048,1]{0,1:T(1,128)}, u32[]{:S(2)}) copy-start(f32[2048,1]{0,1:T(1,128)} %get-tuple-element.122) | copy-start | bytes 24580
  188.6 16.9 %copy-start.54 = (f32[2048,1]{0,1:T(1,128)S(1)}, f32[2048,1]{0,1:T(1,128)}, u32[]{:S(2)}) copy-start(f32[2048,1]{0,1:T(1,128)} %get-tuple-element.201) | copy-start | bytes 24580
  188.6 16.9 %copy-start.55 = (f32[2048,1]{0,1:T(1,128)S(1)}, f32[2048,1]{0,1:T(1,128)}, u32[]{:S(2)}) copy-start(f32[2048,1]{0,1:T(1,128)} %get-tuple-element.105) | copy-start | bytes 24580
  188.6 16.9 %copy-start.56 = (f32[2048,1]{0,1:T(1,128)S(1)}, f32[2048,1]{0,1:T(1,128)}, u32[]{:S(2)}) copy-start(f32[2048,1]{0,1:T(1,128)} %get-tuple-element.106) | copy-start | bytes 24580
  188.6 16.9 %copy-start.57 = (f32[2048,1]{0,1:T(1,128)S(1)}, f32[2048,1]{0,1:T(1,128)}, u32[]{:S(2)}) copy-start(f32[2048,1]{0,1:T(1,128)} %get-tuple-element.107) | copy-start | bytes 24580
  200.8 23.2 %all-to-all-start = ((f32[4,165,128]{2,1,0:T(8,128)}), f32[4,165,128]{2,1,0:T(8,128)S(1)}, u32[]{:S(2)}, u32[]{:S(2)}) async-start(f32[4,165,128]{2,1,0:T(8,128)} %broadcast_in_dim.103), calls=%async_computation | async-start | bytes 688128 | tf_op jit(solution)/shard_map/all_to_all | solution.py:17
  204.4 19.6 %copy-start.58 = (s32[2048]{0:T(1024)S(1)}, s32[2048]{0:T(1024)}, u32[]{:S(2)}) copy-start(s32[2048]{0:T(1024)} %param.19) | copy-start | bytes 24580
  224.0 8.7 %copy-start.5 = (f32[165,128]{1,0:T(8,128)}, f32[165,128]{1,0:T(8,128)S(1)}, u32[]{:S(2)}) copy-start(f32[165,128]{1,0:T(8,128)S(1)} %reduce_sum.29) | copy-start | bytes 253444
  (4 other events, 8.2 us)
where the time goes:
time: 240 us; the launch traced here: 238 us
  local copies, waits for them, and re-layouts  83.3 us (35%)
  blocking collectives  63.6 us (26%)
  matrix products  45 us (19%)
  other arithmetic  25 us (10%)
  starting transfers between devices  19 us (8%)
    all_gather x3, blocking collectives, all_blocks(): pieces = lax.all_gather(pieces, axes[k], axis=0, tiled=True)  52.9 us
    dot_general x4, matrix products, interact_local(): jnp.dot(stacked, flat_ops, precision=precise, preferred_element_type=jnp....  35.6 us
    gather x7, local copies, waits for them, and re-layouts, interact_local(): picked = jnp.take(cell_rows, jnp.transpose(shifted), axis=0)  26.6 us
    another operation x1, local copies, waits for them, and re-layouts, monomial_rows(): return jnp.stack(rows, axis=1)  18.4 us
    gather x2, local copies, waits for them, and re-layouts, evaluate(): picked = jnp.take(fine_rows, leaves, axis=0)  11.4 us
    all_gather x1, blocking collectives, gathered_total(): pieces = lax.all_gather(value, axis)  10.7 us
    mul x14, other arithmetic, monomial_rows(): powers[triple[0]][0] * powers[triple[1]][1] * powers[triple[2]][2]  10.4 us
    transpose x1, local copies, waits for them, and re-layouts, shards(): flat_ops = jnp.transpose(interaction_ops, (0, 2, 1)).reshape(-1, coeffs)  9.13 us
  transfers between devices with their start and end apart: 3, of which 0 were waited for; matrix products, arithmetic and copies ran while one was open for 25% of the time, Pallas kernels for 0%

commit v1 on v0

--- a/solution.py
+++ b/solution.py
@@ -22,11 +22,6 @@
     return jnp.sum(everything, axis=0)
 
 
-def gathered_total(value, axis):
-    pieces = lax.all_gather(value, axis)
-    return pieces.sum(axis=0)
-
-
 def extended(block, sides, width):
     for axis, dim in sides:
         count = lax.axis_size(axis)
@@ -38,26 +33,6 @@
         high = lax.ppermute(lax.slice_in_dim(block, 0, width, axis=dim), axis, backward)
         block = jnp.concatenate([low, block, high], axis=dim)
     return block
-
-
-def joined_along(pieces, dim):
-    shape = list(pieces.shape[1:])
-    shape[dim] *= pieces.shape[0]
-    return jnp.moveaxis(pieces, 0, dim).reshape(shape)
-
-
-def all_blocks(value, axes, sequence):
-    pieces = value[None]
-    for k in sequence:
-        pieces = lax.all_gather(pieces, axes[k], axis=0, tiled=True)
-    held = [lax.axis_size(axes[k]) for k in reversed(sequence)]
-    pieces = pieces.reshape(*held, *value.shape)
-    turned = sorted(range(len(sequence)), key=lambda place: sequence[len(sequence) - 1 - place])
-    return pieces.transpose(*turned, *range(len(sequence), pieces.ndim)).reshape(-1, *value.shape)
-
-
-def gathered_by_axis(value, axes, sequence, dim):
-    return joined_along(all_blocks(value, axes, sequence), dim)
 
 
 def exponents():
@@ -126,12 +101,14 @@
     domain = lax.axis_index(DOM)
     coeffs = interaction_ops.shape[1]
     flat_ops = jnp.transpose(interaction_ops, (0, 2, 1)).reshape(-1, coeffs)
-    fine_moments = gathered_total(fine_partial[0], "sub")
+    fine_moments = taken_together(fine_partial[0], "sub")
     wide_fine = extended(fine_moments, ((DOM, 1),), slab_cells)
     wide_mid = upward(wide_fine, upward_ops)
     mid_moments = wide_mid[:, mid_cells : 2 * mid_cells]
     own_top = upward(mid_moments, upward_ops)
-    top_moments = gathered_by_axis(own_top, DOM, (0, 1, 2), 1)
+    pieces = sent_to_all(jnp.transpose(own_top), ("dom_1", "dom_2"))
+    pieces = sent_to_all(pieces, "dom_0")
+    top_moments = jnp.transpose(pieces.reshape(-1, coeffs))
     upper_moments = upward(top_moments, upward_ops)
     upper_span = max(1, top_cells // 8)
     upper_first = domain * top_cells // 8

time: 240 us -> 214 us (0.89)
  blocking collectives: 63.6 us -> 0 us
  starting transfers between devices: 19 us -> 42 us
  waiting for transfers between devices: 0.01 us -> 9.11 us
  local copies, waits for them, and re-layouts: 83.3 us -> 86.4 us
    all_gather x4 -> x0, blocking collectives: 63.6 us -> none  [the longest x3 52.9 us: all_blocks(): pieces = lax.all_gather(pieces, axes[k], axis=0, tiled=True)]
    all_to_all x1 -> x4, starting transfers between devices: 3.63 us -> 29.6 us  [sent_to_all(): return lax.all_to_all(copies, axis, split_axis=0, concat_axis=0, tiled=True)]
    all_to_all x1 -> x4, waiting for transfers between devices: 0.01 us -> 8.16 us  [sent_to_all(): return lax.all_to_all(copies, axis, split_axis=0, concat_axis=0, tiled=True)]
    select_n x5, other arithmetic: 4.28 us -> 9.35 us  [interact_local(): picked = jnp.take(cell_rows, jnp.transpose(shifted), axis=0)]
    broadcast_in_dim x1 -> x4, local copies, waits for them, and re-layouts: 0.77 us -> 3.81 us  [sent_to_all(): copies = jnp.broadcast_to(value, (lax.axis_size(axis), *value.shape))]
    gather x7, local copies, waits for them, and re-layouts: 26.6 us -> 29.2 us  [interact_local(): picked = jnp.take(cell_rows, jnp.transpose(shifted), axis=0)]
    ppermute x1, starting transfers between devices: 7.45 us -> 4.84 us  [extended(): lax.ppermute(lax.slice_in_dim(block, block.shape[dim] - width, None, axis...]
  transfers between devices with their start and end apart: 3 -> 6, of which waited for: 0 -> 2; matrix products, arithmetic and copies ran while one was open for 25% -> 43% of each run, Pallas kernels for 0% -> 0%
where the time goes in v1:
time: 214 us; the launch traced here: 211 us
  local copies, waits for them, and re-layouts  86.4 us (40%)
  matrix products  45.7 us (21%)
  starting transfers between devices  42 us (20%)
  other arithmetic  26.6 us (12%)
  waiting for transfers between devices  9.11 us (4%)
    dot_general x4, matrix products, interact_local(): jnp.dot(stacked, flat_ops, precision=precise, preferred_element_type=jnp....  36.3 us
    all_to_all x4, starting transfers between devices, sent_to_all(): return lax.all_to_all(copies, axis, split_axis=0, concat_axis=0, tiled=True)  29.6 us
    gather x7, local copies, waits for them, and re-layouts, interact_local(): picked = jnp.take(cell_rows, jnp.transpose(shifted), axis=0)  29.2 us
    another operation x1, local copies, waits for them, and re-layouts, monomial_rows(): return jnp.stack(rows, axis=1)  18.4 us
    gather x2, local copies, waits for them, and re-layouts, evaluate(): picked = jnp.take(fine_rows, leaves, axis=0)  11.3 us
    mul x14, other arithmetic, monomial_rows(): powers[triple[0]][0] * powers[triple[1]][1] * powers[triple[2]][2]  9.69 us
    select_n x5, other arithmetic, interact_local(): picked = jnp.take(cell_rows, jnp.transpose(shifted), axis=0)  9.35 us
    transpose x1, local copies, waits for them, and re-layouts, shards(): flat_ops = jnp.transpose(interaction_ops, (0, 2, 1)).reshape(-1, coeffs)  9.12 us
  transfers between devices with their start and end apart: 6, of which 2 were waited for; matrix products, arithmetic and copies ran while one was open for 43% of the time, Pallas kernels for 0%

profile of v1, /device:TPU:1, one launch (start us, length us, event | category | flops | bytes accessed | tf_op | source)
XLA Modules:
  0.0 211.5 jit_solution(5112260057239284217)
XLA Ops:
  0.7 1.0 copy.903
  1.7 0.7 broadcast_in_dim.95
  2.4 4.8 %all-to-all-start = ((f32[4,165,128]{2,1,0:T(8,128)}), f32[4,165,128]{2,1,0:T(8,128)S(1)}, u32[]{:S(2)}, u32[]{:S(2)}) async-start(f32[4,165,128]{2,1,0:T(8,128)} %broadcast_in_dim.95), calls=%async_computation | async-start | bytes 688128 | tf_op jit(solution)/shard_map/all_to_all | solution.py:17
  7.3 0.8 fusion.53
  8.1 0.7 fusion.128
  8.8 0.7 fusion.160
  9.5 0.7 fusion.175
  10.2 0.7 fusion.174
  10.9 0.7 fusion.71
  11.6 0.7 fusion.100
  12.3 0.7 fusion.68
  13.0 0.7 fusion.107
  13.7 0.6 slice_bitcast_fusion.13
  14.3 0.6 slice_bitcast_fusion.7
  14.9 0.6 slice_bitcast_fusion.19
  15.8 0.6 pad_clamp_fusion.1
  16.4 0.5 compare_and_fusion.4
  17.3 0.7 fusion.85
  18.0 0.7 fusion.104
  18.7 0.7 fusion.163
  19.4 0.7 fusion.152
  20.1 0.7 fusion.58
  20.8 0.6 slice_bitcast_fusion.1
  21.4 0.6 compare_and_fusion.2
  22.0 0.7 fusion.138
  22.7 0.6 pad_clamp_fusion.2
  23.3 9.1 %copy.846 = f32[47,165,165]{1,0,2:T(8,128)} copy(f32[47,165,165]{1,2,0:T(8,128)} %bitcast.640) | data formatting | bytes 10236600 | tf_op jit(solution)/shard_map/transpose | solution.py:103
  32.6 8.6 %reshape.2609 = f32[7755,165]{0,1:T(8,128)} reshape(f32[47,165,165]{1,0,2:T(8,128)} %copy.846) | data formatting | bytes 10236600 | tf_op jit(solution)/shard_map/reshape | solution.py:103
  41.3 0.7 copy.829
  42.0 0.6 compare_and_fusion.3
  42.7 4.8 %collective-permute-start = (f32[165,128]{0,1:T(8,128)S(1)}, f32[165,128]{0,1:T(8,128)S(1)}, u32[]{:S(2)}, u32[]{:S(2)}) collective-permute-start(f32[165,128]{0,1:T(8,128)S(1)} %copy.831), channel_id=1, source_target_pairs={{0,4},{4,8},{8,12},{12,16},{16,20},{20,24},{24,28},{28,32},{32,36}... | collective-permute-start | bytes 253448 | tf_op jit(solution)/shard_map/ppermute | solution.py:30
  47.5 7.5 %collective-permute-start.1 = (f32[165,128]{0,1:T(8,128)S(1)}, f32[165,128]{0,1:T(8,128)S(1)}, u32[]{:S(2)}, u32[]{:S(2)}) collective-permute-start(f32[165,128]{0,1:T(8,128)S(1)} %copy.831), channel_id=1, source_target_pairs={{4,0},{8,4},{12,8},{16,12},{20,16},{24,20},{28,24},{32,28},{36,32}... | collective-permute-start | bytes 253448 | tf_op jit(solution)/shard_map/ppermute | solution.py:33
  55.1 0.9 collective-permute-done.1
  56.1 1.7 fusion.12
  57.8 1.4 fusion.33
  59.2 0.7 broadcast_in_dim.104
  59.8 13.5 %all-to-all-start.1 = ((f32[24,2,165]{2,1,0:T(2,128)}), f32[24,2,165]{2,1,0:T(2,128)}, u32[]{:S(2)}, u32[]{:S(2)}) async-start(f32[24,2,165]{2,1,0:T(2,128)} %broadcast_in_dim.104), calls=%async_computation.1 | async-start | bytes 98304 | tf_op jit(solution)/shard_map/all_to_all | solution.py:17
  73.3 2.9 %gather_fusion.1 = f32[752,165]{1,0:T(8,128)} fusion(f32[49,165]{1,0:T(8,128)S(1)} %concatenate.17, s32[1024]{0:T(1024)S(1)} %pad_clamp_fusion.3), kind=kCustom, calls=%fused_computation.1 | custom fusion | bytes 995648 | tf_op jit(solution)/shard_map/jit(_take)/gather | solution.py:74
  76.2 2.1 %reshape.2622 = f32[16,47,165]{2,1,0:T(8,128)} reshape(f32[752,165]{1,0:T(8,128)} %gather_fusion.1) | data formatting | bytes 992640 | tf_op jit(solution)/shard_map/jit(_take)/gather | solution.py:74
  78.3 2.2 %broadcast_select_fusion.1 = f32[16,47,165]{2,1,0:T(8,128)} fusion(f32[16,47,165]{2,1,0:T(8,128)} %reshape.2622, pred[16,47]{1,0:T(8,128)(4,1)S(1)} %copy-done.59), kind=kLoop, calls=%fused_computation.38 | loop fusion | flops 124080 | bytes 993392 | tf_op jit(solution)/shard_map/jit(_take)/select_n | solution.py:74
  80.6 15.3 %gather_fusion = f32[6016,165]{1,0:T(8,128)} fusion(f32[385,165]{1,0:T(8,128)S(1)} %concatenate.16, s32[6144]{0:T(1024)S(1)} %pad_clamp_fusion), kind=kCustom, calls=%fused_computation | custom fusion | bytes 7965184 | tf_op jit(solution)/shard_map/jit(_take)/gather | solution.py:74
  95.9 7.2 %reshape.2614 = f32[128,47,165]{2,1,0:T(8,128)} reshape(f32[6016,165]{1,0:T(8,128)} %gather_fusion) | data formatting | bytes 7941120 | tf_op jit(solution)/shard_map/jit(_take)/gather | solution.py:74
  103.2 1.6 broadcast_in_dim.105
  104.8 6.8 %all-to-all-start.2 = ((f32[8,24,2,165]{3,2,1,0:T(2,128)}), f32[8,24,2,165]{3,2,1,0:T(2,128)S(1)}, u32[]{:S(2)}, u32[]{:S(2)}) async-start(f32[8,24,2,165]{3,2,1,0:T(2,128)} %broadcast_in_dim.105), calls=%async_computation.2 | async-start | bytes 786432 | tf_op jit(solution)/shard_map/all_to_all | solution.py:17
  111.6 7.0 %broadcast_select_fusion = f32[128,47,165]{2,1,0:T(8,128)} fusion(f32[128,47,165]{2,1,0:T(8,128)} %reshape.2614, pred[128,47]{1,0:T(8,128)(4,1)S(1)} %copy-done.27), kind=kLoop, calls=%fused_computation.7 | loop fusion | flops 992640 | bytes 7947136 | tf_op jit(solution)/shard_map/jit(_take)/select_n | solution.py:74
  118.6 8.2 %all-to-all-done.2 = f32[8,24,2,165]{3,2,1,0:T(2,128)S(1)} async-done(((f32[8,24,2,165]{3,2,1,0:T(2,128)}), f32[8,24,2,165]{3,2,1,0:T(2,128)S(1)}, u32[]{:S(2)}, u32[]{:S(2)}) %all-to-all-start.2) | async-done | bytes 253472 | tf_op jit(solution)/shard_map/all_to_all | solution.py:17
  127.1 1.7 fusion.23
  128.8 0.7 gather_fusion.3
  129.9 6.2 %convolution_bitcast_fusion.2 = f32[165,1,1]{0,1,2:T(1,128)S(1)} fusion(f32[7755,1]{0,1:T(1,128)S(1)} %reshape.2667, f32[7755,165]{0,1:T(8,128)} %reshape.2609), kind=kOutput, calls=%fused_computation.33 | convolution fusion | flops 15354900 | bytes 5149980 | tf_op jit(solution)/shard_map/dot_general | solution.py:76
  136.1 1.5 fusion.2
  137.7 0.8 gather_fusion.2
  138.6 8.8 %fusion.32 = f32[165,2,1]{0,1,2:T(2,128)S(1)} fusion(f32[2,47,165]{2,1,0:T(8,128)S(1)} %broadcast_select_fusion.2, f32[8,165]{1,0:T(8,128)S(1)} %bitcast.646, s32[]{:T(128)S(6)} %select_n.135, f32[47,165,165]{2,1,0:T(8,128)} %param.12), kind=kOutput, calls=%fused_computation.31 | convolution fusion | flops 30710130 | bytes 5182984 | tf_op jit(solution)/shard_map/dot_general | solution.py:76
  147.4 1.5 fusion.28
  148.9 9.0 %fusion.27 = f32[165,16,1]{0,1,2:T(8,128)S(1)} fusion(f32[16,47,165]{2,1,0:T(8,128)S(1)} %copy-done.2, f32[165,2,8]{0,1,2:T(2,128)S(1)} %fusion.28, f32[47,165,165]{2,1,0:T(8,128)} %param.12), kind=kOutput, calls=%fused_computation.27 | convolution fusion | flops 245681040 | bytes 5635740 | tf_op jit(solution)/shard_map/dot_general | solution.py:76
  158.0 1.5 fusion.14
  160.1 12.3 %fusion.20 = f32[165,128]{1,0:T(8,128)S(1)} fusion(f32[165,128]{1,0:T(8,128)S(1)} %copy.851, f32[128,47,165]{2,1,0:T(8,128)} %broadcast_select_fusion, f32[47,165,165]{2,1,0:T(8,128)} %param.12), kind=kOutput, calls=%fused_computation.23 | convolution fusion | flops 1965448320 | bytes 9257820 | tf_op jit(solution)/shard_map/dot_general | solution.py:76
  172.4 0.8 broadcast_in_dim.111
  173.2 4.5 %all-to-all-start.3 = ((f32[4,165,128]{2,1,0:T(8,128)}), f32[4,165,128]{2,1,0:T(8,128)S(1)}, u32[]{:S(2)}, u32[]{:S(2)}) async-start(f32[4,165,128]{2,1,0:T(8,128)} %broadcast_in_dim.111), calls=%async_computation.3 | async-start | bytes 688128 | tf_op jit(solution)/shard_map/all_to_all | solution.py:17
  177.7 0.7 compare_and_fusion.1
  178.8 18.4 %stack.284 = f32[2048,165]{0,1:T(8,128)S(1)} concatenate(f32[2048,1]{0,1:T(1,128)S(1)} %broadcast.99, f32[2048,1]{0,1:T(1,128)} %get-tuple-element.257, f32[2048,1]{0,1:T(1,128)} %get-tuple-element.258, f32[2048,1]{0,1:T(1,128)} %get-tuple-element.259, f32[2048,1]{0,1:T(1,128)} %get-tuple-element.243, f32[2048,1]{0,1:T(1,128)S(1)} %get-tuple-element.114, ...), dimensions={1} | concatenate | bytes 2703360 | tf_op jit(solution)/shard_map/while/body/eval_jaxpr/stack | solution.py:54
  197.2 0.7 fusion.44
  198.0 8.6 %gather_fusion.4 = f32[2048,165]{1,0:T(8,128)} fusion(f32[128,165]{1,0:T(8,128)S(1)} %bitcast.639, s32[2048]{0:T(1024)S(1)} %fusion.44), kind=kCustom, calls=%fused_computation.4 | custom fusion | bytes 2711552 | tf_op jit(solution)/shard_map/while/body/eval_jaxpr/jit(_take)/gather | solution.py:136
  206.6 2.7 %copy.854 = f32[2048,165]{0,1:T(8,128)} copy(f32[2048,165]{1,0:T(8,128)} %gather_fusion.4) | data formatting | bytes 2703360 | tf_op jit(solution)/shard_map/while/body/eval_jaxpr/jit(_take)/gather | solution.py:136
  209.3 2.2 %multiply_reduce_fusion = f32[2048]{0:T(1024)} fusion(f32[2048,165]{0,1:T(8,128)S(1)} %stack.284, f32[2048,165]{0,1:T(8,128)} %copy.854, pred[2048]{0:T(1024)(128)(4,1)S(1)} %compare_and_fusion.1), kind=kLoop, calls=%fused_computation.8 | loop fusion | flops 1011712 | bytes 2713600 | tf_op jit(solution)/shard_map/while/body/eval_jaxpr/reduce_sum | solution.py:137
  (160 shorter events, 2.2 us)
Async XLA Ops:
  0.6 135.5 %copy-start = (f32[8,165,165]{2,0,1:T(8,128)S(1)}, f32[8,165,165]{2,0,1:T(8,128)}, u32[]{:S(2)}) copy-start(f32[8,165,165]{2,0,1:T(8,128)} %param.13) | copy-start | bytes 2613604
  0.7 14.9 %copy-start.58 = (s32[47,48]{1,0:T(8,128)S(1)}, s32[47,48]{1,0:T(8,128)}, u32[]{:S(2)}) copy-start(s32[47,48]{1,0:T(8,128)} %param.17) | copy-start | bytes 27076
  0.7 15.7 %copy-start.62 = (s32[47,2]{0,1:T(2,128)S(1)}, s32[47,2]{0,1:T(2,128)}, u32[]{:S(2)}) copy-start(s32[47,2]{0,1:T(2,128)} %param.16) | copy-start | bytes 1132
  0.7 16.3 %copy-start.57 = (s32[47,128]{1,0:T(8,128)S(1)}, s32[47,128]{1,0:T(8,128)}, u32[]{:S(2)}) copy-start(s32[47,128]{1,0:T(8,128)} %param.14) | copy-start | bytes 72196
  2.4 40.1 %all-to-all-start = ((f32[4,165,128]{2,1,0:T(8,128)}), f32[4,165,128]{2,1,0:T(8,128)S(1)}, u32[]{:S(2)}, u32[]{:S(2)}) async-start(f32[4,165,128]{2,1,0:T(8,128)} %broadcast_in_dim.95), calls=%async_computation | async-start | bytes 688128 | tf_op jit(solution)/shard_map/all_to_all | solution.py:17
  7.3 14.2 %copy-start.60 = (s32[47,16]{0,1:T(8,128)S(1)}, s32[47,16]{0,1:T(8,128)}, u32[]{:S(2)}) copy-start(s32[47,16]{0,1:T(8,128)} %param.15) | copy-start | bytes 9028
  8.8 23.7 %copy-start.15 = (f32[2048,1]{0,1:T(1,128)}, f32[2048,1]{0,1:T(1,128)S(1)}, u32[]{:S(2)}) copy-start(f32[2048,1]{0,1:T(1,128)S(1)} %get-tuple-element.137) | copy-start | bytes 24580
  8.8 23.7 %copy-start.17 = (f32[2048,1]{0,1:T(1,128)}, f32[2048,1]{0,1:T(1,128)S(1)}, u32[]{:S(2)}) copy-start(f32[2048,1]{0,1:T(1,128)S(1)} %get-tuple-element.139) | copy-start | bytes 24580
  9.5 23.0 %copy-start.7 = (f32[2048,1]{0,1:T(1,128)}, f32[2048,1]{0,1:T(1,128)S(1)}, u32[]{:S(2)}) copy-start(f32[2048,1]{0,1:T(1,128)S(1)} %get-tuple-element.146) | copy-start | bytes 24580
  9.5 23.0 %copy-start.19 = (f32[2048,1]{0,1:T(1,128)}, f32[2048,1]{0,1:T(1,128)S(1)}, u32[]{:S(2)}) copy-start(f32[2048,1]{0,1:T(1,128)S(1)} %get-tuple-element.48) | copy-start | bytes 24580
  9.5 23.0 %copy-start.21 = (f32[2048,1]{0,1:T(1,128)}, f32[2048,1]{0,1:T(1,128)S(1)}, u32[]{:S(2)}) copy-start(f32[2048,1]{0,1:T(1,128)S(1)} %get-tuple-element.149) | copy-start | bytes 24580
  10.2 22.3 %copy-start.5 = (f32[2048,1]{0,1:T(1,128)}, f32[2048,1]{0,1:T(1,128)S(1)}, u32[]{:S(2)}) copy-start(f32[2048,1]{0,1:T(1,128)S(1)} %get-tuple-element.84) | copy-start | bytes 24580
  10.2 22.3 %copy-start.9 = (f32[2048,1]{0,1:T(1,128)}, f32[2048,1]{0,1:T(1,128)S(1)}, u32[]{:S(2)}) copy-start(f32[2048,1]{0,1:T(1,128)S(1)} %get-tuple-element.86) | copy-start | bytes 24580
  10.2 22.3 %copy-start.11 = (f32[2048,1]{0,1:T(1,128)}, f32[2048,1]{0,1:T(1,128)S(1)}, u32[]{:S(2)}) copy-start(f32[2048,1]{0,1:T(1,128)S(1)} %get-tuple-element.88) | copy-start | bytes 24580
  10.2 22.3 %copy-start.13 = (f32[2048,1]{0,1:T(1,128)}, f32[2048,1]{0,1:T(1,128)S(1)}, u32[]{:S(2)}) copy-start(f32[2048,1]{0,1:T(1,128)S(1)} %get-tuple-element.90) | copy-start | bytes 24580
  10.9 21.6 %copy-start.23 = (f32[2048,1]{0,1:T(1,128)}, f32[2048,1]{0,1:T(1,128)S(1)}, u32[]{:S(2)}) copy-start(f32[2048,1]{0,1:T(1,128)S(1)} %get-tuple-element.76) | copy-start | bytes 24580
  10.9 21.6 %copy-start.25 = (f32[2048,1]{0,1:T(1,128)}, f32[2048,1]{0,1:T(1,128)S(1)}, u32[]{:S(2)}) copy-start(f32[2048,1]{0,1:T(1,128)S(1)} %get-tuple-element.80) | copy-start | bytes 24580
  41.2 14.9 %copy-start.1 = (f32[8,165,165]{2,0,1:T(8,128)S(1)}, f32[8,165,165]{2,0,1:T(8,128)}, u32[]{:S(2)}) copy-start(f32[8,165,165]{2,0,1:T(8,128)} %param.11) | copy-start | bytes 2613604
  42.7 12.4 %collective-permute-start = (f32[165,128]{0,1:T(8,128)S(1)}, f32[165,128]{0,1:T(8,128)S(1)}, u32[]{:S(2)}, u32[]{:S(2)}) collective-permute-start(f32[165,128]{0,1:T(8,128)S(1)} %copy.831), channel_id=1, source_target_pairs={{0,4},{4,8},{8,12},{12,16},{16,20},{20,24},{24,28},{28,32},{32,36}... | collective-permute-start | bytes 253448 | tf_op jit(solution)/shard_map/ppermute | solution.py:30
  47.5 8.5 %collective-permute-start.1 = (f32[165,128]{0,1:T(8,128)S(1)}, f32[165,128]{0,1:T(8,128)S(1)}, u32[]{:S(2)}, u32[]{:S(2)}) collective-permute-start(f32[165,128]{0,1:T(8,128)S(1)} %copy.831), channel_id=1, source_target_pairs={{4,0},{8,4},{12,8},{16,12},{20,16},{24,20},{28,24},{32,28},{36,32}... | collective-permute-start | bytes 253448 | tf_op jit(solution)/shard_map/ppermute | solution.py:33
  59.8 43.3 %all-to-all-start.1 = ((f32[24,2,165]{2,1,0:T(2,128)}), f32[24,2,165]{2,1,0:T(2,128)}, u32[]{:S(2)}, u32[]{:S(2)}) async-start(f32[24,2,165]{2,1,0:T(2,128)} %broadcast_in_dim.104), calls=%async_computation.1 | async-start | bytes 98304 | tf_op jit(solution)/shard_map/all_to_all | solution.py:17
  95.9 15.7 %copy-start.27 = (pred[128,47]{1,0:T(8,128)(4,1)S(1)}, pred[128,47]{1,0:T(8,128)(4,1)}, u32[]{:S(2)}) copy-start(pred[128,47]{1,0:T(8,128)(4,1)} %copy.829) | copy-start | bytes 18052
  104.8 22.0 %all-to-all-start.2 = ((f32[8,24,2,165]{3,2,1,0:T(2,128)}), f32[8,24,2,165]{3,2,1,0:T(2,128)S(1)}, u32[]{:S(2)}, u32[]{:S(2)}) async-start(f32[8,24,2,165]{3,2,1,0:T(2,128)} %broadcast_in_dim.105), calls=%async_computation.2 | async-start | bytes 786432 | tf_op jit(solution)/shard_map/all_to_all | solution.py:17
  159.7 18.7 %copy-start.6 = (f32[2048,1]{0,1:T(1,128)S(1)}, f32[2048,1]{0,1:T(1,128)}, u32[]{:S(2)}) copy-start(f32[2048,1]{0,1:T(1,128)} %copy-done.5) | copy-start | bytes 24580
  159.7 18.7 %copy-start.8 = (f32[2048,1]{0,1:T(1,128)S(1)}, f32[2048,1]{0,1:T(1,128)}, u32[]{:S(2)}) copy-start(f32[2048,1]{0,1:T(1,128)} %copy-done.7) | copy-start | bytes 24580
  159.7 18.7 %copy-start.10 = (f32[2048,1]{0,1:T(1,128)S(1)}, f32[2048,1]{0,1:T(1,128)}, u32[]{:S(2)}) copy-start(f32[2048,1]{0,1:T(1,128)} %copy-done.9) | copy-start | bytes 24580
  159.8 18.7 %copy-start.12 = (f32[2048,1]{0,1:T(1,128)S(1)}, f32[2048,1]{0,1:T(1,128)}, u32[]{:S(2)}) copy-start(f32[2048,1]{0,1:T(1,128)} %copy-done.11) | copy-start | bytes 24580
  159.8 18.7 %copy-start.14 = (f32[2048,1]{0,1:T(1,128)S(1)}, f32[2048,1]{0,1:T(1,128)}, u32[]{:S(2)}) copy-start(f32[2048,1]{0,1:T(1,128)} %copy-done.13) | copy-start | bytes 24580
  159.8 18.7 %copy-start.16 = (f32[2048,1]{0,1:T(1,128)S(1)}, f32[2048,1]{0,1:T(1,128)}, u32[]{:S(2)}) copy-start(f32[2048,1]{0,1:T(1,128)} %copy-done.15) | copy-start | bytes 24580
  159.8 18.7 %copy-start.18 = (f32[2048,1]{0,1:T(1,128)S(1)}, f32[2048,1]{0,1:T(1,128)}, u32[]{:S(2)}) copy-start(f32[2048,1]{0,1:T(1,128)} %copy-done.17) | copy-start | bytes 24580
  159.8 18.7 %copy-start.20 = (f32[2048,1]{0,1:T(1,128)S(1)}, f32[2048,1]{0,1:T(1,128)}, u32[]{:S(2)}) copy-start(f32[2048,1]{0,1:T(1,128)} %copy-done.19) | copy-start | bytes 24580
  159.8 18.7 %copy-start.22 = (f32[2048,1]{0,1:T(1,128)S(1)}, f32[2048,1]{0,1:T(1,128)}, u32[]{:S(2)}) copy-start(f32[2048,1]{0,1:T(1,128)} %copy-done.21) | copy-start | bytes 24580
  159.8 18.7 %copy-start.24 = (f32[2048,1]{0,1:T(1,128)S(1)}, f32[2048,1]{0,1:T(1,128)}, u32[]{:S(2)}) copy-start(f32[2048,1]{0,1:T(1,128)} %copy-done.23) | copy-start | bytes 24580
  159.8 18.7 %copy-start.26 = (f32[2048,1]{0,1:T(1,128)S(1)}, f32[2048,1]{0,1:T(1,128)}, u32[]{:S(2)}) copy-start(f32[2048,1]{0,1:T(1,128)} %copy-done.25) | copy-start | bytes 24580
  159.8 18.7 %copy-start.28 = (f32[2048,1]{0,1:T(1,128)S(1)}, f32[2048,1]{0,1:T(1,128)}, u32[]{:S(2)}) copy-start(f32[2048,1]{0,1:T(1,128)} %get-tuple-element.133) | copy-start | bytes 24580
  159.8 18.7 %copy-start.29 = (f32[2048,1]{0,1:T(1,128)S(1)}, f32[2048,1]{0,1:T(1,128)}, u32[]{:S(2)}) copy-start(f32[2048,1]{0,1:T(1,128)} %get-tuple-element.134) | copy-start | bytes 24580
  159.9 18.7 %copy-start.30 = (f32[2048,1]{0,1:T(1,128)S(1)}, f32[2048,1]{0,1:T(1,128)}, u32[]{:S(2)}) copy-start(f32[2048,1]{0,1:T(1,128)} %get-tuple-element.135) | copy-start | bytes 24580
  159.9 18.7 %copy-start.31 = (f32[2048,1]{0,1:T(1,128)S(1)}, f32[2048,1]{0,1:T(1,128)}, u32[]{:S(2)}) copy-start(f32[2048,1]{0,1:T(1,128)} %get-tuple-element.136) | copy-start | bytes 24580
  159.9 18.7 %copy-start.32 = (f32[2048,1]{0,1:T(1,128)S(1)}, f32[2048,1]{0,1:T(1,128)}, u32[]{:S(2)}) copy-start(f32[2048,1]{0,1:T(1,128)} %get-tuple-element.138) | copy-start | bytes 24580
  159.9 18.7 %copy-start.33 = (f32[2048,1]{0,1:T(1,128)S(1)}, f32[2048,1]{0,1:T(1,128)}, u32[]{:S(2)}) copy-start(f32[2048,1]{0,1:T(1,128)} %get-tuple-element.140) | copy-start | bytes 24580
  159.9 18.7 %copy-start.34 = (f32[2048,1]{0,1:T(1,128)S(1)}, f32[2048,1]{0,1:T(1,128)}, u32[]{:S(2)}) copy-start(f32[2048,1]{0,1:T(1,128)} %get-tuple-element.142) | copy-start | bytes 24580
  159.9 18.7 %copy-start.35 = (f32[2048,1]{0,1:T(1,128)S(1)}, f32[2048,1]{0,1:T(1,128)}, u32[]{:S(2)}) copy-start(f32[2048,1]{0,1:T(1,128)} %get-tuple-element.190) | copy-start | bytes 24580
  159.9 18.7 %copy-start.36 = (f32[2048,1]{0,1:T(1,128)S(1)}, f32[2048,1]{0,1:T(1,128)}, u32[]{:S(2)}) copy-start(f32[2048,1]{0,1:T(1,128)} %get-tuple-element.47) | copy-start | bytes 24580
  159.9 18.7 %copy-start.37 = (f32[2048,1]{0,1:T(1,128)S(1)}, f32[2048,1]{0,1:T(1,128)}, u32[]{:S(2)}) copy-start(f32[2048,1]{0,1:T(1,128)} %get-tuple-element.143) | copy-start | bytes 24580
  159.9 18.7 %copy-start.38 = (f32[2048,1]{0,1:T(1,128)S(1)}, f32[2048,1]{0,1:T(1,128)}, u32[]{:S(2)}) copy-start(f32[2048,1]{0,1:T(1,128)} %get-tuple-element.144) | copy-start | bytes 24580
  159.9 18.7 %copy-start.39 = (f32[2048,1]{0,1:T(1,128)S(1)}, f32[2048,1]{0,1:T(1,128)}, u32[]{:S(2)}) copy-start(f32[2048,1]{0,1:T(1,128)} %get-tuple-element.145) | copy-start | bytes 24580
  160.0 18.7 %copy-start.40 = (f32[2048,1]{0,1:T(1,128)S(1)}, f32[2048,1]{0,1:T(1,128)}, u32[]{:S(2)}) copy-start(f32[2048,1]{0,1:T(1,128)} %get-tuple-element.147) | copy-start | bytes 24580
  160.0 18.7 %copy-start.41 = (f32[2048,1]{0,1:T(1,128)S(1)}, f32[2048,1]{0,1:T(1,128)}, u32[]{:S(2)}) copy-start(f32[2048,1]{0,1:T(1,128)} %get-tuple-element.148) | copy-start | bytes 24580
  160.0 18.7 %copy-start.42 = (f32[2048,1]{0,1:T(1,128)S(1)}, f32[2048,1]{0,1:T(1,128)}, u32[]{:S(2)}) copy-start(f32[2048,1]{0,1:T(1,128)} %get-tuple-element.150) | copy-start | bytes 24580
  160.0 18.7 %copy-start.43 = (f32[2048,1]{0,1:T(1,128)S(1)}, f32[2048,1]{0,1:T(1,128)}, u32[]{:S(2)}) copy-start(f32[2048,1]{0,1:T(1,128)} %get-tuple-element.231) | copy-start | bytes 24580
  160.0 18.7 %copy-start.44 = (f32[2048,1]{0,1:T(1,128)S(1)}, f32[2048,1]{0,1:T(1,128)}, u32[]{:S(2)}) copy-start(f32[2048,1]{0,1:T(1,128)} %get-tuple-element.111) | copy-start | bytes 24580
  160.0 18.7 %copy-start.45 = (f32[2048,1]{0,1:T(1,128)S(1)}, f32[2048,1]{0,1:T(1,128)}, u32[]{:S(2)}) copy-start(f32[2048,1]{0,1:T(1,128)} %get-tuple-element.112) | copy-start | bytes 24580
  160.0 18.7 %copy-start.46 = (f32[2048,1]{0,1:T(1,128)S(1)}, f32[2048,1]{0,1:T(1,128)}, u32[]{:S(2)}) copy-start(f32[2048,1]{0,1:T(1,128)} %get-tuple-element.113) | copy-start | bytes 24580
  160.0 18.7 %copy-start.47 = (f32[2048,1]{0,1:T(1,128)S(1)}, f32[2048,1]{0,1:T(1,128)}, u32[]{:S(2)}) copy-start(f32[2048,1]{0,1:T(1,128)} %get-tuple-element.115) | copy-start | bytes 24580
  160.0 18.7 %copy-start.48 = (f32[2048,1]{0,1:T(1,128)S(1)}, f32[2048,1]{0,1:T(1,128)}, u32[]{:S(2)}) copy-start(f32[2048,1]{0,1:T(1,128)} %get-tuple-element.116) | copy-start | bytes 24580
  160.0 18.7 %copy-start.49 = (f32[2048,1]{0,1:T(1,128)S(1)}, f32[2048,1]{0,1:T(1,128)}, u32[]{:S(2)}) copy-start(f32[2048,1]{0,1:T(1,128)} %get-tuple-element.117) | copy-start | bytes 24580
  160.1 18.7 %copy-start.50 = (f32[2048,1]{0,1:T(1,128)S(1)}, f32[2048,1]{0,1:T(1,128)}, u32[]{:S(2)}) copy-start(f32[2048,1]{0,1:T(1,128)} %get-tuple-element.118) | copy-start | bytes 24580
  160.1 18.7 %copy-start.51 = (f32[2048,1]{0,1:T(1,128)S(1)}, f32[2048,1]{0,1:T(1,128)}, u32[]{:S(2)}) copy-start(f32[2048,1]{0,1:T(1,128)} %get-tuple-element.119) | copy-start | bytes 24580
  160.1 18.7 %copy-start.52 = (f32[2048,1]{0,1:T(1,128)S(1)}, f32[2048,1]{0,1:T(1,128)}, u32[]{:S(2)}) copy-start(f32[2048,1]{0,1:T(1,128)} %get-tuple-element.120) | copy-start | bytes 24580
  160.1 18.7 %copy-start.53 = (f32[2048,1]{0,1:T(1,128)S(1)}, f32[2048,1]{0,1:T(1,128)}, u32[]{:S(2)}) copy-start(f32[2048,1]{0,1:T(1,128)} %get-tuple-element.199) | copy-start | bytes 24580
  160.1 18.7 %copy-start.54 = (f32[2048,1]{0,1:T(1,128)S(1)}, f32[2048,1]{0,1:T(1,128)}, u32[]{:S(2)}) copy-start(f32[2048,1]{0,1:T(1,128)} %get-tuple-element.103) | copy-start | bytes 24580
  160.1 18.7 %copy-start.55 = (f32[2048,1]{0,1:T(1,128)S(1)}, f32[2048,1]{0,1:T(1,128)}, u32[]{:S(2)}) copy-start(f32[2048,1]{0,1:T(1,128)} %get-tuple-element.104) | copy-start | bytes 24580
  160.1 18.7 %copy-start.56 = (f32[2048,1]{0,1:T(1,128)S(1)}, f32[2048,1]{0,1:T(1,128)}, u32[]{:S(2)}) copy-start(f32[2048,1]{0,1:T(1,128)} %get-tuple-element.105) | copy-start | bytes 24580
  173.2 24.7 %all-to-all-start.3 = ((f32[4,165,128]{2,1,0:T(8,128)}), f32[4,165,128]{2,1,0:T(8,128)S(1)}, u32[]{:S(2)}, u32[]{:S(2)}) async-start(f32[4,165,128]{2,1,0:T(8,128)} %broadcast_in_dim.111), calls=%async_computation.3 | async-start | bytes 688128 | tf_op jit(solution)/shard_map/all_to_all | solution.py:17
  (6 other events, 29.0 us)

commit v2 on v1

v2 whole, which is shorter than its diff:
```python
import jax
import jax.numpy as jnp
from jax import lax
from jax.experimental import pallas as pl
from jax.experimental.pallas import tpu as pltpu
from jax.sharding import Mesh
from jax.sharding import PartitionSpec as P

ORDER = 8
F32, BF16, I32 = jnp.float32, jnp.bfloat16, jnp.int32
VMEM = pltpu.VMEM


def split(value):
    high = value.astype(BF16)
    return high, (value - high.astype(F32)).astype(BF16)


def halves(pair):
    return pair[:, :128] + pair[:, 128:]


def mm(a, b):
    return jnp.dot(a, b, preferred_element_type=F32)


def mm_nt(a, b):
    return lax.dot_general(a, b, (((1,), (1,)), ((), ())), preferred_element_type=F32)


def gathered(high, low, chosen):
    return jnp.concatenate([mm(high, chosen).astype(BF16), mm(low, chosen).astype(BF16)], axis=1)


def child_picker(rows, octant):
    r = lax.broadcasted_iota(I32, (rows, 128), 0)
    c = lax.broadcasted_iota(I32, (rows, 128), 1)
    return (r == 8 * c + octant).astype(F32).astype(BF16)


def child_spreader(octant):
    r = lax.broadcasted_iota(I32, (128, 128), 0)
    c = lax.broadcasted_iota(I32, (128, 128), 1)
    return (c == 8 * r + octant).astype(F32).astype(BF16)


def raised(moments, uph, upl, rows):
    high, low = split(moments)
    total = None
    for o in range(8):
        picked = gathered(high, low, child_picker(rows, o))
        term = mm(uph[o], picked) + mm(upl[o], picked)
        total = term if total is None else total + term
    return halves(total)


def lowered(expansion, dnh, dnl):
    high, low = split(expansion)
    total = None
    for o in range(8):
        spread = gathered(high, low, child_spreader(o))
        term = mm(dnh[o], spread) + mm(dnl[o], spread)
        total = term if total is None else total + term
    return halves(total)


def split_ops_kernel(up_ref, down_ref, uph, upl, dnh, dnl):
    for o in range(8):
        uph[o], upl[o] = split(up_ref[:, o, :])
        dnh[o], dnl[o] = split(down_ref[:, o, :])


def split_ops(upward_ops, downward_ops):
    n = upward_ops.shape[1]
    shape = jax.ShapeDtypeStruct((8, n, n), BF16)
    return pl.pallas_call(
        split_ops_kernel,
        out_shape=(shape,) * 4,
        in_specs=[pl.BlockSpec(memory_space=VMEM)] * 2,
        out_specs=(pl.BlockSpec(memory_space=VMEM),) * 4,
        compiler_params=pltpu.CompilerParams(vmem_limit_bytes=16 << 20),
        name="split_ops",
    )(jnp.transpose(upward_ops, (1, 0, 2)), jnp.transpose(downward_ops, (1, 0, 2)))


def own_kernel(parts, uph, upl, fine_ref, top_ref):
    fine = parts[0] + parts[1] + parts[2] + parts[3]
    fine_ref[...] = fine
    mid = raised(fine, uph, upl, 128)
    top = raised(mid, uph, upl, 128)
    rows = jnp.transpose(top)[:2]
    for i in range(top_ref.shape[0]):
        top_ref[i] = rows


def own_moments(parts, uph, upl, copies):
    n = parts.shape[1]
    return pl.pallas_call(
        own_kernel,
        out_shape=(jax.ShapeDtypeStruct((n, 128), F32), jax.ShapeDtypeStruct((copies, 2, n), F32)),
        in_specs=[pl.BlockSpec(memory_space=VMEM)] * 3,
        out_specs=(pl.BlockSpec(memory_space=VMEM),) * 2,
        compiler_params=pltpu.CompilerParams(vmem_limit_bytes=16 << 20),
        name="own_moments",
    )(parts, uph, upl)


GROUP = 8


def near_kernel(place, left, own, right, uph, upl, fl, ml, ops, fine_out, mid_out, wide, mids, xs, acc_a, acc_b):
    slots, n = ops.shape[0], ops.shape[1]
    for i, ref in enumerate((left, own, right)):
        wide[0, :, pl.ds(128 * i, 128)], wide[1, :, pl.ds(128 * i, 128)] = split(ref[...])
    total = None
    for o in range(8):
        picked = gathered(wide[0], wide[1], child_picker(384, o))
        term = mm(uph[o], picked) + mm(upl[o], picked)
        total = term if total is None else total + term
    mids[:, pl.ds(0, 128)], mids[:, pl.ds(128, 128)] = split(halves(total))
    anchor = place[0] * 128 - 128
    mid_anchor = place[0] * 16 - 16
    lane = lax.broadcasted_iota(I32, (1, 128), 1)
    part = (lane // 16) % 2 * 128
    acc_a[...] = jnp.zeros_like(acc_a)
    acc_b[...] = jnp.zeros_like(acc_b)

    def load(g, count):
        for q in range(0, count, 4):
            row = ml[pl.ds((g + q) // 4, 1), :]
            row = jnp.where(row >= 0, row - mid_anchor + part, -1)
            source = lax.broadcasted_iota(I32, (256, 128), 0)
            tile = mm(mids[...], (source == row).astype(F32).astype(BF16)).astype(BF16)
            for jj in range(q, min(q + 4, count)):
                xs[jj, :, pl.ds(128, 128)] = jnp.where(lane // 32 == jj - q, tile, jnp.zeros_like(tile))
        for q in range(0, count, 2):
            rows = []
            for jj in range(q, min(q + 2, count)):
                row = fl[pl.ds(g + jj, 1), :]
                rows.append(jnp.where(row >= 0, row - anchor, -1))
            row = jnp.concatenate(rows, axis=1)
            source = lax.broadcasted_iota(I32, (384, row.shape[1]), 0)
            chosen = (source == row).astype(F32).astype(BF16)
            for h in range(2):
                got = mm(wide[h], chosen).astype(BF16)
                for i in range(len(rows)):
                    xs[q + i, :, pl.ds(256 * h, 128)] = got[:, 128 * i : 128 * (i + 1)]

    def use(g, count):
        a = b = None
        for jj in range(count):
            oh, ol = split(ops[g + jj])
            x = xs[jj]
            ta = mm(oh, x[:, :256]) + mm(ol, x[:, :256])
            tb = mm(oh, x[:, 256:])
            a = ta if a is None else a + ta
            b = tb if b is None else b + tb
        acc_a[...] += a
        acc_b[...] += b

    for g in range(0, slots, GROUP):
        count = min(GROUP, slots - g)
        load(g, count)
        use(g, count)
    fine_out[...] = acc_a[:, pl.ds(0, 128)] + acc_b[...]
    folded = acc_a[:, pl.ds(128, 128)]
    for shift in (64, 32, 16):
        folded = folded + pltpu.roll(folded, shift, 1)
    mid_out[...] = folded


def near_terms(place, left, own, right, uph, upl, fine_list, mid_rows, ops):
    n = ops.shape[1]
    vm = pl.BlockSpec(memory_space=VMEM)
    return pl.pallas_call(
        near_kernel,
        out_shape=(jax.ShapeDtypeStruct((n, 128), F32),) * 2,
        in_specs=[pl.BlockSpec(memory_space=pltpu.SMEM)] + [vm] * 8,
        out_specs=(vm,) * 2,
        scratch_shapes=[
            pltpu.VMEM((2, n, 384), BF16),
            pltpu.VMEM((n, 256), BF16),
            pltpu.VMEM((GROUP, n, 384), BF16),
            pltpu.VMEM((n, 256), F32),
            pltpu.VMEM((n, 128), F32),
        ],
        compiler_params=pltpu.CompilerParams(vmem_limit_bytes=12 << 20),
        name="near_terms",
    )(place, left, own, right, uph, upl, fine_list, mid_rows, ops)


def far_kernel(
    place, tl, ul, table, uph, upl, dnh, dnl, fine_term, mid_term, ops, out,
    rows, upper, chosen, top_col, upper_col,
):
    slots, n = ops.shape[0], ops.shape[1]
    parents = rows.shape[1] - 8
    rows[:, pl.ds(parents, 8), :] = jnp.zeros((8, 8, n), F32)
    upper[...] = jnp.zeros_like(upper)
    for a in range(table.shape[0]):
        for b in range(table.shape[1]):
            for i in range(2):
                cell = (a * table.shape[1] + b) * 2 + i
                rows[cell % 8, pl.ds(cell // 8, 1), :] = table[a, b, pl.ds(i, 1), :]
    total = None
    for o in range(8):
        high, low = split(rows[o, pl.ds(0, parents), :])
        term = mm_nt(high, uph[o]) + mm_nt(high, upl[o]) + mm_nt(low, uph[o])
        total = term if total is None else total + term
    upper[pl.ds(0, parents), :] = total
    parent = place[0] // 4
    for j in range(slots):
        for t in range(2):
            index = tl[t, j]
            index = jnp.where(index >= 0, index, parents * 8)
            chosen[3 * j + t] = jnp.broadcast_to(rows[index & 7, pl.ds(index >> 3, 1), :], (8, n))
        index = ul[j, parent]
        index = jnp.where(index >= 0, index, parents)
        chosen[3 * j + 2] = jnp.broadcast_to(upper[pl.ds(index, 1), :], (8, n))
    lane = lax.broadcasted_iota(I32, (8, 128), 1)

    def block(start, size):
        sums = [jnp.zeros((size, n), F32)] * 3
        for j in range(slots):
            piece = ops[j, pl.ds(start, size), :]
            for t in range(3):
                sums[t] = sums[t] + piece * chosen[3 * j + t, :size]
        s0, s1, s2 = [jnp.sum(s, axis=1, keepdims=True) for s in sums]
        here = lane[:size]
        top_col[pl.ds(start, size), :] = jnp.where(here == 0, s0, jnp.where(here == 1, s1, 0.0))
        upper_col[pl.ds(start, size), :] = jnp.where(here < 2, s2, 0.0)

    def step(i, carry):
        block(pl.multiple_of(i * 8, 8), 8)
        return carry

    lax.fori_loop(0, n // 8, step, 0)
    if n % 8:
        block(n // 8 * 8, n % 8)
    both = jnp.concatenate(split(upper_col[...]), axis=1)
    octant = lax.rem(place[0] * 2, 8)
    lane = lax.broadcasted_iota(I32, (n, 128), 1)
    from_upper = [halves(mm(dnh[octant + i], both) + mm(dnl[octant + i], both)) for i in range(2)]
    local_top = top_col[...] + jnp.where(lane == 0, from_upper[0], jnp.where(lane == 1, from_upper[1], 0.0))
    local_mid = lowered(local_top, dnh, dnl) + mid_term[...]
    local_mid = jnp.where(lane < 16, local_mid, 0.0)
    local_fine = lowered(local_mid, dnh, dnl) + fine_term[...]
    for i in range(out.shape[0]):
        out[i] = local_fine


def far_terms(place, top_list, upper_list, table, uph, upl, dnh, dnl, fine_term, mid_term, ops, copies):
    slots, n = ops.shape[0], ops.shape[1]
    cells = table.shape[0] * table.shape[1] * 2
    vm, sm = pl.BlockSpec(memory_space=VMEM), pl.BlockSpec(memory_space=pltpu.SMEM)
    return pl.pallas_call(
        far_kernel,
        out_shape=jax.ShapeDtypeStruct((copies, n, 128), F32),
        in_specs=[sm] * 3 + [vm] * 8,
        out_specs=vm,
        scratch_shapes=[
            pltpu.VMEM((8, cells // 8 + 8, n), F32),
            pltpu.VMEM((cells // 8 + 8, n), F32),
            pltpu.VMEM((3 * slots, 8, n), F32),
            pltpu.VMEM((n, 128), F32),
            pltpu.VMEM((n, 128), F32),
        ],
        compiler_params=pltpu.CompilerParams(vmem_limit_bytes=12 << 20),
        name="far_terms",
    )(place, jnp.transpose(top_list), upper_list, table, uph, upl, dnh, dnl, fine_term, mid_term, ops)


def exponents():
    entries = []
    for degree in range(ORDER + 1):
        for along_x in range(degree, -1, -1):
            for along_y in range(degree - along_x, -1, -1):
                entries.append((along_x, along_y, degree - along_x - along_y))
    return entries


def monomial_kernel(powers, coords, high_ref, low_ref):
    n = powers.shape[0]
    terms = []
    value = None
    for axis in range(3):
        e = powers[:, pl.ds(axis, 1)]
        base = coords[pl.ds(axis, 1), :]
        for bit in range(4):
            factor = jnp.where((e >> bit) & 1 == 1, base, 1.0)
            value = factor if value is None else value * factor
            base = base * base
    high_ref[...], low_ref[...] = split(value)


def monomials(coords):
    table = jnp.asarray(exponents(), I32)
    n, particles = table.shape[0], coords.shape[1]
    width = 512
    return pl.pallas_call(
        monomial_kernel,
        grid=(particles // width,),
        out_shape=(jax.ShapeDtypeStruct((n, particles), BF16),) * 2,
        in_specs=[pl.BlockSpec((n, 3), lambda i: (0, 0)), pl.BlockSpec((3, width), lambda i: (0, i))],
        out_specs=(pl.BlockSpec((n, width), lambda i: (0, i)),) * 2,
        name="monomials",
    )(table, coords)


def potential_kernel(parts, leaves, high_ref, low_ref, fine_ref, out):
    fine = parts[0] + parts[1] + parts[2] + parts[3]
    fine_ref[...] = fine
    fh, fl = split(jnp.transpose(fine))
    width = 512
    cell = lax.broadcasted_iota(I32, (128, width), 0)
    for k in range(out.shape[1] // width):
        at = pl.ds(k * width, width)
        mh, ml = high_ref[:, at], low_ref[:, at]
        values = mm(fh, mh) + mm(fl, mh) + mm(fh, ml)
        out[:, at] = jnp.sum(jnp.where(cell == leaves[:, at], values, 0.0), axis=0, keepdims=True)


def potentials(parts, leaves, high, low):
    n = parts.shape[1]
    particles = leaves.shape[1]
    vm = pl.BlockSpec(memory_space=VMEM)
    return pl.pallas_call(
        potential_kernel,
        out_shape=(jax.ShapeDtypeStruct((n, 128), F32), jax.ShapeDtypeStruct((1, particles), F32)),
        in_specs=[vm] * 4,
        out_specs=(vm,) * 2,
        compiler_params=pltpu.CompilerParams(vmem_limit_bytes=16 << 20),
        name="potentials",
    )(parts, leaves, high, low)


DOM = ("dom_0", "dom_1", "dom_2")
DOM_SUB = ("dom_0", "dom_1", "dom_2", "sub")


def exchanged(copies, axes):
    return lax.all_to_all(copies, axes, split_axis=0, concat_axis=0, tiled=True)


def copied(value, count):
    return jnp.broadcast_to(value, (count, *value.shape))


def shards(
    fine_partial,
    upward_ops,
    interaction_ops,
    downward_ops,
    fine_list,
    mid_list,
    top_list,
    upper_list,
    positions,
    leaf_cell,
):
    slab_cells = fine_partial.shape[2]
    slots = interaction_ops.shape[0]
    subs, slabs = lax.axis_size("sub"), lax.axis_size(DOM)
    domain = lax.axis_index(DOM)
    place = domain.astype(I32).reshape(1)
    uph, upl, dnh, dnl = split_ops(upward_ops, downward_ops)
    parts = exchanged(copied(fine_partial[0], subs), "sub")
    own, tops = own_moments(parts, uph, upl, lax.axis_size(DOM[1:]))
    forward = [(i, i + 1) for i in range(slabs - 1)]
    backward = [(target, source) for source, target in forward]
    left = lax.ppermute(own, DOM, forward)
    right = lax.ppermute(own, DOM, backward)
    line = exchanged(tops, DOM[1:])
    table = exchanged(copied(line, lax.axis_size(DOM[0])), DOM[0])
    rows = -(-slots // 4)
    mid_rows = jnp.pad(mid_list, ((0, rows * 4 - slots), (0, 0)), constant_values=-1)
    mid_rows = jnp.concatenate([mid_rows, mid_rows], axis=1).reshape(rows, 128)
    fine_term, mid_term = near_terms(place, left, own, right, uph, upl, fine_list, mid_rows, interaction_ops)
    partial = far_terms(
        place, top_list, upper_list, table, uph, upl, dnh, dnl, fine_term, mid_term, interaction_ops, subs
    )
    high, low = monomials(positions)
    leaves = (leaf_cell - domain * slab_cells).reshape(1, -1)
    local_fine, potential = potentials(exchanged(partial, "sub"), leaves, high, low)
    return local_fine, potential.reshape(-1)


def solution(mesh):
    torus = Mesh(
        mesh.devices.reshape(8, 12, 2, mesh.shape["sub"]), ("dom_0", "dom_1", "dom_2", "sub")
    )
    return jax.shard_map(
        shards,
        mesh=torus,
        in_specs=(
            P("sub", None, DOM),
            P(),
            P("sub", None, None),
            P(),
            P("sub", DOM),
            P("sub", DOM),
            P("sub", DOM),
            P("sub", None),
            P(None, DOM_SUB),
            P(DOM_SUB),
        ),
        out_specs=(P(None, DOM), P(DOM_SUB)),
        check_vma=False,
    )
```

time: 214 us -> 108 us (0.50)
  the two profiles are of different devices: /device:TPU:1 before, /device:TPU:32 now
where the time goes in v2:
time: 108 us; the launch traced here: 107 us
  Pallas kernels  35.2 us (33%)
  blocking collectives  25.7 us (24%)
  starting transfers between devices  25.4 us (24%)
  local copies, waits for them, and re-layouts  15.6 us (14%)
  waiting for transfers between devices  4.84 us (4%)
    all_to_all x1, blocking collectives, exchanged(): return lax.all_to_all(copies, axes, split_axis=0, concat_axis=0, tiled=True)  25.7 us
    all_to_all x3, starting transfers between devices, exchanged(): return lax.all_to_all(copies, axes, split_axis=0, concat_axis=0, tiled=True)  16.3 us
    unnamed x27, local copies, waits for them, and re-layouts  13.9 us
    pallas_call x1, Pallas kernels, far_terms(): pl.pallas_call(far_kernel, out_shape=jax.ShapeDtypeStruct((copies, n, 128...  10.6 us
    pallas_call x1, Pallas kernels, near_terms(): pl.pallas_call(near_kernel, out_shape=(jax.ShapeDtypeStruct((n, 128), F32...  8.84 us
    pallas_call x1, Pallas kernels, split_ops(): pl.pallas_call(split_ops_kernel, out_shape=(shape,) * 4, in_specs=[pl.Blo...  8.21 us
    ppermute x1, starting transfers between devices, shards(): right = lax.ppermute(own, DOM, backward)  7.14 us
    pallas_call x1, Pallas kernels, monomials(): pl.pallas_call(monomial_kernel, grid=(particles // width,), out_shape=(ja...  4 us
  transfers between devices with their start and end apart: 5, of which 3 were waited for; matrix products, arithmetic and copies ran while one was open for 0% of the time, Pallas kernels for 20%

profile of v2, /device:TPU:32, one launch (start us, length us, event | category | flops | bytes accessed | tf_op | source)
XLA Modules:
  0.0 107.4 jit_solution(15406976351989196475)
XLA Ops:
  0.6 0.9 copy.17
  1.5 0.8 broadcast_in_dim.6
  2.3 4.3 %all-to-all-start = ((f32[4,165,128]{2,1,0:T(8,128)}), f32[4,165,128]{2,1,0:T(8,128)S(1)}, u32[]{:S(2)}, u32[]{:S(2)}) async-start(f32[4,165,128]{2,1,0:T(8,128)} %broadcast_in_dim.6), calls=%async_computation | async-start | bytes 688128 | tf_op jit(solution)/shard_map/all_to_all | solution.py:342
  6.6 0.0 copy-start.2
  6.6 1.3 %copy-done.2 = f32[8,165,165]{2,0,1:T(8,128)S(1)} copy-done((f32[8,165,165]{2,0,1:T(8,128)S(1)}, f32[8,165,165]{2,0,1:T(8,128)}, u32[]{:S(2)}) %copy-start.2) | copy-done | bytes 871224
  7.9 0.0 copy-start.3
  7.9 1.3 %copy-done.3 = f32[8,165,165]{2,0,1:T(8,128)S(1)} copy-done((f32[8,165,165]{2,0,1:T(8,128)S(1)}, f32[8,165,165]{2,0,1:T(8,128)}, u32[]{:S(2)}) %copy-start.3) | copy-done | bytes 871224
  9.2 8.2 %split_ops.1 = (bf16[8,165,165]{2,1,0:T(8,128)(2,1)S(1)}, bf16[8,165,165]{2,1,0:T(8,128)(2,1)S(1)}, bf16[8,165,165]{2,1,0:T(8,128)(2,1)S(1)}, bf16[8,165,165]{2,1,0:T(8,128)(2,1)S(1)}) custom-call(f32[165,8,165]{2,1,0:T(8,128)S(1)} %bitcast.9, f32[165,8,165]{2,1,0:T(8,128)S(1)} %bitcast.10), custom_call_target="tpu_custom_call" | custom-call | tf_op jit(solution)/shard_map/split_ops/pallas_call | solution.py:76
  17.5 0.0 all-to-all-done.parts
  17.5 0.0 copy-start.11
  17.5 0.0 copy-start.8
  17.5 2.3 %own_moments.1 = (f32[165,128]{1,0:T(8,128)S(1)}, f32[24,2,165]{2,1,0:T(2,128)S(1)}) custom-call(f32[4,165,128]{2,1,0:T(8,128)S(1)} %all-to-all-done.parts, bf16[8,165,165]{2,1,0:T(8,128)(2,1)S(1)} %get-tuple-element.14.uph, bf16[8,165,165]{2,1,0:T(8,128)(2,1)S(1)} %get-tuple-element.15.upl), custom_call_target="tpu_custom_call" | custom-call | tf_op jit(solution)/shard_map/own_moments/pallas_call | solution.py:98
  19.8 25.7 %all_to_all.20 = f32[24,2,165]{2,1,0:T(2,128)S(1)} all-to-all(f32[24,2,165]{2,1,0:T(2,128)S(1)} %get-tuple-element.16), channel_id=1, replica_groups=mesh['dom_0'=8,'dom_1'=12,'dom_2'=2,'sub'=4] {'dom_1','dom_2'}, dimensions={0} | all-to-all | bytes 63360 | tf_op jit(solution)/shard_map/all_to_all | solution.py:342
  45.4 0.8 broadcast_in_dim.7
  46.3 7.2 %all-to-all-start.2 = ((f32[8,24,2,165]{3,2,1,0:T(2,128)}), f32[8,24,2,165]{3,2,1,0:T(2,128)S(1)}, u32[]{:S(2)}, u32[]{:S(2)}) async-start(f32[8,24,2,165]{3,2,1,0:T(2,128)} %broadcast_in_dim.7), calls=%async_computation.2 | async-start | bytes 786432 | tf_op jit(solution)/shard_map/all_to_all | solution.py:342
  53.5 0.0 copy-done.11
  53.5 1.9 %collective-permute-start = (f32[165,128]{1,0:T(8,128)S(1)}, f32[165,128]{1,0:T(8,128)S(1)}, u32[]{:S(2)}, u32[]{:S(2)}) collective-permute-start(f32[165,128]{1,0:T(8,128)S(1)} %get-tuple-element.19.own), channel_id=1, source_target_pairs={{0,4},{4,8},{8,12},{12,16},{16,20},{20,24},{24,28},{28,32},{32,36}... | collective-permute-start | bytes 253448 | tf_op jit(solution)/shard_map/ppermute | solution.py:371
  55.4 7.1 %collective-permute-start.1 = (f32[165,128]{1,0:T(8,128)S(1)}, f32[165,128]{1,0:T(8,128)S(1)}, u32[]{:S(2)}, u32[]{:S(2)}) collective-permute-start(f32[165,128]{1,0:T(8,128)S(1)} %get-tuple-element.19.own), channel_id=1, source_target_pairs={{4,0},{8,4},{12,8},{16,12},{20,16},{24,20},{28,24},{32,28},{36,32}... | collective-permute-start | bytes 253448 | tf_op jit(solution)/shard_map/ppermute | solution.py:372
  62.6 0.1 copy.14
  62.7 0.1 reshape.17.ml
  62.7 0.4 collective-permute-done.left
  63.2 1.3 %collective-permute-done.1.right = f32[165,128]{1,0:T(8,128)S(1)} collective-permute-done((f32[165,128]{1,0:T(8,128)S(1)}, f32[165,128]{1,0:T(8,128)S(1)}, u32[]{:S(2)}, u32[]{:S(2)}) %collective-permute-start.1) | collective-permute-done | bytes 84512 | tf_op jit(solution)/shard_map/ppermute | solution.py:372
  64.5 0.0 copy-done.8
  64.5 0.0 copy-start
  64.5 3.3 %copy-done = f32[47,165,165]{2,1,0:T(8,128)S(1)} copy-done((f32[47,165,165]{2,1,0:T(8,128)S(1)}, f32[47,165,165]{2,1,0:T(8,128)}, u32[]{:S(2)}) %copy-start) | copy-done | bytes 5118324
  67.8 0.0 copy-start.9
  67.8 0.0 copy-start.10
  67.8 8.8 %near_terms.1 = (f32[165,128]{1,0:T(8,128)S(1)}, f32[165,128]{1,0:T(8,128)S(1)}) custom-call(s32[1]{0:T(128)} %bitcast.place, f32[165,128]{1,0:T(8,128)S(1)} %collective-permute-done.left, f32[165,128]{1,0:T(8,128)S(1)} %get-tuple-element.19.own, f32[165,128]{1,0:T(8,128)S(1)} %collective-permute-done.1.right, ...), custom_call_target="tpu_custom_call" | custom-call | tf_op jit(solution)/shard_map/near_terms/pallas_call | solution.py:175
  76.6 0.0 copy-start.6
  76.6 0.6 copy-done.6
  77.3 0.0 all-to-all-done.2.table
  77.3 0.0 copy-done.9
  77.3 0.0 copy-done.10
  77.3 0.0 copy-start.1
  77.3 3.3 %copy-done.1 = f32[47,165,165]{2,1,0:T(8,128)S(1)} copy-done((f32[47,165,165]{2,1,0:T(8,128)S(1)}, f32[47,165,165]{2,1,0:T(8,128)}, u32[]{:S(2)}) %copy-start.1) | copy-done | bytes 5118324
  80.6 0.0 copy-start.7
  80.6 0.9 copy-done.7
  81.5 0.0 copy-start.12
  81.5 10.6 %far_terms.1 = f32[4,165,128]{2,1,0:T(8,128)} custom-call(s32[1]{0:T(128)} %bitcast.place, s32[2,47]{1,0:T(2,128)S(1)} %bitcast.12, s32[47,48]{1,0:T(8,128)S(1)} %copy-done.9, f32[8,24,2,165]{3,2,1,0:T(2,128)S(1)} %all-to-all-done.2.table, bf16[8,165,165]{2,1,0:T(8,128)(2,1)S(1)} %get-tuple-element.14.uph, bf16[8,165,165]{2,1,0:T(8,128)(2,1)S(1)} %get-tuple-element.15.upl, ...), custom_call_target="tpu_custom_call" | custom-call | tf_op jit(solution)/shard_map/far_terms/pallas_call | solution.py:256
  92.1 4.8 %all-to-all-start.3 = ((f32[4,165,128]{2,1,0:T(8,128)}), f32[4,165,128]{2,1,0:T(8,128)S(1)}, u32[]{:S(2)}, u32[]{:S(2)}) async-start(f32[4,165,128]{2,1,0:T(8,128)} %far_terms.1), calls=%async_computation.3 | async-start | bytes 688128 | tf_op jit(solution)/shard_map/all_to_all | solution.py:342
  96.9 4.0 %monomials.1 = (bf16[165,2048]{1,0:T(8,128)(2,1)}, bf16[165,2048]{1,0:T(8,128)(2,1)}) custom-call(s32[165,3]{1,0:T(8,128)} %constant.25.clone.powers, f32[3,2048]{1,0:T(4,128)} %coords.1), custom_call_target="tpu_custom_call" | custom-call | tf_op jit(solution)/shard_map/monomials/pallas_call | solution.py:300
  100.9 0.0 copy-done.12
  100.9 3.1 %all-to-all-done.3.parts = f32[4,165,128]{2,1,0:T(8,128)S(1)} async-done(((f32[4,165,128]{2,1,0:T(8,128)}), f32[4,165,128]{2,1,0:T(8,128)S(1)}, u32[]{:S(2)}, u32[]{:S(2)}) %all-to-all-start.3) | async-done | bytes 337952 | tf_op jit(solution)/shard_map/all_to_all | solution.py:342
  104.0 0.0 copy-start.4
  104.0 1.1 %copy-done.4 = bf16[165,2048]{1,0:T(8,128)(2,1)S(1)} copy-done((bf16[165,2048]{1,0:T(8,128)(2,1)S(1)}, bf16[165,2048]{1,0:T(8,128)(2,1)}, u32[]{:S(2)}) %copy-start.4) | copy-done | bytes 675864
  105.1 0.0 copy-start.5
  105.1 1.1 %copy-done.5 = bf16[165,2048]{1,0:T(8,128)(2,1)S(1)} copy-done((bf16[165,2048]{1,0:T(8,128)(2,1)S(1)}, bf16[165,2048]{1,0:T(8,128)(2,1)}, u32[]{:S(2)}) %copy-start.5) | copy-done | bytes 675864
  106.2 1.2 %potentials.1 = (f32[165,128]{1,0:T(8,128)}, f32[1,2048]{1,0:T(1,128)}) custom-call(f32[4,165,128]{2,1,0:T(8,128)S(1)} %all-to-all-done.3.parts, s32[1,2048]{1,0:T(1,128)S(1)} %bitcast.11, bf16[165,2048]{1,0:T(8,128)(2,1)S(1)} %copy-done.4, bf16[165,2048]{1,0:T(8,128)(2,1)S(1)} %copy-done.5), custom_call_target="tpu_custom_call" | custom-call | tf_op jit(solution)/shard_map/potentials/pallas_call | solution.py:327
  (3 shorter events, 0.0 us)
Async XLA Ops:
  2.3 15.2 %all-to-all-start = ((f32[4,165,128]{2,1,0:T(8,128)}), f32[4,165,128]{2,1,0:T(8,128)S(1)}, u32[]{:S(2)}, u32[]{:S(2)}) async-start(f32[4,165,128]{2,1,0:T(8,128)} %broadcast_in_dim.6), calls=%async_computation | async-start | bytes 688128 | tf_op jit(solution)/shard_map/all_to_all | solution.py:342
  6.6 1.3 %copy-start.2 = (f32[8,165,165]{2,0,1:T(8,128)S(1)}, f32[8,165,165]{2,0,1:T(8,128)}, u32[]{:S(2)}) copy-start(f32[8,165,165]{2,0,1:T(8,128)} %param.12) | copy-start | bytes 2613604
  7.9 1.3 %copy-start.3 = (f32[8,165,165]{2,0,1:T(8,128)S(1)}, f32[8,165,165]{2,0,1:T(8,128)}, u32[]{:S(2)}) copy-start(f32[8,165,165]{2,0,1:T(8,128)} %param.14) | copy-start | bytes 2613604
  17.5 36.0 %copy-start.11 = (s32[47,16]{0,1:T(8,128)S(1)}, s32[47,16]{0,1:T(8,128)}, u32[]{:S(2)}) copy-start(s32[47,16]{0,1:T(8,128)} %param.16) | copy-start | bytes 9028
  17.5 47.0 %copy-start.8 = (s32[47,128]{1,0:T(8,128)S(1)}, s32[47,128]{1,0:T(8,128)}, u32[]{:S(2)}) copy-start(s32[47,128]{1,0:T(8,128)} %fl.1) | copy-start | bytes 72196
  46.3 31.0 %all-to-all-start.2 = ((f32[8,24,2,165]{3,2,1,0:T(2,128)}), f32[8,24,2,165]{3,2,1,0:T(2,128)S(1)}, u32[]{:S(2)}, u32[]{:S(2)}) async-start(f32[8,24,2,165]{3,2,1,0:T(2,128)} %broadcast_in_dim.7), calls=%async_computation.2 | async-start | bytes 786432 | tf_op jit(solution)/shard_map/all_to_all | solution.py:342
  53.5 9.7 %collective-permute-start = (f32[165,128]{1,0:T(8,128)S(1)}, f32[165,128]{1,0:T(8,128)S(1)}, u32[]{:S(2)}, u32[]{:S(2)}) collective-permute-start(f32[165,128]{1,0:T(8,128)S(1)} %get-tuple-element.19.own), channel_id=1, source_target_pairs={{0,4},{4,8},{8,12},{12,16},{16,20},{20,24},{24,28},{28,32},{32,36}... | collective-permute-start | bytes 253448 | tf_op jit(solution)/shard_map/ppermute | solution.py:371
  55.4 9.0 %collective-permute-start.1 = (f32[165,128]{1,0:T(8,128)S(1)}, f32[165,128]{1,0:T(8,128)S(1)}, u32[]{:S(2)}, u32[]{:S(2)}) collective-permute-start(f32[165,128]{1,0:T(8,128)S(1)} %get-tuple-element.19.own), channel_id=1, source_target_pairs={{4,0},{8,4},{12,8},{16,12},{20,16},{24,20},{28,24},{32,28},{36,32}... | collective-permute-start | bytes 253448 | tf_op jit(solution)/shard_map/ppermute | solution.py:372
  64.5 3.3 %copy-start = (f32[47,165,165]{2,1,0:T(8,128)S(1)}, f32[47,165,165]{2,1,0:T(8,128)}, u32[]{:S(2)}) copy-start(f32[47,165,165]{2,1,0:T(8,128)} %ops.3) | copy-start | bytes 15354904
  67.8 9.5 %copy-start.9 = (s32[47,48]{1,0:T(8,128)S(1)}, s32[47,48]{1,0:T(8,128)}, u32[]{:S(2)}) copy-start(s32[47,48]{1,0:T(8,128)} %ul.1) | copy-start | bytes 27076
  67.8 9.5 %copy-start.10 = (s32[47,2]{0,1:T(2,128)S(1)}, s32[47,2]{0,1:T(2,128)}, u32[]{:S(2)}) copy-start(s32[47,2]{0,1:T(2,128)} %param.17) | copy-start | bytes 1132
  76.6 0.6 copy-start.6
  77.3 3.3 %copy-start.1 = (f32[47,165,165]{2,1,0:T(8,128)S(1)}, f32[47,165,165]{2,1,0:T(8,128)}, u32[]{:S(2)}) copy-start(f32[47,165,165]{2,1,0:T(8,128)} %ops.3) | copy-start | bytes 15354904
  80.6 0.9 copy-start.7
  81.5 19.4 %copy-start.12 = (s32[2048]{0:T(1024)S(1)}, s32[2048]{0:T(1024)}, u32[]{:S(2)}) copy-start(s32[2048]{0:T(1024)} %param.20) | copy-start | bytes 24580
  92.1 11.9 %all-to-all-start.3 = ((f32[4,165,128]{2,1,0:T(8,128)}), f32[4,165,128]{2,1,0:T(8,128)S(1)}, u32[]{:S(2)}, u32[]{:S(2)}) async-start(f32[4,165,128]{2,1,0:T(8,128)} %far_terms.1), calls=%async_computation.3 | async-start | bytes 688128 | tf_op jit(solution)/shard_map/all_to_all | solution.py:342
  104.0 1.1 %copy-start.4 = (bf16[165,2048]{1,0:T(8,128)(2,1)S(1)}, bf16[165,2048]{1,0:T(8,128)(2,1)}, u32[]{:S(2)}) copy-start(bf16[165,2048]{1,0:T(8,128)(2,1)} %get-tuple-element.22.high_ref) | copy-start | bytes 2027524
  105.1 1.1 %copy-start.5 = (bf16[165,2048]{1,0:T(8,128)(2,1)S(1)}, bf16[165,2048]{1,0:T(8,128)(2,1)}, u32[]{:S(2)}) copy-start(bf16[165,2048]{1,0:T(8,128)(2,1)} %get-tuple-element.23.low_ref) | copy-start | bytes 2027524

commit v3 on v2

v3 whole, which is shorter than its diff:
```python
import jax
import jax.numpy as jnp
from jax import lax
from jax.experimental import pallas as pl
from jax.experimental.pallas import tpu as pltpu
from jax.sharding import Mesh
from jax.sharding import PartitionSpec as P


ORDER = 8
F32, BF16, I32 = jnp.float32, jnp.bfloat16, jnp.int32
VMEM = pltpu.VMEM


def split(value):
    high = value.astype(BF16)
    return high, (value - high.astype(F32)).astype(BF16)


def in_hbm(value):
    return pltpu.with_memory_space_constraint(value, pltpu.HBM)


def halves(pair):
    return pair[:, :128] + pair[:, 128:]


def mm(a, b):
    return jnp.dot(a, b, preferred_element_type=F32)


def mm_nt(a, b):
    return lax.dot_general(a, b, (((1,), (1,)), ((), ())), preferred_element_type=F32)


def gathered(high, low, chosen):
    return jnp.concatenate([mm(high, chosen).astype(BF16), mm(low, chosen).astype(BF16)], axis=1)


def ones_where(shape, test):
    rows = lax.broadcasted_iota(I32, shape, 0)
    lanes = lax.broadcasted_iota(I32, shape, 1)
    return test(rows, lanes).astype(F32).astype(BF16)


def octant_sum(high, low, pair):
    lane = lax.broadcasted_iota(I32, (1, 256), 1) % 8
    total = None
    for o in range(8):
        term = mm(high[o], pair) + mm(low[o], pair)
        total = jnp.where(lane == o, term, 0.0 if total is None else total)
    return halves(total)


def raised(moments, uph, upl):
    summed = octant_sum(uph, upl, jnp.concatenate(split(moments), axis=1))
    parent = ones_where((128, 128), lambda r, c: r // 8 == c)
    high, low = split(summed)
    return mm(high, parent) + mm(low, parent)


def lowered(expansion, dnh, dnl):
    child = ones_where((128, 128), lambda r, c: c // 8 == r)
    return octant_sum(dnh, dnl, gathered(*split(expansion), child))


def split_kernel(ops_hbm, high, low, parts, sems):
    copies = [pltpu.make_async_copy(ops_hbm.at[:, o, :], parts.at[o], sems.at[o]) for o in range(8)]
    for copy in copies:
        copy.start()
    for o in range(8):
        copies[o].wait()
        high[o], low[o] = split(parts[o])


def split_ops(ops, kept=VMEM):
    n = ops.shape[1]
    return pl.pallas_call(
        split_kernel,
        out_shape=(kept((8, n, n), BF16),) * 2,
        in_specs=[pl.BlockSpec(memory_space=pltpu.HBM)],
        out_specs=(pl.BlockSpec(memory_space=VMEM),) * 2,
        scratch_shapes=[pltpu.VMEM((8, n, n), F32), pltpu.SemaphoreType.DMA((8,))],
        compiler_params=pltpu.CompilerParams(vmem_limit_bytes=8 << 20),
    )(in_hbm(jnp.transpose(ops, (1, 0, 2))))


MID_AT = 168
SHIFT = 64


def packed(first, second):
    n = first.shape[1]
    blank = jnp.zeros((1, SHIFT - (n - 128)), F32)
    rests = jnp.concatenate([first[:, 128:], blank, second[:, 128:], blank], axis=1)
    return jnp.concatenate([first[:, :128], rests, second[:, :128]], axis=1)


def own_kernel(parts, uph, upl, own_ref, top_ref):
    n = parts.shape[1]
    fine = (parts[0] + parts[1] + parts[2] + parts[3])[:, 0, :]
    own_ref[pl.ds(0, n), :] = fine
    mid = raised(fine, uph, upl)
    rows = jnp.transpose(mid)[:16]
    own_ref[pl.ds(MID_AT, 16), :] = rows[:, :128]
    own_ref[pl.ds(MID_AT + 16, 16), pl.ds(0, n - 128)] = rows[:, 128:]
    rows = jnp.transpose(raised(mid, uph, upl))
    row = packed(rows[:1], rows[1:2])
    for i in range(top_ref.shape[0]):
        top_ref[i] = row


def own_moments(parts, uph, upl, copies):
    return pl.pallas_call(
        own_kernel,
        out_shape=(VMEM((MID_AT + 32, 128), F32), VMEM((copies, 1, 384), F32)),
        in_specs=[pl.BlockSpec(memory_space=VMEM)] * 3,
        out_specs=(pl.BlockSpec(memory_space=VMEM),) * 2,
        compiler_params=pltpu.CompilerParams(vmem_limit_bytes=4 << 20),
        name="own_moments",
    )(parts, uph, upl)


def line_kernel(line, out):
    rows = line[:, 0, :]
    for i in range(out.shape[0]):
        out[i] = rows


def line_copies(line, copies):
    return pl.pallas_call(
        line_kernel,
        out_shape=jax.ShapeDtypeStruct((copies, line.shape[0], line.shape[2]), F32),
        in_specs=[pl.BlockSpec(memory_space=VMEM)],
        out_specs=pl.BlockSpec(memory_space=VMEM),
        compiler_params=pltpu.CompilerParams(vmem_limit_bytes=2 << 20),
        name="line_copies",
    )(line)


GROUP = 4


def near_kernel(place, left, own, right, fl, ml, ops_hbm, fine_out, mid_out, ops, full, rows, mids, mid_rows, xa, xb, acc_a, acc_b, sems):
    slots, n = ops.shape[0], ops.shape[1]
    groups = -(-slots // GROUP)
    size = [min(GROUP, slots - k * GROUP) for k in range(groups)]
    copies = []
    for k in range(0, groups, 2):
        at = pl.ds(k * GROUP, sum(size[k : k + 2]))
        copies.append(pltpu.make_async_copy(ops_hbm.at[at], ops.at[at], sems.at[k // 2]))
        copies[-1].start()
    rows[...] = jnp.zeros_like(rows)
    for i, ref in enumerate((left, own, right)):
        full[i] = ref[pl.ds(0, n), :]
        rows[pl.ds(16 * i, 16), pl.ds(0, 128)] = ref[pl.ds(MID_AT, 16), :]
        rows[pl.ds(16 * i, 16), pl.ds(128, n - 128)] = ref[pl.ds(MID_AT + 16, 16), pl.ds(0, n - 128)]
    mid = jnp.transpose(rows[...])[:n]
    mids[:, pl.ds(0, 128)], mids[:, pl.ds(128, 128)] = split(mid)
    anchor = place[0] * 128 - 128
    mid_anchor = place[0] * 16 - 16
    lane = lax.broadcasted_iota(I32, (1, 128), 1)
    part = (lane // 16) % 2 * 128
    listed = ml[...]
    listed = jnp.where(listed >= 0, listed - mid_anchor, -1).astype(F32).astype(BF16)
    spread = ones_where((16, 128), lambda r, c: c % 16 == r)
    mid_rows[...] = lax.dot_general(listed, spread, (((0,), (0,)), ((), ())), preferred_element_type=F32).astype(I32)
    acc_a[...] = jnp.zeros_like(acc_a)
    acc_b[...] = jnp.zeros_like(acc_b)

    def load(k, count, xs):
        row = jnp.full((1, 128), -1, I32)
        for jj in range(count):
            row = jnp.where(lane // 32 == jj, mid_rows[pl.ds(k * GROUP + jj, 1), :], row)
        row = jnp.where(row >= 0, row + part, -1)
        source = lax.broadcasted_iota(I32, (256, 128), 0)
        tile = mm(mids[...], (source == row).astype(F32).astype(BF16)).astype(BF16)
        for jj in range(count):
            xs[jj, :, pl.ds(128, 128)] = jnp.where(lane // 32 == jj, tile, jnp.zeros_like(tile))
            row = fl[pl.ds(k * GROUP + jj, 1), :]
            row = jnp.where(row >= 0, row - anchor, 512)
            index = jnp.broadcast_to(row & 127, (n, 128))
            got = jnp.zeros((n, 128), F32)
            for i in range(3):
                moved = jnp.take_along_axis(full[i], index, axis=1, mode="promise_in_bounds")
                got = jnp.where(row >> 7 == i, moved, got)
            xs[jj, :, pl.ds(0, 128)], xs[jj, :, pl.ds(256, 128)] = split(got)

    def use(k, count, xs):
        a = b = None
        for jj in range(count):
            oh, ol = split(ops[k * GROUP + jj])
            x = xs[jj]
            ta = mm(oh, x[:, :256]) + mm(ol, x[:, :256])
            tb = mm(oh, x[:, 256:])
            a = ta if a is None else a + ta
            b = tb if b is None else b + tb
        acc_a[...] += a
        acc_b[...] += b

    load(0, GROUP, xa)

    def ready(i):
        at = pl.ds(0, 2 * GROUP)
        if isinstance(i, int):
            copies[i].wait()
        else:
            pltpu.make_async_copy(ops_hbm.at[at], ops.at[at], sems.at[i]).wait()

    def step(i, carry):
        ready(i)
        load(2 * i + 1, GROUP, xb)
        use(2 * i, GROUP, xa)
        load(2 * i + 2, GROUP, xa)
        use(2 * i + 1, GROUP, xb)
        return carry

    steady = groups // 2 - 1
    lax.fori_loop(0, steady, step, 0)
    bufs = (xa, xb)
    for k in range(2 * steady, groups):
        if k % 2 == 0:
            ready(k // 2)
        if k + 1 < groups:
            load(k + 1, size[k + 1], bufs[(k + 1) % 2])
        use(k, size[k], bufs[k % 2])
    fine_out[...] = acc_a[:, pl.ds(0, 128)] + acc_b[...]
    folded = acc_a[:, pl.ds(128, 128)]
    for shift in (64, 32, 16):
        folded = folded + pltpu.roll(folded, shift, 1)
    mid_out[...] = folded


def near_terms(place, left, own, right, fine_list, mid_list, ops):
    slots, n = ops.shape[0], ops.shape[1]
    vm = pl.BlockSpec(memory_space=VMEM)
    return pl.pallas_call(
        near_kernel,
        out_shape=(VMEM((n, 128), F32),) * 2,
        in_specs=[pl.BlockSpec(memory_space=pltpu.SMEM)] + [vm] * 5 + [pl.BlockSpec(memory_space=pltpu.HBM)],
        out_specs=(vm,) * 2,
        scratch_shapes=[
            pltpu.VMEM((slots, n, n), F32),
            pltpu.VMEM((3, n, 128), F32),
            pltpu.VMEM((128, 256), F32),
            pltpu.VMEM((n, 256), BF16),
            pltpu.VMEM((slots, 128), I32),
            pltpu.VMEM((GROUP, n, 384), BF16),
            pltpu.VMEM((GROUP, n, 384), BF16),
            pltpu.VMEM((n, 256), F32),
            pltpu.VMEM((n, 128), F32),
            pltpu.SemaphoreType.DMA((-(-slots // (2 * GROUP)),)),
        ],
        compiler_params=pltpu.CompilerParams(vmem_limit_bytes=20 << 20),
        name="near_terms",
    )(place, left, own, right, fine_list, jnp.transpose(mid_list), in_hbm(ops))


TALL = 24
FIRST = (3, 2, 2)


def far_kernel(
    place, tl, ul, table, uph, upl, fine_term, mid_term, dnh_hbm, dnl_hbm, ops_hbm, out,
    ops, dnh, dnl, tiles, rows, upper, chosen, top_col, upper_col, sems, down_sems,
):
    slots, n = ops.shape[0], ops.shape[1]
    loads = []
    for k, at in enumerate(range(0, n, TALL)):
        where = (slice(None), pl.ds(at, min(TALL, n - at)))
        loads.append(pltpu.make_async_copy(ops_hbm.at[where], ops.at[where], sems.at[k]))
    down_loads = [
        pltpu.make_async_copy(source, target, down_sems.at[k])
        for k, (source, target) in enumerate(((dnh_hbm, dnh), (dnl_hbm, dnl)))
    ]
    queue = loads + down_loads

    def begin(count):
        for _ in range(count):
            queue.pop(0).start()

    begin(FIRST[0])
    parents = rows.shape[1] - 8
    rows[:, pl.ds(parents, 8), :] = jnp.zeros((8, 8, n), F32)
    upper[...] = jnp.zeros_like(upper)
    for k in range(3):
        tiles[k] = table[:, pl.ds(128 * k, 128)]
    for q in range(4):
        first, rest, second = [tiles[k, pl.ds(q, parents, stride=4), :] for k in range(3)]
        for i, (body, tail) in enumerate(((first, rest), (second, pltpu.roll(rest, SHIFT, 1)))):
            rows[2 * q + i, pl.ds(0, parents), pl.ds(0, 128)] = body
            rows[2 * q + i, pl.ds(0, parents), pl.ds(128, n - 128)] = tail[:, : n - 128]
    begin(FIRST[1])
    total = None
    for o in range(8):
        both = jnp.concatenate(split(rows[o, pl.ds(0, parents), :]), axis=0)
        term = mm_nt(both, uph[o])
        term = term[:parents] + term[parents:] + mm_nt(both[:parents], upl[o])
        total = term if total is None else total + term
    upper[pl.ds(0, parents), :] = total
    begin(FIRST[2])
    parent = place[0] // 4
    for j in range(slots):
        for t in range(2):
            index = tl[t, j]
            index = jnp.where(index >= 0, index, parents * 8)
            chosen[3 * j + t] = jnp.broadcast_to(rows[index & 7, pl.ds(index >> 3, 1), :], (8, n))
        index = ul[j, parent]
        index = jnp.where(index >= 0, index, parents)
        chosen[3 * j + 2] = jnp.broadcast_to(upper[pl.ds(index, 1), :], (8, n))
    begin(len(queue))

    def block(start, size):
        edges = [(at, min(8, size - at)) for at in range(0, size, 8)]
        sums = [[jnp.zeros((height, n), F32)] * 3 for _, height in edges]
        for j in range(slots):
            factors = [chosen[3 * j + t] for t in range(3)]
            for part, (at, height) in zip(sums, edges, strict=True):
                piece = ops[j, pl.ds(start + at, height), :]
                for t in range(3):
                    part[t] = part[t] + piece * factors[t][:height]
        for part, (at, height) in zip(sums, edges, strict=True):
            s0, s1, s2 = [jnp.sum(s, axis=1, keepdims=True) for s in part]
            lane = lax.broadcasted_iota(I32, (height, 128), 1)
            where = pl.ds(start + at, height)
            top_col[where, :] = jnp.where(lane == 0, s0, jnp.where(lane == 1, s1, 0.0))
            upper_col[where, :] = jnp.where(lane < 2, s2, 0.0)

    def step(i, carry):
        at = pl.multiple_of(i * TALL, TALL)
        where = (slice(None), pl.ds(at, TALL))
        pltpu.make_async_copy(ops_hbm.at[where], ops.at[where], sems.at[i]).wait()
        block(at, TALL)
        return carry

    lax.fori_loop(0, n // TALL, step, 0)
    if n % TALL:
        loads[-1].wait()
        block(n // TALL * TALL, n % TALL)
    for load in down_loads:
        load.wait()
    both = jnp.concatenate(split(upper_col[...]), axis=1)
    octant = lax.rem(place[0] * 2, 8)
    lane = lax.broadcasted_iota(I32, (n, 128), 1)
    from_upper = [halves(mm(dnh[octant + i], both) + mm(dnl[octant + i], both)) for i in range(2)]
    local_top = top_col[...] + jnp.where(lane == 0, from_upper[0], jnp.where(lane == 1, from_upper[1], 0.0))
    local_mid = lowered(local_top, dnh, dnl) + mid_term[...]
    local_mid = jnp.where(lane < 16, local_mid, 0.0)
    local_fine = lowered(local_mid, dnh, dnl) + fine_term[...]
    for i in range(out.shape[0]):
        out[i] = local_fine


def far_terms(place, top_list, upper_list, table, uph, upl, dnh, dnl, fine_term, mid_term, ops, copies):
    slots, n = ops.shape[0], ops.shape[1]
    parents = table.shape[0] // 4
    vm, sm = pl.BlockSpec(memory_space=VMEM), pl.BlockSpec(memory_space=pltpu.SMEM)
    return pl.pallas_call(
        far_kernel,
        out_shape=VMEM((copies, n, 128), F32),
        in_specs=[sm] * 3 + [vm] * 5 + [pl.BlockSpec(memory_space=pltpu.HBM)] * 3,
        out_specs=vm,
        scratch_shapes=[
            pltpu.VMEM((slots, n, n), F32),
            pltpu.VMEM((8, n, n), BF16),
            pltpu.VMEM((8, n, n), BF16),
            pltpu.VMEM((3, table.shape[0], 128), F32),
            pltpu.VMEM((8, parents + 8, n), F32),
            pltpu.VMEM((parents + 8, n), F32),
            pltpu.VMEM((3 * slots, 8, n), F32),
            pltpu.VMEM((n, 128), F32),
            pltpu.VMEM((n, 128), F32),
            pltpu.SemaphoreType.DMA((-(-n // TALL),)),
            pltpu.SemaphoreType.DMA((2,)),
        ],
        compiler_params=pltpu.CompilerParams(vmem_limit_bytes=20 << 20),
        name="far_terms",
    )(
        place, jnp.transpose(top_list), upper_list, table, uph, upl, fine_term, mid_term,
        in_hbm(dnh), in_hbm(dnl), in_hbm(ops),
    )


def exponents():
    entries = []
    for degree in range(ORDER + 1):
        for along_x in range(degree, -1, -1):
            for along_y in range(degree - along_x, -1, -1):
                entries.append((along_x, along_y, degree - along_x - along_y))
    return entries


def monomial_kernel(powers, coords, high_ref, low_ref):
    value = None
    for axis in range(3):
        e = powers[:, pl.ds(axis, 1)]
        base = coords[pl.ds(axis, 1), :]
        for bit in range(4):
            factor = jnp.where((e >> bit) & 1 == 1, base, 1.0)
            value = factor if value is None else value * factor
            base = base * base
    high_ref[...], low_ref[...] = split(value)


def monomials(coords):
    table = jnp.asarray(exponents(), I32)
    n, particles = table.shape[0], coords.shape[1]
    width = 512
    return pl.pallas_call(
        monomial_kernel,
        grid=(particles // width,),
        out_shape=(jax.ShapeDtypeStruct((n, particles), BF16),) * 2,
        in_specs=[pl.BlockSpec((n, 3), lambda i: (0, 0)), pl.BlockSpec((3, width), lambda i: (0, i))],
        out_specs=(pl.BlockSpec((n, width), lambda i: (0, i)),) * 2,
        compiler_params=pltpu.CompilerParams(vmem_limit_bytes=4 << 20),
        name="monomials",
    )(table, coords)


def potential_kernel(place, parts, leaves, high_ref, low_ref, fine_ref, out):
    fine = parts[0] + parts[1] + parts[2] + parts[3]
    fine_ref[...] = fine
    fh, fl = split(jnp.transpose(fine))
    width = 512
    cell = lax.broadcasted_iota(I32, (128, width), 0) + place[0] * 128
    for k in range(out.shape[1] // width):
        at = pl.ds(k * width, width)
        mh, ml = high_ref[:, at], low_ref[:, at]
        values = mm(fh, mh) + mm(fl, mh) + mm(fh, ml)
        out[:, at] = jnp.sum(jnp.where(cell == leaves[:, at], values, 0.0), axis=0, keepdims=True)


def potentials(place, parts, leaves, high, low):
    n = parts.shape[1]
    particles = leaves.shape[1]
    vm = pl.BlockSpec(memory_space=VMEM)
    return pl.pallas_call(
        potential_kernel,
        out_shape=(jax.ShapeDtypeStruct((n, 128), F32), jax.ShapeDtypeStruct((1, particles), F32)),
        in_specs=[pl.BlockSpec(memory_space=pltpu.SMEM)] + [vm] * 4,
        out_specs=(vm,) * 2,
        compiler_params=pltpu.CompilerParams(vmem_limit_bytes=4 << 20),
        name="potentials",
    )(place, parts, leaves, high, low)


DOM = ("dom_0", "dom_1", "dom_2")
DOM_SUB = ("dom_0", "dom_1", "dom_2", "sub")


def exchanged(copies, axes):
    return lax.all_to_all(copies, axes, split_axis=0, concat_axis=0, tiled=True)


def copied(value, count):
    return jnp.broadcast_to(value, (count, *value.shape))


def shards(
    fine_partial,
    upward_ops,
    interaction_ops,
    downward_ops,
    fine_list,
    mid_list,
    top_list,
    upper_list,
    positions,
    leaf_cell,
):
    subs, slabs = lax.axis_size("sub"), lax.axis_size(DOM)
    domain = lax.axis_index(DOM).astype(I32)
    place = domain.reshape(1)
    uph, upl = split_ops(upward_ops)
    dnh, dnl = split_ops(downward_ops, pltpu.HBM)
    parts = exchanged(copied(lax.optimization_barrier(jnp.transpose(fine_partial, (1, 0, 2))), subs), "sub")
    own, tops = own_moments(parts, uph, upl, lax.axis_size(DOM[1:]))
    line = exchanged(tops, DOM[1:])
    left = lax.ppermute(own, DOM, [(i, i + 1) for i in range(slabs - 1)])
    right = lax.ppermute(own, DOM, [(i + 1, i) for i in range(slabs - 1)])
    table = exchanged(line_copies(line, lax.axis_size(DOM[0])), DOM[0])
    table = table.reshape(-1, table.shape[2])
    fine_term, mid_term = near_terms(place, left, own, right, fine_list, mid_list, interaction_ops)
    partial = far_terms(
        place, top_list, upper_list, table, uph, upl, dnh, dnl, fine_term, mid_term, interaction_ops, subs
    )
    high, low = monomials(positions)
    parts = exchanged(partial, "sub")
    local_fine, potential = potentials(place, parts, leaf_cell.reshape(1, -1), high, low)
    return local_fine, potential.reshape(-1)


def solution(mesh):
    torus = Mesh(
        mesh.devices.reshape(8, 12, 2, mesh.shape["sub"]), ("dom_0", "dom_1", "dom_2", "sub")
    )
    return jax.shard_map(
        shards,
        mesh=torus,
        in_specs=(
            P("sub", None, DOM),
            P(),
            P("sub", None, None),
            P(),
            P("sub", DOM),
            P("sub", DOM),
            P("sub", DOM),
            P("sub", None),
            P(None, DOM_SUB),
            P(DOM_SUB),
        ),
        out_specs=(P(None, DOM), P(DOM_SUB)),
        check_vma=False,
    )
```

time: 108 us -> 89.3 us (0.83)
  local copies, waits for them, and re-layouts: 15.6 us -> 1.85 us
  Pallas kernels: 35.2 us -> 25.7 us
  waiting for transfers between devices: 4.84 us -> 11 us
  starting transfers between devices: 25.4 us -> 23.8 us
    unnamed x27 -> x15, local copies, waits for them, and re-layouts: 13.9 us -> 0.95 us
    all_to_all x3, waiting for transfers between devices: 3.11 us -> 11 us  [exchanged(): return lax.all_to_all(copies, axes, split_axis=0, concat_axis=0, tiled=True)]
    pallas_call x4 -> x6, Pallas kernels: 30 us -> 22.7 us  [the longest x1 9.21 us: far_terms(): pl.pallas_call(far_kernel, out_shape=VMEM((copies, n, 128), F32), in_spec...]
    pallas_call x1, Pallas kernels: 4 us -> 1.82 us  [monomials(): pl.pallas_call(monomial_kernel, grid=(particles // width,), out_shape=(ja...]
    ppermute x2, waiting for transfers between devices: 1.73 us -> 0.01 us  [the longest x1 0.01 us: shards(): left = lax.ppermute(own, DOM, [(i, i + 1) for i in range(slabs - 1)])]
    all_to_all x3, starting transfers between devices: 16.3 us -> 15 us  [exchanged(): return lax.all_to_all(copies, axes, split_axis=0, concat_axis=0, tiled=True)]
  transfers between devices with their start and end apart: 5 -> 5, of which waited for: 3 -> 2; matrix products, arithmetic and copies ran while one was open for 0% -> 0% of each run, Pallas kernels for 20% -> 14%
where the time goes in v3:
time: 89.3 us; the launch traced here: 88.8 us
  Pallas kernels  25.7 us (29%)
  blocking collectives  25.5 us (29%)
  starting transfers between devices  23.8 us (27%)
  waiting for transfers between devices  11 us (12%)
  local copies, waits for them, and re-layouts  1.85 us (2%)
    all_to_all x1, blocking collectives, exchanged(): return lax.all_to_all(copies, axes, split_axis=0, concat_axis=0, tiled=True)  25.5 us
    all_to_all x3, starting transfers between devices, exchanged(): return lax.all_to_all(copies, axes, split_axis=0, concat_axis=0, tiled=True)  15 us
    all_to_all x3, waiting for transfers between devices, exchanged(): return lax.all_to_all(copies, axes, split_axis=0, concat_axis=0, tiled=True)  11 us
    pallas_call x1, Pallas kernels, far_terms(): pl.pallas_call(far_kernel, out_shape=VMEM((copies, n, 128), F32), in_spec...  9.21 us
    ppermute x1, starting transfers between devices, shards(): right = lax.ppermute(own, DOM, [(i + 1, i) for i in range(slabs - 1)])  6.96 us
    pallas_call x1, Pallas kernels, near_terms(): pl.pallas_call(near_kernel, out_shape=(VMEM((n, 128), F32),) * 2, in_spec...  6.43 us
    pallas_call x2, Pallas kernels, split_ops(): pl.pallas_call(split_kernel, out_shape=(kept((8, n, n), BF16),) * 2, in_s...  4.5 us
    ppermute x1, starting transfers between devices, shards(): left = lax.ppermute(own, DOM, [(i, i + 1) for i in range(slabs - 1)])  1.91 us
  transfers between devices with their start and end apart: 5, of which 2 were waited for; matrix products, arithmetic and copies ran while one was open for 0% of the time, Pallas kernels for 14%

profile of v3, /device:TPU:32, one launch (start us, length us, event | category | flops | bytes accessed | tf_op | source)
XLA Modules:
  0.0 88.8 jit_solution(7457788827369816035)
XLA Ops:
  0.6 0.9 %copy.15 = f32[165,1,128]{2,0,1:T(8,128)S(1)} copy(f32[165,1,128]{2,1,0:T(1,128)} %bitcast.19) | data formatting | bytes 168960
  1.5 0.9 %broadcast_in_dim.3 = f32[4,165,1,128]{3,2,1,0:T(1,128)} broadcast(f32[165,128]{1,0:T(8,128)S(1)} %bitcast.18), dimensions={1,3} | broadcast | bytes 422400 | tf_op jit(solution)/shard_map/broadcast_in_dim | solution.py:456
  2.4 4.3 %all-to-all-start = ((f32[4,165,1,128]{3,2,1,0:T(1,128)}), f32[4,165,1,128]{3,2,1,0:T(1,128)S(1)}, u32[]{:S(2)}, u32[]{:S(2)}) async-start(f32[4,165,1,128]{3,2,1,0:T(1,128)} %broadcast_in_dim.3), calls=%async_computation | async-start | bytes 675840 | tf_op jit(solution)/shard_map/all_to_all | solution.py:452
  6.7 1.7 %shard_map.122 = (bf16[8,165,165]{2,1,0:T(8,128)(2,1)S(1)}, bf16[8,165,165]{2,1,0:T(8,128)(2,1)S(1)}) custom-call(f32[165,8,165]{2,1,0:T(8,128)} %bitcast.16), custom_call_target="tpu_custom_call" | custom-call | tf_op jit(solution)/shard_map/pallas_call | solution.py:78
  8.4 5.8 %all-to-all-done.parts = f32[4,165,1,128]{3,2,1,0:T(1,128)S(1)} async-done(((f32[4,165,1,128]{3,2,1,0:T(1,128)}), f32[4,165,1,128]{3,2,1,0:T(1,128)S(1)}, u32[]{:S(2)}, u32[]{:S(2)}) %all-to-all-start) | async-done | bytes 337952 | tf_op jit(solution)/shard_map/all_to_all | solution.py:452
  14.2 1.8 %own_moments.1 = (f32[200,128]{1,0:T(8,128)S(1)}, f32[24,1,384]{2,1,0:T(1,128)S(1)}) custom-call(f32[4,165,1,128]{3,2,1,0:T(1,128)S(1)} %all-to-all-done.parts, bf16[8,165,165]{2,1,0:T(8,128)(2,1)S(1)} %get-tuple-element.14.uph, bf16[8,165,165]{2,1,0:T(8,128)(2,1)S(1)} %get-tuple-element.15.upl), custom_call_target="tpu_custom_call" | custom-call | tf_op jit(solution)/shard_map/own_moments/pallas_call | solution.py:114
  16.0 0.0 copy-start.2
  16.1 0.0 copy-start.5
  16.1 25.5 %all_to_all.20.line = f32[24,1,384]{2,1,0:T(1,128)S(1)} all-to-all(f32[24,1,384]{2,1,0:T(1,128)S(1)} %get-tuple-element.16), channel_id=1, replica_groups=mesh['dom_0'=8,'dom_1'=12,'dom_2'=2,'sub'=4] {'dom_1','dom_2'}, dimensions={0} | all-to-all | bytes 73728 | tf_op jit(solution)/shard_map/all_to_all | solution.py:452
  41.5 0.7 line_copies.1
  42.3 7.2 %all-to-all-start.2 = ((f32[8,24,384]{2,1,0:T(8,128)}), f32[8,24,384]{2,1,0:T(8,128)S(1)}, u32[]{:S(2)}, u32[]{:S(2)}) async-start(f32[8,24,384]{2,1,0:T(8,128)} %line_copies.1), calls=%async_computation.2 | async-start | bytes 589824 | tf_op jit(solution)/shard_map/all_to_all | solution.py:452
  49.5 1.9 %collective-permute-start = (f32[200,128]{1,0:T(8,128)S(1)}, f32[200,128]{1,0:T(8,128)S(1)}, u32[]{:S(2)}, u32[]{:S(2)}) collective-permute-start(f32[200,128]{1,0:T(8,128)S(1)} %get-tuple-element.17.own), channel_id=1, source_target_pairs={{0,4},{4,8},{8,12},{12,16},{16,20},{20,24},{24,28},{28,32},{32,36}... | collective-permute-start | bytes 307208 | tf_op jit(solution)/shard_map/ppermute | solution.py:479
  51.4 7.0 %collective-permute-start.1 = (f32[200,128]{1,0:T(8,128)S(1)}, f32[200,128]{1,0:T(8,128)S(1)}, u32[]{:S(2)}, u32[]{:S(2)}) collective-permute-start(f32[200,128]{1,0:T(8,128)S(1)} %get-tuple-element.17.own), channel_id=1, source_target_pairs={{4,0},{8,4},{12,8},{16,12},{20,16},{24,20},{28,24},{32,28},{36,32}... | collective-permute-start | bytes 307208 | tf_op jit(solution)/shard_map/ppermute | solution.py:480
  58.4 2.8 %shard_map.123 = (bf16[8,165,165]{2,1,0:T(8,128)(2,1)}, bf16[8,165,165]{2,1,0:T(8,128)(2,1)}) custom-call(f32[165,8,165]{2,1,0:T(8,128)} %bitcast.17), custom_call_target="tpu_custom_call" | custom-call | tf_op jit(solution)/shard_map/pallas_call | solution.py:78
  61.2 0.0 collective-permute-done.left
  61.2 0.0 collective-permute-done.1.right
  61.2 0.0 copy-done.2
  61.2 0.0 copy-done.5
  61.2 0.0 copy-start.3
  61.2 0.0 copy-start.6
  61.3 6.4 %near_terms.1 = (f32[165,128]{1,0:T(8,128)S(1)}, f32[165,128]{1,0:T(8,128)S(1)}) custom-call(s32[1]{0:T(128)} %bitcast.place, f32[200,128]{1,0:T(8,128)S(1)} %collective-permute-done.left, f32[200,128]{1,0:T(8,128)S(1)} %get-tuple-element.17.own, f32[200,128]{1,0:T(8,128)S(1)} %collective-permute-done.1.right, s32[47,128]{1,0:T(8,128)S(1)} %copy-done.2, ...), custom_call_target="tpu_custom_call" | custom-call | tf_op jit(solution)/shard_map/near_terms/pallas_call | solution.py:237
  67.7 0.0 all-to-all-done.2
  67.7 0.0 copy-done.3
  67.7 0.0 copy-done.6
  67.7 0.0 copy-start
  67.7 0.0 copy-start.1
  67.7 0.0 copy-start.4
  67.8 9.2 %far_terms.1 = f32[4,165,128]{2,1,0:T(8,128)} custom-call(s32[1]{0:T(128)} %bitcast.place, s32[2,47]{1,0:T(2,128)S(1)} %bitcast.15, s32[47,48]{1,0:T(8,128)S(1)} %copy-done.3, f32[192,384]{1,0:T(8,128)S(1)} %bitcast.12, bf16[8,165,165]{2,1,0:T(8,128)(2,1)S(1)} %get-tuple-element.14.uph, bf16[8,165,165]{2,1,0:T(8,128)(2,1)S(1)} %get-tuple-element.15.upl, ...), custom_call_target="tpu_custom_call" | custom-call | tf_op jit(solution)/shard_map/far_terms/pallas_call | solution.py:358
  77.0 3.5 %all-to-all-start.3 = ((f32[4,165,128]{2,1,0:T(8,128)}), f32[4,165,128]{2,1,0:T(8,128)S(1)}, u32[]{:S(2)}, u32[]{:S(2)}) async-start(f32[4,165,128]{2,1,0:T(8,128)} %far_terms.1), calls=%async_computation.3 | async-start | bytes 688128 | tf_op jit(solution)/shard_map/all_to_all | solution.py:452
  80.5 0.0 copy-done
  80.5 0.0 copy-done.1
  80.5 1.8 %monomials.1 = (bf16[165,2048]{1,0:T(8,128)(2,1)S(1)}, bf16[165,2048]{1,0:T(8,128)(2,1)S(1)}) custom-call(s32[165,3]{1,0:T(8,128)S(1)} %copy-done, f32[3,2048]{1,0:T(4,128)S(1)} %copy-done.1), custom_call_target="tpu_custom_call" | custom-call | tf_op jit(solution)/shard_map/monomials/pallas_call | solution.py:409
  82.3 5.2 %all-to-all-done.3.parts = f32[4,165,128]{2,1,0:T(8,128)S(1)} async-done(((f32[4,165,128]{2,1,0:T(8,128)}), f32[4,165,128]{2,1,0:T(8,128)S(1)}, u32[]{:S(2)}, u32[]{:S(2)}) %all-to-all-start.3) | async-done | bytes 337952 | tf_op jit(solution)/shard_map/all_to_all | solution.py:452
  87.5 0.0 copy-done.4
  87.5 1.2 %potentials.1 = (f32[165,128]{1,0:T(8,128)}, f32[1,2048]{1,0:T(1,128)}) custom-call(s32[1]{0:T(128)} %bitcast.place, f32[4,165,128]{2,1,0:T(8,128)S(1)} %all-to-all-done.3.parts, s32[1,2048]{1,0:T(1,128)S(1)} %bitcast.13, bf16[165,2048]{1,0:T(8,128)(2,1)S(1)} %get-tuple-element.22.high_ref, bf16[165,2048]{1,0:T(8,128)(2,1)S(1)} %get-tuple-element.23.low_ref), custom_call_target="tpu_custom_call" | custom-call | tf_op jit(solution)/shard_map/potentials/pallas_call | solution.py:437
Async XLA Ops:
  2.4 11.8 %all-to-all-start = ((f32[4,165,1,128]{3,2,1,0:T(1,128)}), f32[4,165,1,128]{3,2,1,0:T(1,128)S(1)}, u32[]{:S(2)}, u32[]{:S(2)}) async-start(f32[4,165,1,128]{3,2,1,0:T(1,128)} %broadcast_in_dim.3), calls=%async_computation | async-start | bytes 675840 | tf_op jit(solution)/shard_map/all_to_all | solution.py:452
  16.0 45.2 %copy-start.2 = (s32[47,128]{1,0:T(8,128)S(1)}, s32[47,128]{1,0:T(8,128)}, u32[]{:S(2)}) copy-start(s32[47,128]{1,0:T(8,128)} %fl.1) | copy-start | bytes 72196
  16.1 45.2 %copy-start.5 = (s32[47,16]{0,1:T(8,128)S(1)}, s32[47,16]{0,1:T(8,128)}, u32[]{:S(2)}) copy-start(s32[47,16]{0,1:T(8,128)} %param.16) | copy-start | bytes 9028
  42.3 25.4 %all-to-all-start.2 = ((f32[8,24,384]{2,1,0:T(8,128)}), f32[8,24,384]{2,1,0:T(8,128)S(1)}, u32[]{:S(2)}, u32[]{:S(2)}) async-start(f32[8,24,384]{2,1,0:T(8,128)} %line_copies.1), calls=%async_computation.2 | async-start | bytes 589824 | tf_op jit(solution)/shard_map/all_to_all | solution.py:452
  49.5 11.7 %collective-permute-start = (f32[200,128]{1,0:T(8,128)S(1)}, f32[200,128]{1,0:T(8,128)S(1)}, u32[]{:S(2)}, u32[]{:S(2)}) collective-permute-start(f32[200,128]{1,0:T(8,128)S(1)} %get-tuple-element.17.own), channel_id=1, source_target_pairs={{0,4},{4,8},{8,12},{12,16},{16,20},{20,24},{24,28},{28,32},{32,36}... | collective-permute-start | bytes 307208 | tf_op jit(solution)/shard_map/ppermute | solution.py:479
  51.4 9.8 %collective-permute-start.1 = (f32[200,128]{1,0:T(8,128)S(1)}, f32[200,128]{1,0:T(8,128)S(1)}, u32[]{:S(2)}, u32[]{:S(2)}) collective-permute-start(f32[200,128]{1,0:T(8,128)S(1)} %get-tuple-element.17.own), channel_id=1, source_target_pairs={{4,0},{8,4},{12,8},{16,12},{20,16},{24,20},{28,24},{32,28},{36,32}... | collective-permute-start | bytes 307208 | tf_op jit(solution)/shard_map/ppermute | solution.py:480
  61.2 6.5 %copy-start.3 = (s32[47,48]{1,0:T(8,128)S(1)}, s32[47,48]{1,0:T(8,128)}, u32[]{:S(2)}) copy-start(s32[47,48]{1,0:T(8,128)} %ul.1) | copy-start | bytes 27076
  61.2 6.5 %copy-start.6 = (s32[47,2]{0,1:T(2,128)S(1)}, s32[47,2]{0,1:T(2,128)}, u32[]{:S(2)}) copy-start(s32[47,2]{0,1:T(2,128)} %param.17) | copy-start | bytes 1132
  67.7 12.7 %copy-start = (s32[165,3]{1,0:T(8,128)S(1)}, s32[165,3]{1,0:T(8,128)}, u32[]{:S(2)}) copy-start(s32[165,3]{1,0:T(8,128)} %constant.21.clone.powers) | copy-start | bytes 5944
  67.7 12.7 %copy-start.1 = (f32[3,2048]{1,0:T(4,128)S(1)}, f32[3,2048]{1,0:T(4,128)}, u32[]{:S(2)}) copy-start(f32[3,2048]{1,0:T(4,128)} %coords.1) | copy-start | bytes 73732
  67.7 19.8 %copy-start.4 = (s32[2048]{0:T(1024)S(1)}, s32[2048]{0:T(1024)}, u32[]{:S(2)}) copy-start(s32[2048]{0:T(1024)} %param.20) | copy-start | bytes 24580
  77.0 10.6 %all-to-all-start.3 = ((f32[4,165,128]{2,1,0:T(8,128)}), f32[4,165,128]{2,1,0:T(8,128)S(1)}, u32[]{:S(2)}, u32[]{:S(2)}) async-start(f32[4,165,128]{2,1,0:T(8,128)} %far_terms.1), calls=%async_computation.3 | async-start | bytes 688128 | tf_op jit(solution)/shard_map/all_to_all | solution.py:452

commit v4 on v3

--- a/solution.py
+++ b/solution.py
@@ -64,25 +64,62 @@
     return octant_sum(dnh, dnl, gathered(*split(expansion), child))
 
 
-def split_kernel(ops_hbm, high, low, parts, sems):
+PITCH = 56
+
+
+def split_kernel(ops_hbm, *refs):
+    count = (len(refs) - 4) // 2
+    small, (high, low), kept, (parts, sems) = refs[:count], refs[count : count + 2], refs[count + 2 : -2], refs[-2:]
     copies = [pltpu.make_async_copy(ops_hbm.at[:, o, :], parts.at[o], sems.at[o]) for o in range(8)]
     for copy in copies:
         copy.start()
+    if small:
+        top = small[0][...]
+        kept[0][...] = jnp.where(top >= 0, (top & 7) * PITCH + (top >> 3), PITCH - 8)
+        upper = small[1][...]
+        kept[1][...] = jnp.where(upper >= 0, upper, PITCH - 8)
+    for source, target in zip(small[2:], kept[2:], strict=True):
+        target[...] = source[...]
     for o in range(8):
         copies[o].wait()
         high[o], low[o] = split(parts[o])
 
 
-def split_ops(ops, kept=VMEM):
+def split_ops(ops, kept=VMEM, small=()):
     n = ops.shape[1]
+    vm = pl.BlockSpec(memory_space=VMEM)
     return pl.pallas_call(
         split_kernel,
-        out_shape=(kept((8, n, n), BF16),) * 2,
-        in_specs=[pl.BlockSpec(memory_space=pltpu.HBM)],
-        out_specs=(pl.BlockSpec(memory_space=VMEM),) * 2,
+        out_shape=(kept((8, n, n), BF16),) * 2 + tuple(VMEM(x.shape, x.dtype) for x in small),
+        in_specs=[pl.BlockSpec(memory_space=pltpu.HBM)] + [vm] * len(small),
+        out_specs=(vm,) * (2 + len(small)),
         scratch_shapes=[pltpu.VMEM((8, n, n), F32), pltpu.SemaphoreType.DMA((8,))],
         compiler_params=pltpu.CompilerParams(vmem_limit_bytes=8 << 20),
-    )(in_hbm(jnp.transpose(ops, (1, 0, 2))))
+    )(in_hbm(jnp.transpose(ops, (1, 0, 2))), *(in_hbm(x) for x in small))
+
+
+def copies_kernel(part_hbm, out_hbm, buffer, sems):
+    load = pltpu.make_async_copy(part_hbm, buffer, sems.at[0])
+    load.start()
+    load.wait()
+    stores = [pltpu.make_async_copy(buffer, out_hbm.at[i], sems.at[i + 1]) for i in range(out_hbm.shape[0])]
+    for store in stores:
+        store.start()
+    for store in stores:
+        store.wait()
+
+
+def part_copies(part, copies):
+    hbm = pl.BlockSpec(memory_space=pltpu.HBM)
+    return pl.pallas_call(
+        copies_kernel,
+        out_shape=pltpu.HBM((copies, *part.shape), F32),
+        in_specs=[hbm],
+        out_specs=hbm,
+        scratch_shapes=[pltpu.VMEM(part.shape, F32), pltpu.SemaphoreType.DMA((copies + 1,))],
+        compiler_params=pltpu.CompilerParams(vmem_limit_bytes=2 << 20),
+        name="part_copies",
+    )(in_hbm(part))
 
 
 MID_AT = 168
@@ -122,7 +159,7 @@
 
 
 def line_kernel(line, out):
-    rows = line[:, 0, :]
+    rows = jnp.concatenate([line[r ^ 1] for r in range(line.shape[0] - 1, -1, -1)], axis=0)
     for i in range(out.shape[0]):
         out[i] = rows
 
@@ -141,7 +178,7 @@
 GROUP = 4
 
 
-def near_kernel(place, left, own, right, fl, ml, ops_hbm, fine_out, mid_out, ops, full, rows, mids, mid_rows, xa, xb, acc_a, acc_b, sems):
+def near_kernel(place, outer, own, partner, fl, ml, ops_hbm, fine_out, mid_out, ops, full, rows, mids, mid_rows, xa, xb, acc_a, acc_b, sems):
     slots, n = ops.shape[0], ops.shape[1]
     groups = -(-slots // GROUP)
     size = [min(GROUP, slots - k * GROUP) for k in range(groups)]
@@ -151,10 +188,12 @@
         copies.append(pltpu.make_async_copy(ops_hbm.at[at], ops.at[at], sems.at[k // 2]))
         copies[-1].start()
     rows[...] = jnp.zeros_like(rows)
-    for i, ref in enumerate((left, own, right)):
+    second = lax.rem(place[0], 2)
+    for i, ref in ((2 * second, outer), (1, own), (2 - 2 * second, partner)):
+        at = pl.ds(pl.multiple_of(16 * i, 16), 16)
         full[i] = ref[pl.ds(0, n), :]
-        rows[pl.ds(16 * i, 16), pl.ds(0, 128)] = ref[pl.ds(MID_AT, 16), :]
-        rows[pl.ds(16 * i, 16), pl.ds(128, n - 128)] = ref[pl.ds(MID_AT + 16, 16), pl.ds(0, n - 128)]
+        rows[at, pl.ds(0, 128)] = ref[pl.ds(MID_AT, 16), :]
+        rows[at, pl.ds(128, n - 128)] = ref[pl.ds(MID_AT + 16, 16), pl.ds(0, n - 128)]
     mid = jnp.transpose(rows[...])[:n]
     mids[:, pl.ds(0, 128)], mids[:, pl.ds(128, 128)] = split(mid)
     anchor = place[0] * 128 - 128
@@ -231,7 +270,7 @@
     mid_out[...] = folded
 
 
-def near_terms(place, left, own, right, fine_list, mid_list, ops):
+def near_terms(place, outer, own, partner, fine_list, mid_list, ops):
     slots, n = ops.shape[0], ops.shape[1]
     vm = pl.BlockSpec(memory_space=VMEM)
     return pl.pallas_call(
@@ -253,18 +292,25 @@
         ],
         compiler_params=pltpu.CompilerParams(vmem_limit_bytes=20 << 20),
         name="near_terms",
-    )(place, left, own, right, fine_list, jnp.transpose(mid_list), in_hbm(ops))
+    )(place, outer, own, partner, fine_list, mid_list, in_hbm(ops))
 
 
 TALL = 24
+UNROLL = 8
 FIRST = (3, 2, 2)
 
 
 def far_kernel(
-    place, tl, ul, table, uph, upl, fine_term, mid_term, dnh_hbm, dnl_hbm, ops_hbm, out,
-    ops, dnh, dnl, tiles, rows, upper, chosen, top_col, upper_col, sems, down_sems,
+    place, tl_ref, ul_ref, table, uph, upl, fine_term, mid_term, dnh_hbm, dnl_hbm, ops_hbm, out,
+    ops, dnh, dnl, tiles, rows, upper, chosen, top_col, upper_col, tl, ul, sems, down_sems, list_sems,
 ):
     slots, n = ops.shape[0], ops.shape[1]
+    lists = [
+        pltpu.make_async_copy(source, target, list_sems.at[k])
+        for k, (source, target) in enumerate(((tl_ref, tl), (ul_ref, ul)))
+    ]
+    for copy in lists:
+        copy.start()
     loads = []
     for k, at in enumerate(range(0, n, TALL)):
         where = (slice(None), pl.ds(at, min(TALL, n - at)))
@@ -280,34 +326,45 @@
             queue.pop(0).start()
 
     begin(FIRST[0])
-    parents = rows.shape[1] - 8
-    rows[:, pl.ds(parents, 8), :] = jnp.zeros((8, 8, n), F32)
+    parents = PITCH - 8
+    rows[pl.ds(parents, 8), :] = jnp.zeros((8, n), F32)
     upper[...] = jnp.zeros_like(upper)
+    lines = table.shape[0] // 24
     for k in range(3):
-        tiles[k] = table[:, pl.ds(128 * k, 128)]
+        for i in range(lines):
+            tiles[k, pl.ds(24 * (lines - 1 - i), 24), :] = table[pl.ds(24 * i, 24), pl.ds(128 * k, 128)]
     for q in range(4):
         first, rest, second = [tiles[k, pl.ds(q, parents, stride=4), :] for k in range(3)]
         for i, (body, tail) in enumerate(((first, rest), (second, pltpu.roll(rest, SHIFT, 1)))):
-            rows[2 * q + i, pl.ds(0, parents), pl.ds(0, 128)] = body
-            rows[2 * q + i, pl.ds(0, parents), pl.ds(128, n - 128)] = tail[:, : n - 128]
+            at = pl.ds((2 * q + i) * PITCH, parents)
+            rows[at, pl.ds(0, 128)] = body
+            rows[at, pl.ds(128, n - 128)] = tail[:, : n - 128]
     begin(FIRST[1])
     total = None
     for o in range(8):
-        both = jnp.concatenate(split(rows[o, pl.ds(0, parents), :]), axis=0)
+        both = jnp.concatenate(split(rows[pl.ds(o * PITCH, parents), :]), axis=0)
         term = mm_nt(both, uph[o])
         term = term[:parents] + term[parents:] + mm_nt(both[:parents], upl[o])
         total = term if total is None else total + term
     upper[pl.ds(0, parents), :] = total
     begin(FIRST[2])
     parent = place[0] // 4
-    for j in range(slots):
+    for copy in lists:
+        copy.wait()
+
+    def choose(j):
         for t in range(2):
-            index = tl[t, j]
-            index = jnp.where(index >= 0, index, parents * 8)
-            chosen[3 * j + t] = jnp.broadcast_to(rows[index & 7, pl.ds(index >> 3, 1), :], (8, n))
-        index = ul[j, parent]
-        index = jnp.where(index >= 0, index, parents)
-        chosen[3 * j + 2] = jnp.broadcast_to(upper[pl.ds(index, 1), :], (8, n))
+            chosen[3 * j + t] = jnp.broadcast_to(rows[pl.ds(tl[t, j], 1), :], (8, n))
+        chosen[3 * j + 2] = jnp.broadcast_to(upper[pl.ds(ul[j, parent], 1), :], (8, n))
+
+    def some(i, carry):
+        for k in range(UNROLL):
+            choose(i * UNROLL + k)
+        return carry
+
+    lax.fori_loop(0, slots // UNROLL, some, 0)
+    for j in range(slots // UNROLL * UNROLL, slots):
+        choose(j)
     begin(len(queue))
 
     def block(start, size):
@@ -358,25 +415,28 @@
     return pl.pallas_call(
         far_kernel,
         out_shape=VMEM((copies, n, 128), F32),
-        in_specs=[sm] * 3 + [vm] * 5 + [pl.BlockSpec(memory_space=pltpu.HBM)] * 3,
+        in_specs=[sm] + [vm] * 7 + [pl.BlockSpec(memory_space=pltpu.HBM)] * 3,
         out_specs=vm,
         scratch_shapes=[
             pltpu.VMEM((slots, n, n), F32),
             pltpu.VMEM((8, n, n), BF16),
             pltpu.VMEM((8, n, n), BF16),
             pltpu.VMEM((3, table.shape[0], 128), F32),
-            pltpu.VMEM((8, parents + 8, n), F32),
+            pltpu.VMEM((8 * PITCH, n), F32),
             pltpu.VMEM((parents + 8, n), F32),
             pltpu.VMEM((3 * slots, 8, n), F32),
             pltpu.VMEM((n, 128), F32),
             pltpu.VMEM((n, 128), F32),
+            pltpu.SMEM(top_list.shape, I32),
+            pltpu.SMEM(upper_list.shape, I32),
             pltpu.SemaphoreType.DMA((-(-n // TALL),)),
+            pltpu.SemaphoreType.DMA((2,)),
             pltpu.SemaphoreType.DMA((2,)),
         ],
         compiler_params=pltpu.CompilerParams(vmem_limit_bytes=20 << 20),
         name="far_terms",
     )(
-        place, jnp.transpose(top_list), upper_list, table, uph, upl, fine_term, mid_term,
+        place, top_list, upper_list, table, uph, upl, fine_term, mid_term,
         in_hbm(dnh), in_hbm(dnl), in_hbm(ops),
     )
 
@@ -409,7 +469,7 @@
     return pl.pallas_call(
         monomial_kernel,
         grid=(particles // width,),
-        out_shape=(jax.ShapeDtypeStruct((n, particles), BF16),) * 2,
+        out_shape=(pltpu.HBM((n, particles), BF16),) * 2,
         in_specs=[pl.BlockSpec((n, 3), lambda i: (0, 0)), pl.BlockSpec((3, width), lambda i: (0, i))],
         out_specs=(pl.BlockSpec((n, width), lambda i: (0, i)),) * 2,
         compiler_params=pltpu.CompilerParams(vmem_limit_bytes=4 << 20),
@@ -444,16 +504,17 @@
     )(place, parts, leaves, high, low)
 
 
-DOM = ("dom_0", "dom_1", "dom_2")
-DOM_SUB = ("dom_0", "dom_1", "dom_2", "sub")
-
-
-def exchanged(copies, axes):
-    return lax.all_to_all(copies, axes, split_axis=0, concat_axis=0, tiled=True)
-
-
-def copied(value, count):
-    return jnp.broadcast_to(value, (count, *value.shape))
+DOM = ("dom_0", "dom_1")
+DOM_SUB = ("dom_0", "dom_1", "sub")
+
+
+ORDER_1 = [i ^ 1 for i in range(23, -1, -1)]
+ORDER_0 = list(range(7, -1, -1))
+
+
+def exchanged(copies, axis, order=None):
+    groups = None if order is None else [order]
+    return lax.all_to_all(copies, axis, split_axis=0, concat_axis=0, tiled=True, axis_index_groups=groups)
 
 
 def shards(
@@ -471,16 +532,17 @@
     subs, slabs = lax.axis_size("sub"), lax.axis_size(DOM)
     domain = lax.axis_index(DOM).astype(I32)
     place = domain.reshape(1)
-    uph, upl = split_ops(upward_ops)
+    lists = (jnp.transpose(top_list), upper_list, fine_list, jnp.transpose(mid_list))
+    uph, upl, top_list, upper_list, fine_list, mid_list = split_ops(upward_ops, small=lists)
     dnh, dnl = split_ops(downward_ops, pltpu.HBM)
-    parts = exchanged(copied(lax.optimization_barrier(jnp.transpose(fine_partial, (1, 0, 2))), subs), "sub")
-    own, tops = own_moments(parts, uph, upl, lax.axis_size(DOM[1:]))
-    line = exchanged(tops, DOM[1:])
-    left = lax.ppermute(own, DOM, [(i, i + 1) for i in range(slabs - 1)])
-    right = lax.ppermute(own, DOM, [(i + 1, i) for i in range(slabs - 1)])
-    table = exchanged(line_copies(line, lax.axis_size(DOM[0])), DOM[0])
+    parts = exchanged(part_copies(jnp.transpose(fine_partial, (1, 0, 2)), subs), "sub")
+    own, tops = own_moments(parts, uph, upl, lax.axis_size(DOM[1]))
+    line = exchanged(tops, DOM[1], ORDER_1)
+    outer = lax.ppermute(own, DOM, [(i, i + 2 * (i % 2) - 1) for i in range(1, slabs - 1)])
+    partner = lax.ppermute(own, DOM, [(i, i ^ 1) for i in range(slabs)])
+    table = exchanged(line_copies(line, lax.axis_size(DOM[0])), DOM[0], ORDER_0)
     table = table.reshape(-1, table.shape[2])
-    fine_term, mid_term = near_terms(place, left, own, right, fine_list, mid_list, interaction_ops)
+    fine_term, mid_term = near_terms(place, outer, own, partner, fine_list, mid_list, interaction_ops)
     partial = far_terms(
         place, top_list, upper_list, table, uph, upl, dnh, dnl, fine_term, mid_term, interaction_ops, subs
     )
@@ -492,7 +554,7 @@
 
 def solution(mesh):
     torus = Mesh(
-        mesh.devices.reshape(8, 12, 2, mesh.shape["sub"]), ("dom_0", "dom_1", "dom_2", "sub")
+        mesh.devices.reshape(8, 24, mesh.shape["sub"]), ("dom_0", "dom_1", "sub")
     )
     return jax.shard_map(
         shards,

time: 89.3 us -> 86.2 us (0.965)
  the two profiles are of different devices: /device:TPU:32 before, /device:TPU:8 now
where the time goes in v4:
time: 86.2 us; the launch traced here: 85.5 us
  Pallas kernels  27.7 us (32%)
  blocking collectives  23.6 us (27%)
  starting transfers between devices  20.5 us (24%)
  waiting for transfers between devices  10.7 us (12%)
  local copies, waits for them, and re-layouts  2.22 us (3%)
    all_to_all x1, blocking collectives, exchanged(): lax.all_to_all(copies, axis, split_axis=0, concat_axis=0, tiled=True, axi...  23.6 us
    all_to_all x3, starting transfers between devices, exchanged(): lax.all_to_all(copies, axis, split_axis=0, concat_axis=0, tiled=True, axi...  15.3 us
    all_to_all x3, waiting for transfers between devices, exchanged(): lax.all_to_all(copies, axis, split_axis=0, concat_axis=0, tiled=True, axi...  10.6 us
    pallas_call x1, Pallas kernels, far_terms(): pl.pallas_call(far_kernel, out_shape=VMEM((copies, n, 128), F32), in_spec...  7.81 us
    pallas_call x1, Pallas kernels, near_terms(): pl.pallas_call(near_kernel, out_shape=(VMEM((n, 128), F32),) * 2, in_spec...  6.43 us
    pallas_call x2, Pallas kernels, split_ops(): pl.pallas_call(split_kernel, out_shape=(kept((8, n, n), BF16),) * 2 + tup...  5.28 us
    ppermute x1, starting transfers between devices, shards(): lax.ppermute(own, DOM, [(i, i + 2 * (i % 2) - 1) for i in range(1, slabs...  3.28 us
    pallas_call x1, Pallas kernels, monomials(): pl.pallas_call(monomial_kernel, grid=(particles // width,), out_shape=(pl...  2.81 us
  transfers between devices with their start and end apart: 5, of which 2 were waited for; matrix products, arithmetic and copies ran while one was open for 0% of the time, Pallas kernels for 17%

profile of v4, /device:TPU:8, one launch (start us, length us, event | category | flops | bytes accessed | tf_op | source)
XLA Modules:
  0.0 85.5 jit_solution(9609101724231959869)
XLA Ops:
  0.6 1.7 %part_copies.1 = f32[4,165,1,128]{3,2,1,0:T(1,128)} custom-call(f32[165,1,128]{2,1,0:T(1,128)} %bitcast.13), custom_call_target="tpu_custom_call" | custom-call | tf_op jit(solution)/shard_map/part_copies/pallas_call | solution.py:114
  2.3 4.3 %all-to-all-start = ((f32[4,165,1,128]{3,2,1,0:T(1,128)}), f32[4,165,1,128]{3,2,1,0:T(1,128)S(1)}, u32[]{:S(2)}, u32[]{:S(2)}) async-start(f32[4,165,1,128]{3,2,1,0:T(1,128)} %part_copies.1), calls=%async_computation | async-start | bytes 675840 | tf_op jit(solution)/shard_map/all_to_all | solution.py:517
  6.6 2.5 %shard_map.122 = (bf16[8,165,165]{2,1,0:T(8,128)(2,1)S(1)}, bf16[8,165,165]{2,1,0:T(8,128)(2,1)S(1)}, s32[2,47]{1,0:T(2,128)S(1)}, s32[47,48]{1,0:T(8,128)S(1)},...) custom-call(f32[165,8,165]{2,1,0:T(8,128)} %bitcast.11, s32[2,47]{1,0:T(2,128)} %bitcast.15, s32[47,48]{1,0:T(8,128)} %refs_1_.1, ...), custom_call_target="tpu_custom_call" | custom-call | tf_op jit(solution)/shard_map/pallas_call | solution.py:91
  9.1 5.0 %all-to-all-done.parts = f32[4,165,1,128]{3,2,1,0:T(1,128)S(1)} async-done(((f32[4,165,1,128]{3,2,1,0:T(1,128)}), f32[4,165,1,128]{3,2,1,0:T(1,128)S(1)}, u32[]{:S(2)}, u32[]{:S(2)}) %all-to-all-start) | async-done | bytes 337952 | tf_op jit(solution)/shard_map/all_to_all | solution.py:517
  14.1 1.8 %own_moments.1 = (f32[200,128]{1,0:T(8,128)S(1)}, f32[24,1,384]{2,1,0:T(1,128)S(1)}) custom-call(f32[4,165,1,128]{3,2,1,0:T(1,128)S(1)} %all-to-all-done.parts, bf16[8,165,165]{2,1,0:T(8,128)(2,1)S(1)} %get-tuple-element.20.uph, bf16[8,165,165]{2,1,0:T(8,128)(2,1)S(1)} %get-tuple-element.21.upl), custom_call_target="tpu_custom_call" | custom-call | tf_op jit(solution)/shard_map/own_moments/pallas_call | solution.py:151
  15.9 23.6 %all_to_all.20.line = f32[24,1,384]{2,1,0:T(1,128)S(1)} all-to-all(f32[24,1,384]{2,1,0:T(1,128)S(1)} %get-tuple-element.22), channel_id=1, replica_groups={{88,92,80,84,72,76,64,68,56,60,48,52,40,44,32,36,24,28,16,20,8,12,0,4},..., dimensions={0} | all-to-all | bytes 73728 | tf_op jit(solution)/shard_map/all_to_all | solution.py:517
  39.5 0.7 line_copies.1
  40.2 7.5 %all-to-all-start.2 = ((f32[8,24,384]{2,1,0:T(8,128)}), f32[8,24,384]{2,1,0:T(8,128)S(1)}, u32[]{:S(2)}, u32[]{:S(2)}) async-start(f32[8,24,384]{2,1,0:T(8,128)} %line_copies.1), calls=%async_computation.2 | async-start | bytes 589824 | tf_op jit(solution)/shard_map/all_to_all | solution.py:517
  47.8 3.3 %collective-permute-start = (f32[200,128]{1,0:T(8,128)S(1)}, f32[200,128]{1,0:T(8,128)S(1)}, u32[]{:S(2)}, u32[]{:S(2)}) collective-permute-start(f32[200,128]{1,0:T(8,128)S(1)} %get-tuple-element.23.own), channel_id=1, source_target_pairs={{4,8},{8,4},{12,16},{16,12},{20,24},{24,20},{28,32},{32,28},{36,40... | collective-permute-start | bytes 307208 | tf_op jit(solution)/shard_map/ppermute | solution.py:541
  51.0 1.9 %collective-permute-start.1 = (f32[200,128]{1,0:T(8,128)S(1)}, f32[200,128]{1,0:T(8,128)S(1)}, u32[]{:S(2)}, u32[]{:S(2)}) collective-permute-start(f32[200,128]{1,0:T(8,128)S(1)} %get-tuple-element.23.own), channel_id=1, source_target_pairs={{0,4},{4,0},{8,12},{12,8},{16,20},{20,16},{24,28},{28,24},{32,36},... | collective-permute-start | bytes 307208 | tf_op jit(solution)/shard_map/ppermute | solution.py:542
  53.0 2.8 %shard_map.123 = (bf16[8,165,165]{2,1,0:T(8,128)(2,1)}, bf16[8,165,165]{2,1,0:T(8,128)(2,1)}) custom-call(f32[165,8,165]{2,1,0:T(8,128)} %bitcast.12), custom_call_target="tpu_custom_call" | custom-call | tf_op jit(solution)/shard_map/pallas_call | solution.py:91
  55.8 0.0 collective-permute-done.outer
  55.8 0.0 collective-permute-done.1.partner
  55.8 6.4 %near_terms.1 = (f32[165,128]{1,0:T(8,128)S(1)}, f32[165,128]{1,0:T(8,128)S(1)}) custom-call(s32[1]{0:T(128)} %bitcast.place, f32[200,128]{1,0:T(8,128)S(1)} %collective-permute-done.outer, f32[200,128]{1,0:T(8,128)S(1)} %get-tuple-element.23.own, f32[200,128]{1,0:T(8,128)S(1)} %collective-permute-done.1.partner, s32[47,128]{1,0:T(8,128)S(1)} %get-tuple-element.24.fl, ...), custom_call_target="tpu_custom_call" | custom-call | tf_op jit(solution)/shard_map/near_terms/pallas_call | solution.py:276
  62.3 0.0 all-to-all-done.2
  62.3 0.0 copy-start.2
  62.3 0.0 copy-start.3
  62.3 0.0 copy-start.4
  62.3 7.8 %far_terms.1 = f32[4,165,128]{2,1,0:T(8,128)} custom-call(s32[1]{0:T(128)} %bitcast.place, s32[2,47]{1,0:T(2,128)S(1)} %get-tuple-element.18.tl_ref, s32[47,48]{1,0:T(8,128)S(1)} %get-tuple-element.19.ul_ref, f32[192,384]{1,0:T(8,128)S(1)} %bitcast.9, bf16[8,165,165]{2,1,0:T(8,128)(2,1)S(1)} %get-tuple-element.20.uph, ...), custom_call_target="tpu_custom_call" | custom-call | tf_op jit(solution)/shard_map/far_terms/pallas_call | solution.py:415
  70.1 3.5 %all-to-all-start.3 = ((f32[4,165,128]{2,1,0:T(8,128)}), f32[4,165,128]{2,1,0:T(8,128)S(1)}, u32[]{:S(2)}, u32[]{:S(2)}) async-start(f32[4,165,128]{2,1,0:T(8,128)} %far_terms.1), calls=%async_computation.3 | async-start | bytes 688128 | tf_op jit(solution)/shard_map/all_to_all | solution.py:517
  73.6 0.0 copy-done.2
  73.6 0.0 copy-done.3
  73.6 2.8 %monomials.1 = (bf16[165,2048]{1,0:T(8,128)(2,1)}, bf16[165,2048]{1,0:T(8,128)(2,1)}) custom-call(s32[165,3]{1,0:T(8,128)S(1)} %copy-done.2, f32[3,2048]{1,0:T(4,128)S(1)} %copy-done.3), custom_call_target="tpu_custom_call" | custom-call | tf_op jit(solution)/shard_map/monomials/pallas_call | solution.py:469
  76.4 5.6 %all-to-all-done.3.parts = f32[4,165,128]{2,1,0:T(8,128)S(1)} async-done(((f32[4,165,128]{2,1,0:T(8,128)}), f32[4,165,128]{2,1,0:T(8,128)S(1)}, u32[]{:S(2)}, u32[]{:S(2)}) %all-to-all-start.3) | async-done | bytes 337952 | tf_op jit(solution)/shard_map/all_to_all | solution.py:517
  82.1 0.0 copy-done.4
  82.1 0.0 copy-start
  82.1 1.1 %copy-done = bf16[165,2048]{1,0:T(8,128)(2,1)S(1)} copy-done((bf16[165,2048]{1,0:T(8,128)(2,1)S(1)}, bf16[165,2048]{1,0:T(8,128)(2,1)}, u32[]{:S(2)}) %copy-start) | copy-done | bytes 675864
  83.2 0.0 copy-start.1
  83.2 1.1 %copy-done.1 = bf16[165,2048]{1,0:T(8,128)(2,1)S(1)} copy-done((bf16[165,2048]{1,0:T(8,128)(2,1)S(1)}, bf16[165,2048]{1,0:T(8,128)(2,1)}, u32[]{:S(2)}) %copy-start.1) | copy-done | bytes 675864
  84.3 1.2 %potentials.1 = (f32[165,128]{1,0:T(8,128)}, f32[1,2048]{1,0:T(1,128)}) custom-call(s32[1]{0:T(128)} %bitcast.place, f32[4,165,128]{2,1,0:T(8,128)S(1)} %all-to-all-done.3.parts, s32[1,2048]{1,0:T(1,128)S(1)} %bitcast.10, bf16[165,2048]{1,0:T(8,128)(2,1)S(1)} %copy-done, bf16[165,2048]{1,0:T(8,128)(2,1)S(1)} %copy-done.1), custom_call_target="tpu_custom_call" | custom-call | tf_op jit(solution)/shard_map/potentials/pallas_call | solution.py:497
Async XLA Ops:
  2.3 11.8 %all-to-all-start = ((f32[4,165,1,128]{3,2,1,0:T(1,128)}), f32[4,165,1,128]{3,2,1,0:T(1,128)S(1)}, u32[]{:S(2)}, u32[]{:S(2)}) async-start(f32[4,165,1,128]{3,2,1,0:T(1,128)} %part_copies.1), calls=%async_computation | async-start | bytes 675840 | tf_op jit(solution)/shard_map/all_to_all | solution.py:517
  40.2 22.0 %all-to-all-start.2 = ((f32[8,24,384]{2,1,0:T(8,128)}), f32[8,24,384]{2,1,0:T(8,128)S(1)}, u32[]{:S(2)}, u32[]{:S(2)}) async-start(f32[8,24,384]{2,1,0:T(8,128)} %line_copies.1), calls=%async_computation.2 | async-start | bytes 589824 | tf_op jit(solution)/shard_map/all_to_all | solution.py:517
  47.8 8.1 %collective-permute-start = (f32[200,128]{1,0:T(8,128)S(1)}, f32[200,128]{1,0:T(8,128)S(1)}, u32[]{:S(2)}, u32[]{:S(2)}) collective-permute-start(f32[200,128]{1,0:T(8,128)S(1)} %get-tuple-element.23.own), channel_id=1, source_target_pairs={{4,8},{8,4},{12,16},{16,12},{20,24},{24,20},{28,32},{32,28},{36,40... | collective-permute-start | bytes 307208 | tf_op jit(solution)/shard_map/ppermute | solution.py:541
  51.0 4.8 %collective-permute-start.1 = (f32[200,128]{1,0:T(8,128)S(1)}, f32[200,128]{1,0:T(8,128)S(1)}, u32[]{:S(2)}, u32[]{:S(2)}) collective-permute-start(f32[200,128]{1,0:T(8,128)S(1)} %get-tuple-element.23.own), channel_id=1, source_target_pairs={{0,4},{4,0},{8,12},{12,8},{16,20},{20,16},{24,28},{28,24},{32,36},... | collective-permute-start | bytes 307208 | tf_op jit(solution)/shard_map/ppermute | solution.py:542
  62.3 11.3 %copy-start.2 = (s32[165,3]{1,0:T(8,128)S(1)}, s32[165,3]{1,0:T(8,128)}, u32[]{:S(2)}) copy-start(s32[165,3]{1,0:T(8,128)} %constant.14.clone.powers) | copy-start | bytes 5944
  62.3 11.3 %copy-start.3 = (f32[3,2048]{1,0:T(4,128)S(1)}, f32[3,2048]{1,0:T(4,128)}, u32[]{:S(2)}) copy-start(f32[3,2048]{1,0:T(4,128)} %coords.1) | copy-start | bytes 73732
  62.3 19.8 %copy-start.4 = (s32[2048]{0:T(1024)S(1)}, s32[2048]{0:T(1024)}, u32[]{:S(2)}) copy-start(s32[2048]{0:T(1024)} %param.20) | copy-start | bytes 24580
  70.1 11.9 %all-to-all-start.3 = ((f32[4,165,128]{2,1,0:T(8,128)}), f32[4,165,128]{2,1,0:T(8,128)S(1)}, u32[]{:S(2)}, u32[]{:S(2)}) async-start(f32[4,165,128]{2,1,0:T(8,128)} %far_terms.1), calls=%async_computation.3 | async-start | bytes 688128 | tf_op jit(solution)/shard_map/all_to_all | solution.py:517
  82.1 1.1 %copy-start = (bf16[165,2048]{1,0:T(8,128)(2,1)S(1)}, bf16[165,2048]{1,0:T(8,128)(2,1)}, u32[]{:S(2)}) copy-start(bf16[165,2048]{1,0:T(8,128)(2,1)} %get-tuple-element.30.high_ref) | copy-start | bytes 2027524
  83.2 1.1 %copy-start.1 = (bf16[165,2048]{1,0:T(8,128)(2,1)S(1)}, bf16[165,2048]{1,0:T(8,128)(2,1)}, u32[]{:S(2)}) copy-start(bf16[165,2048]{1,0:T(8,128)(2,1)} %get-tuple-element.31.low_ref) | copy-start | bytes 2027524

commit v5 on v4

--- a/solution.py
+++ b/solution.py
@@ -10,6 +10,8 @@
 ORDER = 8
 F32, BF16, I32 = jnp.float32, jnp.bfloat16, jnp.int32
 VMEM = pltpu.VMEM
+ORDER_0 = [6, 7, 5, 4, 3, 2, 1, 0]
+ORDER_1 = list(range(23, -1, -1))
 
 
 def split(value):
@@ -68,34 +70,38 @@
 
 
 def split_kernel(ops_hbm, *refs):
-    count = (len(refs) - 4) // 2
+    count = (len(refs) - 2) // 2 if len(refs) > 4 else 0
     small, (high, low), kept, (parts, sems) = refs[:count], refs[count : count + 2], refs[count + 2 : -2], refs[-2:]
     copies = [pltpu.make_async_copy(ops_hbm.at[:, o, :], parts.at[o], sems.at[o]) for o in range(8)]
     for copy in copies:
         copy.start()
     if small:
-        top = small[0][...]
-        kept[0][...] = jnp.where(top >= 0, (top & 7) * PITCH + (top >> 3), PITCH - 8)
-        upper = small[1][...]
-        kept[1][...] = jnp.where(upper >= 0, upper, PITCH - 8)
-    for source, target in zip(small[2:], kept[2:], strict=True):
-        target[...] = source[...]
+        place, top_ref, upper_ref, *others = small
+        top = top_ref[...]
+        kept[0][pl.ds(0, 2), :] = jnp.where(top >= 0, (top & 7) * PITCH + (top >> 3), PITCH - 8)
+        upper = upper_ref[...]
+        upper = jnp.where(upper >= 0, upper, PITCH - 8).astype(F32).astype(BF16)
+        here = ones_where((8, upper.shape[1]), lambda r, c: c == place[0] // 4)
+        kept[0][pl.ds(2, 1), :] = mm_nt(here, upper)[:1].astype(I32)
+        for source, target in zip(others, kept[1:], strict=True):
+            target[...] = source[...]
     for o in range(8):
         copies[o].wait()
         high[o], low[o] = split(parts[o])
 
 
-def split_ops(ops, kept=VMEM, small=()):
+def split_ops(ops, kept=VMEM, lists=()):
     n = ops.shape[1]
-    vm = pl.BlockSpec(memory_space=VMEM)
+    vm, sm = pl.BlockSpec(memory_space=VMEM), pl.BlockSpec(memory_space=pltpu.SMEM)
+    more = (VMEM((3, lists[1].shape[1]), I32), *(VMEM(x.shape, I32) for x in lists[3:])) if lists else ()
     return pl.pallas_call(
         split_kernel,
-        out_shape=(kept((8, n, n), BF16),) * 2 + tuple(VMEM(x.shape, x.dtype) for x in small),
-        in_specs=[pl.BlockSpec(memory_space=pltpu.HBM)] + [vm] * len(small),
-        out_specs=(vm,) * (2 + len(small)),
+        out_shape=(kept((8, n, n), BF16),) * 2 + more,
+        in_specs=[pl.BlockSpec(memory_space=pltpu.HBM)] + [sm] * bool(lists) + [vm] * (len(lists) - 1),
+        out_specs=(vm,) * (2 + len(more)),
         scratch_shapes=[pltpu.VMEM((8, n, n), F32), pltpu.SemaphoreType.DMA((8,))],
         compiler_params=pltpu.CompilerParams(vmem_limit_bytes=8 << 20),
-    )(in_hbm(jnp.transpose(ops, (1, 0, 2))), *(in_hbm(x) for x in small))
+    )(in_hbm(jnp.transpose(ops, (1, 0, 2))), *lists[:1], *(in_hbm(x) for x in lists[1:]))
 
 
 def copies_kernel(part_hbm, out_hbm, buffer, sems):
@@ -124,6 +130,8 @@
 
 MID_AT = 168
 SHIFT = 64
+TAIL = 37
+LINE_ROWS = 64
 
 
 def packed(first, second):
@@ -159,15 +167,26 @@
 
 
 def line_kernel(line, out):
-    rows = jnp.concatenate([line[r ^ 1] for r in range(line.shape[0] - 1, -1, -1)], axis=0)
+    rows = jnp.concatenate([line[ORDER_1.index(i)] for i in range(line.shape[0])], axis=0)
+    first, second, third = [rows[8 * g : 8 * g + 8, 128:256] for g in range(3)]
+    lane = lax.broadcasted_iota(I32, (8, 128), 1)
+
+    def beside(one, two, three):
+        return jnp.where(lane < TAIL, one, jnp.where(lane < 2 * TAIL, two, three))
+
+    tails = (
+        beside(first, pltpu.roll(first, 128 + TAIL - SHIFT, 1), pltpu.roll(second, 2 * TAIL, 1)),
+        beside(pltpu.roll(second, SHIFT, 1), pltpu.roll(third, TAIL, 1), pltpu.roll(third, 2 * TAIL - SHIFT, 1)),
+    )
+    packed_rows = jnp.concatenate([rows[:, :128], rows[:, 256:], *tails], axis=0)
     for i in range(out.shape[0]):
-        out[i] = rows
+        out[i] = packed_rows
 
 
 def line_copies(line, copies):
     return pl.pallas_call(
         line_kernel,
-        out_shape=jax.ShapeDtypeStruct((copies, line.shape[0], line.shape[2]), F32),
+        out_shape=jax.ShapeDtypeStruct((copies, LINE_ROWS, 128), F32),
         in_specs=[pl.BlockSpec(memory_space=VMEM)],
         out_specs=pl.BlockSpec(memory_space=VMEM),
         compiler_params=pltpu.CompilerParams(vmem_limit_bytes=2 << 20),
@@ -301,16 +320,12 @@
 
 
 def far_kernel(
-    place, tl_ref, ul_ref, table, uph, upl, fine_term, mid_term, dnh_hbm, dnl_hbm, ops_hbm, out,
-    ops, dnh, dnl, tiles, rows, upper, chosen, top_col, upper_col, tl, ul, sems, down_sems, list_sems,
+    place, listed_ref, table, uph, upl, fine_term, mid_term, dnh_hbm, dnl_hbm, ops_hbm, out,
+    ops, dnh, dnl, tiles, rows, upper, chosen, top_col, upper_col, listed, sems, down_sems, list_sem,
 ):
     slots, n = ops.shape[0], ops.shape[1]
-    lists = [
-        pltpu.make_async_copy(source, target, list_sems.at[k])
-        for k, (source, target) in enumerate(((tl_ref, tl), (ul_ref, ul)))
-    ]
-    for copy in lists:
-        copy.start()
+    list_load = pltpu.make_async_copy(listed_ref, listed, list_sem)
+    list_load.start()
     loads = []
     for k, at in enumerate(range(0, n, TALL)):
         where = (slice(None), pl.ds(at, min(TALL, n - at)))
@@ -329,13 +344,19 @@
     parents = PITCH - 8
     rows[pl.ds(parents, 8), :] = jnp.zeros((8, n), F32)
     upper[...] = jnp.zeros_like(upper)
-    lines = table.shape[0] // 24
-    for k in range(3):
-        for i in range(lines):
-            tiles[k, pl.ds(24 * (lines - 1 - i), 24), :] = table[pl.ds(24 * i, 24), pl.ds(128 * k, 128)]
+    for i, line in enumerate(ORDER_0):
+        at = LINE_ROWS * i
+        tiles[0, pl.ds(24 * line, 24), :] = table[pl.ds(at, 24), :]
+        tiles[2, pl.ds(24 * line, 24), :] = table[pl.ds(at + 24, 24), :]
+        front, back = table[pl.ds(at + 48, 8), :], table[pl.ds(at + 56, 8), :]
+        moved = (front, pltpu.roll(front, 128 - TAIL, 1), pltpu.roll(front, 128 - 2 * TAIL, 1))
+        moved += (back, pltpu.roll(back, 128 - TAIL, 1), pltpu.roll(back, 128 - 2 * TAIL, 1))
+        for g in range(3):
+            tiles[1, pl.ds(24 * line + 8 * g, 8), :] = moved[2 * g]
+            tiles[3, pl.ds(24 * line + 8 * g, 8), :] = moved[2 * g + 1]
     for q in range(4):
-        first, rest, second = [tiles[k, pl.ds(q, parents, stride=4), :] for k in range(3)]
-        for i, (body, tail) in enumerate(((first, rest), (second, pltpu.roll(rest, SHIFT, 1)))):
+        for i in range(2):
+            body, tail = [tiles[2 * i + k, pl.ds(q, parents, stride=4), :] for k in range(2)]
             at = pl.ds((2 * q + i) * PITCH, parents)
             rows[at, pl.ds(0, 128)] = body
             rows[at, pl.ds(128, n - 128)] = tail[:, : n - 128]
@@ -348,14 +369,12 @@
         total = term if total is None else total + term
     upper[pl.ds(0, parents), :] = total
     begin(FIRST[2])
-    parent = place[0] // 4
-    for copy in lists:
-        copy.wait()
+    list_load.wait()
 
     def choose(j):
         for t in range(2):
-            chosen[3 * j + t] = jnp.broadcast_to(rows[pl.ds(tl[t, j], 1), :], (8, n))
-        chosen[3 * j + 2] = jnp.broadcast_to(upper[pl.ds(ul[j, parent], 1), :], (8, n))
+            chosen[3 * j + t] = jnp.broadcast_to(rows[pl.ds(listed[t, j], 1), :], (8, n))
+        chosen[3 * j + 2] = jnp.broadcast_to(upper[pl.ds(listed[2, j], 1), :], (8, n))
 
     def some(i, carry):
         for k in range(UNROLL):
@@ -408,35 +427,34 @@
         out[i] = local_fine
 
 
-def far_terms(place, top_list, upper_list, table, uph, upl, dnh, dnl, fine_term, mid_term, ops, copies):
+def far_terms(place, listed, table, uph, upl, dnh, dnl, fine_term, mid_term, ops, copies):
     slots, n = ops.shape[0], ops.shape[1]
-    parents = table.shape[0] // 4
+    parents = table.shape[0] // LINE_ROWS * 6
     vm, sm = pl.BlockSpec(memory_space=VMEM), pl.BlockSpec(memory_space=pltpu.SMEM)
     return pl.pallas_call(
         far_kernel,
         out_shape=VMEM((copies, n, 128), F32),
-        in_specs=[sm] + [vm] * 7 + [pl.BlockSpec(memory_space=pltpu.HBM)] * 3,
+        in_specs=[sm] + [vm] * 6 + [pl.BlockSpec(memory_space=pltpu.HBM)] * 3,
         out_specs=vm,
         scratch_shapes=[
             pltpu.VMEM((slots, n, n), F32),
             pltpu.VMEM((8, n, n), BF16),
             pltpu.VMEM((8, n, n), BF16),
-            pltpu.VMEM((3, table.shape[0], 128), F32),
+            pltpu.VMEM((4, 4 * parents, 128), F32),
             pltpu.VMEM((8 * PITCH, n), F32),
             pltpu.VMEM((parents + 8, n), F32),
             pltpu.VMEM((3 * slots, 8, n), F32),
             pltpu.VMEM((n, 128), F32),
             pltpu.VMEM((n, 128), F32),
-            pltpu.SMEM(top_list.shape, I32),
-            pltpu.SMEM(upper_list.shape, I32),
+            pltpu.SMEM(listed.shape, I32),
             pltpu.SemaphoreType.DMA((-(-n // TALL),)),
             pltpu.SemaphoreType.DMA((2,)),
-            pltpu.SemaphoreType.DMA((2,)),
+            pltpu.SemaphoreType.DMA,
         ],
         compiler_params=pltpu.CompilerParams(vmem_limit_bytes=20 << 20),
         name="far_terms",
     )(
-        place, top_list, upper_list, table, uph, upl, fine_term, mid_term,
+        place, listed, table, uph, upl, fine_term, mid_term,
         in_hbm(dnh), in_hbm(dnl), in_hbm(ops),
     )
 
@@ -506,10 +524,6 @@
 
 DOM = ("dom_0", "dom_1")
 DOM_SUB = ("dom_0", "dom_1", "sub")
-
-
-ORDER_1 = [i ^ 1 for i in range(23, -1, -1)]
-ORDER_0 = list(range(7, -1, -1))
 
 
 def exchanged(copies, axis, order=None):
@@ -532,8 +546,8 @@
     subs, slabs = lax.axis_size("sub"), lax.axis_size(DOM)
     domain = lax.axis_index(DOM).astype(I32)
     place = domain.reshape(1)
-    lists = (jnp.transpose(top_list), upper_list, fine_list, jnp.transpose(mid_list))
-    uph, upl, top_list, upper_list, fine_list, mid_list = split_ops(upward_ops, small=lists)
+    lists = (place, jnp.transpose(top_list), upper_list, fine_list, jnp.transpose(mid_list))
+    uph, upl, listed, fine_list, mid_list = split_ops(upward_ops, lists=lists)
     dnh, dnl = split_ops(downward_ops, pltpu.HBM)
     parts = exchanged(part_copies(jnp.transpose(fine_partial, (1, 0, 2)), subs), "sub")
     own, tops = own_moments(parts, uph, upl, lax.axis_size(DOM[1]))
@@ -544,7 +558,7 @@
     table = table.reshape(-1, table.shape[2])
     fine_term, mid_term = near_terms(place, outer, own, partner, fine_list, mid_list, interaction_ops)
     partial = far_terms(
-        place, top_list, upper_list, table, uph, upl, dnh, dnl, fine_term, mid_term, interaction_ops, subs
+        place, listed, table, uph, upl, dnh, dnl, fine_term, mid_term, interaction_ops, subs
     )
     high, low = monomials(positions)
     parts = exchanged(partial, "sub")

time: 86.2 us -> 85.8 us (level)
  transfers between devices with their start and end apart: 5 -> 5, of which waited for: 2 -> 3; matrix products, arithmetic and copies ran while one was open for 0% -> 0% of each run, Pallas kernels for 17% -> 17%
where the time goes in v5:
time: 85.8 us; the launch traced here: 85.1 us
  Pallas kernels  27.8 us (32%)
  blocking collectives  23.3 us (27%)
  starting transfers between devices  20.3 us (24%)
  waiting for transfers between devices  10.7 us (12%)
  local copies, waits for them, and re-layouts  2.22 us (3%)
    all_to_all x1, blocking collectives, exchanged(): lax.all_to_all(copies, axis, split_axis=0, concat_axis=0, tiled=True, axi...  23.3 us
    all_to_all x3, starting transfers between devices, exchanged(): lax.all_to_all(copies, axis, split_axis=0, concat_axis=0, tiled=True, axi...  15.3 us
    all_to_all x3, waiting for transfers between devices, exchanged(): lax.all_to_all(copies, axis, split_axis=0, concat_axis=0, tiled=True, axi...  10.4 us
    pallas_call x1, Pallas kernels, far_terms(): pl.pallas_call(far_kernel, out_shape=VMEM((copies, n, 128), F32), in_spec...  7.79 us
    pallas_call x1, Pallas kernels, near_terms(): pl.pallas_call(near_kernel, out_shape=(VMEM((n, 128), F32),) * 2, in_spec...  6.43 us
    pallas_call x2, Pallas kernels, split_ops(): pl.pallas_call(split_kernel, out_shape=(kept((8, n, n), BF16),) * 2 + mor...  5.28 us
    ppermute x1, starting transfers between devices, shards(): lax.ppermute(own, DOM, [(i, i + 2 * (i % 2) - 1) for i in range(1, slabs...  3.1 us
    pallas_call x1, Pallas kernels, monomials(): pl.pallas_call(monomial_kernel, grid=(particles // width,), out_shape=(pl...  2.82 us
  transfers between devices with their start and end apart: 5, of which 3 were waited for; matrix products, arithmetic and copies ran while one was open for 0% of the time, Pallas kernels for 17%

profile of v5, /device:TPU:8, one launch (start us, length us, event | category | flops | bytes accessed | tf_op | source)
XLA Modules:
  0.0 85.1 jit_solution(13282507967361107989)
XLA Ops:
  0.6 1.7 %part_copies.1 = f32[4,165,1,128]{3,2,1,0:T(1,128)} custom-call(f32[165,1,128]{2,1,0:T(1,128)} %bitcast.13), custom_call_target="tpu_custom_call" | custom-call | tf_op jit(solution)/shard_map/part_copies/pallas_call | solution.py:120
  2.3 4.3 %all-to-all-start = ((f32[4,165,1,128]{3,2,1,0:T(1,128)}), f32[4,165,1,128]{3,2,1,0:T(1,128)S(1)}, u32[]{:S(2)}, u32[]{:S(2)}) async-start(f32[4,165,1,128]{3,2,1,0:T(1,128)} %part_copies.1), calls=%async_computation | async-start | bytes 675840 | tf_op jit(solution)/shard_map/all_to_all | solution.py:531
  6.6 2.5 %shard_map.122 = (bf16[8,165,165]{2,1,0:T(8,128)(2,1)S(1)}, bf16[8,165,165]{2,1,0:T(8,128)(2,1)S(1)}, s32[3,47]{1,0:T(4,128)S(1)}, s32[47,128]{1,0:T(8,128)S(1)}, s32[16,47]{1,0:T(8,128)S(1)}) custom-call(f32[165,8,165]{2,1,0:T(8,128)} %bitcast.11, s32[1]{0:T(128)} %bitcast.refs_0_.place, s32[2,47]{1,0:T(2,128)} %bitcast.15, s32[47,48]{1,0:T(8,128)} %refs_2_.1, ...), custom_call_target="tpu_custom_call" | custom-call | tf_op jit(solution)/shard_map/pallas_call | solution.py:97
  9.1 5.0 %all-to-all-done.parts = f32[4,165,1,128]{3,2,1,0:T(1,128)S(1)} async-done(((f32[4,165,1,128]{3,2,1,0:T(1,128)}), f32[4,165,1,128]{3,2,1,0:T(1,128)S(1)}, u32[]{:S(2)}, u32[]{:S(2)}) %all-to-all-start) | async-done | bytes 337952 | tf_op jit(solution)/shard_map/all_to_all | solution.py:531
  14.1 1.8 %own_moments.1 = (f32[200,128]{1,0:T(8,128)S(1)}, f32[24,1,384]{2,1,0:T(1,128)S(1)}) custom-call(f32[4,165,1,128]{3,2,1,0:T(1,128)S(1)} %all-to-all-done.parts, bf16[8,165,165]{2,1,0:T(8,128)(2,1)S(1)} %get-tuple-element.18.uph, bf16[8,165,165]{2,1,0:T(8,128)(2,1)S(1)} %get-tuple-element.19.upl), custom_call_target="tpu_custom_call" | custom-call | tf_op jit(solution)/shard_map/own_moments/pallas_call | solution.py:159
  15.9 23.3 %all_to_all.20.line = f32[24,1,384]{2,1,0:T(1,128)S(1)} all-to-all(f32[24,1,384]{2,1,0:T(1,128)S(1)} %get-tuple-element.20), channel_id=1, replica_groups={{92,88,84,80,76,72,68,64,60,56,52,48,44,40,36,32,28,24,20,16,12,8,4,0},..., dimensions={0} | all-to-all | bytes 73728 | tf_op jit(solution)/shard_map/all_to_all | solution.py:531
  39.2 0.8 line_copies.1
  40.0 7.5 %all-to-all-start.2 = ((f32[8,64,128]{2,1,0:T(8,128)}), f32[8,64,128]{2,1,0:T(8,128)S(1)}, u32[]{:S(2)}, u32[]{:S(2)}) async-start(f32[8,64,128]{2,1,0:T(8,128)} %line_copies.1), calls=%async_computation.2 | async-start | bytes 524288 | tf_op jit(solution)/shard_map/all_to_all | solution.py:531
  47.6 3.1 %collective-permute-start = (f32[200,128]{1,0:T(8,128)S(1)}, f32[200,128]{1,0:T(8,128)S(1)}, u32[]{:S(2)}, u32[]{:S(2)}) collective-permute-start(f32[200,128]{1,0:T(8,128)S(1)} %get-tuple-element.21.own), channel_id=1, source_target_pairs={{4,8},{8,4},{12,16},{16,12},{20,24},{24,20},{28,32},{32,28},{36,40... | collective-permute-start | bytes 307208 | tf_op jit(solution)/shard_map/ppermute | solution.py:555
  50.7 1.9 %collective-permute-start.1 = (f32[200,128]{1,0:T(8,128)S(1)}, f32[200,128]{1,0:T(8,128)S(1)}, u32[]{:S(2)}, u32[]{:S(2)}) collective-permute-start(f32[200,128]{1,0:T(8,128)S(1)} %get-tuple-element.21.own), channel_id=1, source_target_pairs={{0,4},{4,0},{8,12},{12,8},{16,20},{20,16},{24,28},{28,24},{32,36},... | collective-permute-start | bytes 307208 | tf_op jit(solution)/shard_map/ppermute | solution.py:556
  52.6 2.8 %shard_map.123 = (bf16[8,165,165]{2,1,0:T(8,128)(2,1)}, bf16[8,165,165]{2,1,0:T(8,128)(2,1)}) custom-call(f32[165,8,165]{2,1,0:T(8,128)} %bitcast.12), custom_call_target="tpu_custom_call" | custom-call | tf_op jit(solution)/shard_map/pallas_call | solution.py:97
  55.4 0.2 collective-permute-done.outer
  55.6 0.0 collective-permute-done.1.partner
  55.6 6.4 %near_terms.1 = (f32[165,128]{1,0:T(8,128)S(1)}, f32[165,128]{1,0:T(8,128)S(1)}) custom-call(s32[1]{0:T(128)} %bitcast.refs_0_.place, f32[200,128]{1,0:T(8,128)S(1)} %collective-permute-done.outer, f32[200,128]{1,0:T(8,128)S(1)} %get-tuple-element.21.own, f32[200,128]{1,0:T(8,128)S(1)} %collective-permute-done.1.partner, ...), custom_call_target="tpu_custom_call" | custom-call | tf_op jit(solution)/shard_map/near_terms/pallas_call | solution.py:295
  62.1 0.0 all-to-all-done.2
  62.1 0.0 copy-start.2
  62.1 0.0 copy-start.3
  62.1 0.0 copy-start.4
  62.1 7.8 %far_terms.1 = f32[4,165,128]{2,1,0:T(8,128)} custom-call(s32[1]{0:T(128)} %bitcast.refs_0_.place, s32[3,47]{1,0:T(4,128)S(1)} %get-tuple-element.17.listed_ref, f32[512,128]{1,0:T(8,128)S(1)} %bitcast.9, bf16[8,165,165]{2,1,0:T(8,128)(2,1)S(1)} %get-tuple-element.18.uph, bf16[8,165,165]{2,1,0:T(8,128)(2,1)S(1)} %get-tuple-element.19.upl, ...), custom_call_target="tpu_custom_call" | custom-call | tf_op jit(solution)/shard_map/far_terms/pallas_call | solution.py:434
  69.9 3.5 %all-to-all-start.3 = ((f32[4,165,128]{2,1,0:T(8,128)}), f32[4,165,128]{2,1,0:T(8,128)S(1)}, u32[]{:S(2)}, u32[]{:S(2)}) async-start(f32[4,165,128]{2,1,0:T(8,128)} %far_terms.1), calls=%async_computation.3 | async-start | bytes 688128 | tf_op jit(solution)/shard_map/all_to_all | solution.py:531
  73.4 0.0 copy-done.2
  73.4 0.0 copy-done.3
  73.4 2.8 %monomials.1 = (bf16[165,2048]{1,0:T(8,128)(2,1)}, bf16[165,2048]{1,0:T(8,128)(2,1)}) custom-call(s32[165,3]{1,0:T(8,128)S(1)} %copy-done.2, f32[3,2048]{1,0:T(4,128)S(1)} %copy-done.3), custom_call_target="tpu_custom_call" | custom-call | tf_op jit(solution)/shard_map/monomials/pallas_call | solution.py:487
  76.2 5.4 %all-to-all-done.3.parts = f32[4,165,128]{2,1,0:T(8,128)S(1)} async-done(((f32[4,165,128]{2,1,0:T(8,128)}), f32[4,165,128]{2,1,0:T(8,128)S(1)}, u32[]{:S(2)}, u32[]{:S(2)}) %all-to-all-start.3) | async-done | bytes 337952 | tf_op jit(solution)/shard_map/all_to_all | solution.py:531
  81.7 0.0 copy-done.4
  81.7 0.0 copy-start
  81.7 1.1 %copy-done = bf16[165,2048]{1,0:T(8,128)(2,1)S(1)} copy-done((bf16[165,2048]{1,0:T(8,128)(2,1)S(1)}, bf16[165,2048]{1,0:T(8,128)(2,1)}, u32[]{:S(2)}) %copy-start) | copy-done | bytes 675864
  82.8 0.0 copy-start.1
  82.8 1.1 %copy-done.1 = bf16[165,2048]{1,0:T(8,128)(2,1)S(1)} copy-done((bf16[165,2048]{1,0:T(8,128)(2,1)S(1)}, bf16[165,2048]{1,0:T(8,128)(2,1)}, u32[]{:S(2)}) %copy-start.1) | copy-done | bytes 675864
  83.9 1.2 %potentials.1 = (f32[165,128]{1,0:T(8,128)}, f32[1,2048]{1,0:T(1,128)}) custom-call(s32[1]{0:T(128)} %bitcast.refs_0_.place, f32[4,165,128]{2,1,0:T(8,128)S(1)} %all-to-all-done.3.parts, s32[1,2048]{1,0:T(1,128)S(1)} %bitcast.10, bf16[165,2048]{1,0:T(8,128)(2,1)S(1)} %copy-done, bf16[165,2048]{1,0:T(8,128)(2,1)S(1)} %copy-done.1), custom_call_target="tpu_custom_call" | custom-call | tf_op jit(solution)/shard_map/potentials/pallas_call | solution.py:515
Async XLA Ops:
  2.3 11.8 %all-to-all-start = ((f32[4,165,1,128]{3,2,1,0:T(1,128)}), f32[4,165,1,128]{3,2,1,0:T(1,128)S(1)}, u32[]{:S(2)}, u32[]{:S(2)}) async-start(f32[4,165,1,128]{3,2,1,0:T(1,128)} %part_copies.1), calls=%async_computation | async-start | bytes 675840 | tf_op jit(solution)/shard_map/all_to_all | solution.py:531
  40.0 22.1 %all-to-all-start.2 = ((f32[8,64,128]{2,1,0:T(8,128)}), f32[8,64,128]{2,1,0:T(8,128)S(1)}, u32[]{:S(2)}, u32[]{:S(2)}) async-start(f32[8,64,128]{2,1,0:T(8,128)} %line_copies.1), calls=%async_computation.2 | async-start | bytes 524288 | tf_op jit(solution)/shard_map/all_to_all | solution.py:531
  47.6 8.1 %collective-permute-start = (f32[200,128]{1,0:T(8,128)S(1)}, f32[200,128]{1,0:T(8,128)S(1)}, u32[]{:S(2)}, u32[]{:S(2)}) collective-permute-start(f32[200,128]{1,0:T(8,128)S(1)} %get-tuple-element.21.own), channel_id=1, source_target_pairs={{4,8},{8,4},{12,16},{16,12},{20,24},{24,20},{28,32},{32,28},{36,40... | collective-permute-start | bytes 307208 | tf_op jit(solution)/shard_map/ppermute | solution.py:555
  50.7 5.0 %collective-permute-start.1 = (f32[200,128]{1,0:T(8,128)S(1)}, f32[200,128]{1,0:T(8,128)S(1)}, u32[]{:S(2)}, u32[]{:S(2)}) collective-permute-start(f32[200,128]{1,0:T(8,128)S(1)} %get-tuple-element.21.own), channel_id=1, source_target_pairs={{0,4},{4,0},{8,12},{12,8},{16,20},{20,16},{24,28},{28,24},{32,36},... | collective-permute-start | bytes 307208 | tf_op jit(solution)/shard_map/ppermute | solution.py:556
  62.1 11.3 %copy-start.2 = (s32[165,3]{1,0:T(8,128)S(1)}, s32[165,3]{1,0:T(8,128)}, u32[]{:S(2)}) copy-start(s32[165,3]{1,0:T(8,128)} %constant.14.clone.powers) | copy-start | bytes 5944
  62.1 11.3 %copy-start.3 = (f32[3,2048]{1,0:T(4,128)S(1)}, f32[3,2048]{1,0:T(4,128)}, u32[]{:S(2)}) copy-start(f32[3,2048]{1,0:T(4,128)} %coords.1) | copy-start | bytes 73732
  62.1 19.6 %copy-start.4 = (s32[2048]{0:T(1024)S(1)}, s32[2048]{0:T(1024)}, u32[]{:S(2)}) copy-start(s32[2048]{0:T(1024)} %param.20) | copy-start | bytes 24580
  69.9 11.7 %all-to-all-start.3 = ((f32[4,165,128]{2,1,0:T(8,128)}), f32[4,165,128]{2,1,0:T(8,128)S(1)}, u32[]{:S(2)}, u32[]{:S(2)}) async-start(f32[4,165,128]{2,1,0:T(8,128)} %far_terms.1), calls=%async_computation.3 | async-start | bytes 688128 | tf_op jit(solution)/shard_map/all_to_all | solution.py:531
  81.7 1.1 %copy-start = (bf16[165,2048]{1,0:T(8,128)(2,1)S(1)}, bf16[165,2048]{1,0:T(8,128)(2,1)}, u32[]{:S(2)}) copy-start(bf16[165,2048]{1,0:T(8,128)(2,1)} %get-tuple-element.28.high_ref) | copy-start | bytes 2027524
  82.8 1.1 %copy-start.1 = (bf16[165,2048]{1,0:T(8,128)(2,1)S(1)}, bf16[165,2048]{1,0:T(8,128)(2,1)}, u32[]{:S(2)}) copy-start(bf16[165,2048]{1,0:T(8,128)(2,1)} %get-tuple-element.29.low_ref) | copy-start | bytes 2027524

commit v6 on v5

--- a/solution.py
+++ b/solution.py
@@ -69,63 +69,84 @@
 PITCH = 56
 
 
-def split_kernel(ops_hbm, *refs):
-    count = (len(refs) - 2) // 2 if len(refs) > 4 else 0
-    small, (high, low), kept, (parts, sems) = refs[:count], refs[count : count + 2], refs[count + 2 : -2], refs[-2:]
+def prepare_kernel(
+    place, part_hbm, up_hbm, top_hbm, upper_hbm, fine_hbm, mid_hbm, copies, high, low, listed, fine_out, mid_out,
+    part, ups, top, upper, sems, store_sems, up_sems,
+):
+    pairs = [(part_hbm, part), (top_hbm, top), (upper_hbm, upper), (fine_hbm, fine_out), (mid_hbm, mid_out)]
+    loads = [pltpu.make_async_copy(source, target, sems.at[k]) for k, (source, target) in enumerate(pairs)]
+    up_loads = [pltpu.make_async_copy(up_hbm.at[:, o, :], ups.at[o], up_sems.at[o]) for o in range(8)]
+    for load in loads + up_loads:
+        load.start()
+    loads[0].wait()
+    stores = [pltpu.make_async_copy(part, copies.at[i], store_sems.at[i]) for i in range(copies.shape[0])]
+    for store in stores:
+        store.start()
+    for load in loads[1:]:
+        load.wait()
+    cells = top[...]
+    listed[pl.ds(0, 2), :] = jnp.where(cells >= 0, (cells & 7) * PITCH + (cells >> 3), PITCH - 8)
+    cells = upper[...]
+    cells = jnp.where(cells >= 0, cells, PITCH - 8).astype(F32).astype(BF16)
+    here = ones_where((8, cells.shape[1]), lambda r, c: c == place[0] // 4)
+    listed[pl.ds(2, 1), :] = mm_nt(here, cells)[:1].astype(I32)
+    for o in range(8):
+        up_loads[o].wait()
+        high[o], low[o] = split(ups[o])
+    for store in stores:
+        store.wait()
+
+
+def prepare(place, part, up, top_list, upper_list, fine_list, mid_list, copies):
+    n = part.shape[0]
+    vm, hbm = pl.BlockSpec(memory_space=VMEM), pl.BlockSpec(memory_space=pltpu.HBM)
+    given = (part, jnp.transpose(up, (1, 0, 2)), top_list, upper_list, fine_list, mid_list)
+    return pl.pallas_call(
+        prepare_kernel,
+        out_shape=(
+            pltpu.HBM((copies, *part.shape), F32),
+            VMEM((8, n, n), BF16),
+            VMEM((8, n, n), BF16),
+            VMEM((3, top_list.shape[1]), I32),
+            VMEM(fine_list.shape, I32),
+            VMEM(mid_list.shape, I32),
+        ),
+        in_specs=[pl.BlockSpec(memory_space=pltpu.SMEM)] + [hbm] * 6,
+        out_specs=(hbm,) + (vm,) * 5,
+        scratch_shapes=[
+            pltpu.VMEM(part.shape, F32),
+            pltpu.VMEM((8, n, n), F32),
+            pltpu.VMEM(top_list.shape, I32),
+            pltpu.VMEM(upper_list.shape, I32),
+            pltpu.SemaphoreType.DMA((5,)),
+            pltpu.SemaphoreType.DMA((copies,)),
+            pltpu.SemaphoreType.DMA((8,)),
+        ],
+        compiler_params=pltpu.CompilerParams(vmem_limit_bytes=8 << 20),
+        name="prepare",
+    )(place, *(in_hbm(x) for x in given))
+
+
+def split_kernel(ops_hbm, high, low, parts, sems):
     copies = [pltpu.make_async_copy(ops_hbm.at[:, o, :], parts.at[o], sems.at[o]) for o in range(8)]
     for copy in copies:
         copy.start()
-    if small:
-        place, top_ref, upper_ref, *others = small
-        top = top_ref[...]
-        kept[0][pl.ds(0, 2), :] = jnp.where(top >= 0, (top & 7) * PITCH + (top >> 3), PITCH - 8)
-        upper = upper_ref[...]
-        upper = jnp.where(upper >= 0, upper, PITCH - 8).astype(F32).astype(BF16)
-        here = ones_where((8, upper.shape[1]), lambda r, c: c == place[0] // 4)
-        kept[0][pl.ds(2, 1), :] = mm_nt(here, upper)[:1].astype(I32)
-        for source, target in zip(others, kept[1:], strict=True):
-            target[...] = source[...]
     for o in range(8):
         copies[o].wait()
         high[o], low[o] = split(parts[o])
 
 
-def split_ops(ops, kept=VMEM, lists=()):
+def split_down(ops):
     n = ops.shape[1]
-    vm, sm = pl.BlockSpec(memory_space=VMEM), pl.BlockSpec(memory_space=pltpu.SMEM)
-    more = (VMEM((3, lists[1].shape[1]), I32), *(VMEM(x.shape, I32) for x in lists[3:])) if lists else ()
     return pl.pallas_call(
         split_kernel,
-        out_shape=(kept((8, n, n), BF16),) * 2 + more,
-        in_specs=[pl.BlockSpec(memory_space=pltpu.HBM)] + [sm] * bool(lists) + [vm] * (len(lists) - 1),
-        out_specs=(vm,) * (2 + len(more)),
+        out_shape=(pltpu.HBM((8, n, n), BF16),) * 2,
+        in_specs=[pl.BlockSpec(memory_space=pltpu.HBM)],
+        out_specs=(pl.BlockSpec(memory_space=VMEM),) * 2,
         scratch_shapes=[pltpu.VMEM((8, n, n), F32), pltpu.SemaphoreType.DMA((8,))],
         compiler_params=pltpu.CompilerParams(vmem_limit_bytes=8 << 20),
-    )(in_hbm(jnp.transpose(ops, (1, 0, 2))), *lists[:1], *(in_hbm(x) for x in lists[1:]))
-
-
-def copies_kernel(part_hbm, out_hbm, buffer, sems):
-    load = pltpu.make_async_copy(part_hbm, buffer, sems.at[0])
-    load.start()
-    load.wait()
-    stores = [pltpu.make_async_copy(buffer, out_hbm.at[i], sems.at[i + 1]) for i in range(out_hbm.shape[0])]
-    for store in stores:
-        store.start()
-    for store in stores:
-        store.wait()
-
-
-def part_copies(part, copies):
-    hbm = pl.BlockSpec(memory_space=pltpu.HBM)
-    return pl.pallas_call(
-        copies_kernel,
-        out_shape=pltpu.HBM((copies, *part.shape), F32),
-        in_specs=[hbm],
-        out_specs=hbm,
-        scratch_shapes=[pltpu.VMEM(part.shape, F32), pltpu.SemaphoreType.DMA((copies + 1,))],
-        compiler_params=pltpu.CompilerParams(vmem_limit_bytes=2 << 20),
-        name="part_copies",
-    )(in_hbm(part))
+        name="split_down",
+    )(in_hbm(jnp.transpose(ops, (1, 0, 2))))
 
 
 MID_AT = 168
@@ -195,9 +216,10 @@
 
 
 GROUP = 4
-
-
-def near_kernel(place, outer, own, partner, fl, ml, ops_hbm, fine_out, mid_out, ops, full, rows, mids, mid_rows, xa, xb, acc_a, acc_b, sems):
+TALL = 24
+
+
+def near_kernel(place, outer, own, partner, fl, ml, ops_hbm, fine_out, mid_out, head, ops, full, rows, mids, mid_rows, xa, xb, acc_a, acc_b, sems):
     slots, n = ops.shape[0], ops.shape[1]
     groups = -(-slots // GROUP)
     size = [min(GROUP, slots - k * GROUP) for k in range(groups)]
@@ -282,6 +304,7 @@
         if k + 1 < groups:
             load(k + 1, size[k + 1], bufs[(k + 1) % 2])
         use(k, size[k], bufs[k % 2])
+    head[...] = ops[:, pl.ds(0, TALL), :]
     fine_out[...] = acc_a[:, pl.ds(0, 128)] + acc_b[...]
     folded = acc_a[:, pl.ds(128, 128)]
     for shift in (64, 32, 16):
@@ -294,9 +317,9 @@
     vm = pl.BlockSpec(memory_space=VMEM)
     return pl.pallas_call(
         near_kernel,
-        out_shape=(VMEM((n, 128), F32),) * 2,
+        out_shape=(VMEM((n, 128), F32),) * 2 + (VMEM((slots, TALL, n), F32),),
         in_specs=[pl.BlockSpec(memory_space=pltpu.SMEM)] + [vm] * 5 + [pl.BlockSpec(memory_space=pltpu.HBM)],
-        out_specs=(vm,) * 2,
+        out_specs=(vm,) * 3,
         scratch_shapes=[
             pltpu.VMEM((slots, n, n), F32),
             pltpu.VMEM((3, n, 128), F32),
@@ -314,20 +337,19 @@
     )(place, outer, own, partner, fine_list, mid_list, in_hbm(ops))
 
 
-TALL = 24
 UNROLL = 8
 FIRST = (3, 2, 2)
 
 
 def far_kernel(
-    place, listed_ref, table, uph, upl, fine_term, mid_term, dnh_hbm, dnl_hbm, ops_hbm, out,
+    place, listed_ref, table, uph, upl, fine_term, mid_term, head, dnh_hbm, dnl_hbm, ops_hbm, out,
     ops, dnh, dnl, tiles, rows, upper, chosen, top_col, upper_col, listed, sems, down_sems, list_sem,
 ):
     slots, n = ops.shape[0], ops.shape[1]
     list_load = pltpu.make_async_copy(listed_ref, listed, list_sem)
     list_load.start()
     loads = []
-    for k, at in enumerate(range(0, n, TALL)):
+    for k, at in enumerate(range(TALL, n, TALL)):
         where = (slice(None), pl.ds(at, min(TALL, n - at)))
         loads.append(pltpu.make_async_copy(ops_hbm.at[where], ops.at[where], sems.at[k]))
     down_loads = [
@@ -386,13 +408,13 @@
         choose(j)
     begin(len(queue))
 
-    def block(start, size):
+    def block(start, size, source=ops):
         edges = [(at, min(8, size - at)) for at in range(0, size, 8)]
         sums = [[jnp.zeros((height, n), F32)] * 3 for _, height in edges]
         for j in range(slots):
             factors = [chosen[3 * j + t] for t in range(3)]
             for part, (at, height) in zip(sums, edges, strict=True):
-                piece = ops[j, pl.ds(start + at, height), :]
+                piece = source[j, pl.ds(start + at, height), :]
                 for t in range(3):
                     part[t] = part[t] + piece * factors[t][:height]
         for part, (at, height) in zip(sums, edges, strict=True):
@@ -405,11 +427,12 @@
     def step(i, carry):
         at = pl.multiple_of(i * TALL, TALL)
         where = (slice(None), pl.ds(at, TALL))
-        pltpu.make_async_copy(ops_hbm.at[where], ops.at[where], sems.at[i]).wait()
+        pltpu.make_async_copy(ops_hbm.at[where], ops.at[where], sems.at[i - 1]).wait()
         block(at, TALL)
         return carry
 
-    lax.fori_loop(0, n // TALL, step, 0)
+    block(0, TALL, head)
+    lax.fori_loop(1, n // TALL, step, 0)
     if n % TALL:
         loads[-1].wait()
         block(n // TALL * TALL, n % TALL)
@@ -427,14 +450,14 @@
         out[i] = local_fine
 
 
-def far_terms(place, listed, table, uph, upl, dnh, dnl, fine_term, mid_term, ops, copies):
+def far_terms(place, listed, table, uph, upl, dnh, dnl, fine_term, mid_term, head, ops, copies):
     slots, n = ops.shape[0], ops.shape[1]
     parents = table.shape[0] // LINE_ROWS * 6
     vm, sm = pl.BlockSpec(memory_space=VMEM), pl.BlockSpec(memory_space=pltpu.SMEM)
     return pl.pallas_call(
         far_kernel,
         out_shape=VMEM((copies, n, 128), F32),
-        in_specs=[sm] + [vm] * 6 + [pl.BlockSpec(memory_space=pltpu.HBM)] * 3,
+        in_specs=[sm] + [vm] * 7 + [pl.BlockSpec(memory_space=pltpu.HBM)] * 3,
         out_specs=vm,
         scratch_shapes=[
             pltpu.VMEM((slots, n, n), F32),
@@ -454,7 +477,7 @@
         compiler_params=pltpu.CompilerParams(vmem_limit_bytes=20 << 20),
         name="far_terms",
     )(
-        place, listed, table, uph, upl, fine_term, mid_term,
+        place, listed, table, uph, upl, fine_term, mid_term, head,
         in_hbm(dnh), in_hbm(dnl), in_hbm(ops),
     )
 
@@ -483,14 +506,14 @@
 def monomials(coords):
     table = jnp.asarray(exponents(), I32)
     n, particles = table.shape[0], coords.shape[1]
-    width = 512
+    width = 1024
     return pl.pallas_call(
         monomial_kernel,
         grid=(particles // width,),
         out_shape=(pltpu.HBM((n, particles), BF16),) * 2,
         in_specs=[pl.BlockSpec((n, 3), lambda i: (0, 0)), pl.BlockSpec((3, width), lambda i: (0, i))],
         out_specs=(pl.BlockSpec((n, width), lambda i: (0, i)),) * 2,
-        compiler_params=pltpu.CompilerParams(vmem_limit_bytes=4 << 20),
+        compiler_params=pltpu.CompilerParams(vmem_limit_bytes=8 << 20),
         name="monomials",
     )(table, coords)
 
@@ -546,19 +569,27 @@
     subs, slabs = lax.axis_size("sub"), lax.axis_size(DOM)
     domain = lax.axis_index(DOM).astype(I32)
     place = domain.reshape(1)
-    lists = (place, jnp.transpose(top_list), upper_list, fine_list, jnp.transpose(mid_list))
-    uph, upl, listed, fine_list, mid_list = split_ops(upward_ops, lists=lists)
-    dnh, dnl = split_ops(downward_ops, pltpu.HBM)
-    parts = exchanged(part_copies(jnp.transpose(fine_partial, (1, 0, 2)), subs), "sub")
+    copies, uph, upl, listed, fine_list, mid_list = prepare(
+        place,
+        jnp.transpose(fine_partial, (1, 0, 2)),
+        upward_ops,
+        jnp.transpose(top_list),
+        upper_list,
+        fine_list,
+        jnp.transpose(mid_list),
+        subs,
+    )
+    parts = exchanged(copies, "sub")
     own, tops = own_moments(parts, uph, upl, lax.axis_size(DOM[1]))
     line = exchanged(tops, DOM[1], ORDER_1)
     outer = lax.ppermute(own, DOM, [(i, i + 2 * (i % 2) - 1) for i in range(1, slabs - 1)])
     partner = lax.ppermute(own, DOM, [(i, i ^ 1) for i in range(slabs)])
     table = exchanged(line_copies(line, lax.axis_size(DOM[0])), DOM[0], ORDER_0)
     table = table.reshape(-1, table.shape[2])
-    fine_term, mid_term = near_terms(place, outer, own, partner, fine_list, mid_list, interaction_ops)
+    dnh, dnl = split_down(downward_ops)
+    fine_term, mid_term, head = near_terms(place, outer, own, partner, fine_list, mid_list, interaction_ops)
     partial = far_terms(
-        place, listed, table, uph, upl, dnh, dnl, fine_term, mid_term, interaction_ops, subs
+        place, listed, table, uph, upl, dnh, dnl, fine_term, mid_term, head, interaction_ops, subs
     )
     high, low = monomials(positions)
     parts = exchanged(partial, "sub")

time: 85.8 us -> 85.5 us (level)
  blocking collectives: 23.3 us -> 35.1 us
  waiting for transfers between devices: 10.7 us -> 6.05 us
  starting transfers between devices: 20.3 us -> 16 us
  Pallas kernels: 27.8 us -> 24.7 us
    all_to_all x1 -> x2, blocking collectives: 23.3 us -> 35.1 us  [exchanged(): lax.all_to_all(copies, axis, split_axis=0, concat_axis=0, tiled=True, axi...]
    all_to_all x3 -> x2, waiting for transfers between devices: 10.4 us -> 5.85 us  [exchanged(): lax.all_to_all(copies, axis, split_axis=0, concat_axis=0, tiled=True, axi...]
    all_to_all x3 -> x2, starting transfers between devices: 15.3 us -> 11 us  [exchanged(): lax.all_to_all(copies, axis, split_axis=0, concat_axis=0, tiled=True, axi...]
    pallas_call x4 -> x3, Pallas kernels: 13.4 us -> 11.2 us  [the longest x1 6.52 us: near_terms(): pl.pallas_call(near_kernel, out_shape=(VMEM((n, 128), F32),) * 2 + (VMEM(...]
  transfers between devices with their start and end apart: 5 -> 4, of which waited for: 3 -> 2; matrix products, arithmetic and copies ran while one was open for 0% -> 0% of each run, Pallas kernels for 17% -> 14%
where the time goes in v6:
time: 85.5 us; the launch traced here: 84.9 us
  blocking collectives  35.1 us (41%)
  Pallas kernels  24.7 us (29%)
  starting transfers between devices  16 us (19%)
  waiting for transfers between devices  6.05 us (7%)
  local copies, waits for them, and re-layouts  2.22 us (3%)
    all_to_all x2, blocking collectives, exchanged(): lax.all_to_all(copies, axis, split_axis=0, concat_axis=0, tiled=True, axi...  35.1 us
    all_to_all x2, starting transfers between devices, exchanged(): lax.all_to_all(copies, axis, split_axis=0, concat_axis=0, tiled=True, axi...  11 us
    pallas_call x1, Pallas kernels, far_terms(): pl.pallas_call(far_kernel, out_shape=VMEM((copies, n, 128), F32), in_spec...  7.33 us
    pallas_call x1, Pallas kernels, near_terms(): pl.pallas_call(near_kernel, out_shape=(VMEM((n, 128), F32),) * 2 + (VMEM(...  6.52 us
    all_to_all x2, waiting for transfers between devices, exchanged(): lax.all_to_all(copies, axis, split_axis=0, concat_axis=0, tiled=True, axi...  5.85 us
    ppermute x1, starting transfers between devices, shards(): lax.ppermute(own, DOM, [(i, i + 2 * (i % 2) - 1) for i in range(1, slabs...  3.12 us
    pallas_call x1, Pallas kernels, split_down(): pl.pallas_call(split_kernel, out_shape=(pltpu.HBM((8, n, n), BF16),) * 2,...  2.81 us
    pallas_call x1, Pallas kernels, monomials(): pl.pallas_call(monomial_kernel, grid=(particles // width,), out_shape=(pl...  2.41 us
  transfers between devices with their start and end apart: 4, of which 2 were waited for; matrix products, arithmetic and copies ran while one was open for 0% of the time, Pallas kernels for 14%

profile of v6, /device:TPU:8, one launch (start us, length us, event | category | flops | bytes accessed | tf_op | source)
XLA Modules:
  0.0 84.9 jit_solution(7250170809028828853)
XLA Ops:
  0.6 1.8 %prepare.1 = (f32[4,165,1,128]{3,2,1,0:T(1,128)}, bf16[8,165,165]{2,1,0:T(8,128)(2,1)S(1)}, bf16[8,165,165]{2,1,0:T(8,128)(2,1)S(1)}, s32[3,47]{1,0:T(4,128)S(1)...) custom-call(s32[1]{0:T(128)} %bitcast.place, f32[165,1,128]{2,1,0:T(1,128)} %bitcast.13, f32[165,8,165]{2,1,0:T(8,128)} %bitcast.11, ...), custom_call_target="tpu_custom_call" | custom-call | tf_op jit(solution)/shard_map/prepare/pallas_call | solution.py:104
  2.5 11.8 %all_to_all.20.parts = f32[4,165,1,128]{3,2,1,0:T(1,128)S(1)} all-to-all(f32[4,165,1,128]{3,2,1,0:T(1,128)} %get-tuple-element.20), channel_id=1, replica_groups=mesh['dom_0'=8,'dom_1'=24,'sub'=4] {'sub'}, dimensions={0} | all-to-all | bytes 675840 | tf_op jit(solution)/shard_map/all_to_all | solution.py:554
  14.3 1.8 %own_moments.1 = (f32[200,128]{1,0:T(8,128)S(1)}, f32[24,1,384]{2,1,0:T(1,128)S(1)}) custom-call(f32[4,165,1,128]{3,2,1,0:T(1,128)S(1)} %all_to_all.20.parts, bf16[8,165,165]{2,1,0:T(8,128)(2,1)S(1)} %get-tuple-element.21.uph, bf16[8,165,165]{2,1,0:T(8,128)(2,1)S(1)} %get-tuple-element.22.upl), custom_call_target="tpu_custom_call" | custom-call | tf_op jit(solution)/shard_map/own_moments/pallas_call | solution.py:180
  16.1 23.3 %all_to_all.21.line = f32[24,1,384]{2,1,0:T(1,128)S(1)} all-to-all(f32[24,1,384]{2,1,0:T(1,128)S(1)} %get-tuple-element.23), channel_id=1, replica_groups={{92,88,84,80,76,72,68,64,60,56,52,48,44,40,36,32,28,24,20,16,12,8,4,0},..., dimensions={0} | all-to-all | bytes 73728 | tf_op jit(solution)/shard_map/all_to_all | solution.py:554
  39.4 0.8 line_copies.1
  40.2 7.5 %all-to-all-start.2 = ((f32[8,64,128]{2,1,0:T(8,128)}), f32[8,64,128]{2,1,0:T(8,128)S(1)}, u32[]{:S(2)}, u32[]{:S(2)}) async-start(f32[8,64,128]{2,1,0:T(8,128)} %line_copies.1), calls=%async_computation.2 | async-start | bytes 524288 | tf_op jit(solution)/shard_map/all_to_all | solution.py:554
  47.7 3.1 %collective-permute-start = (f32[200,128]{1,0:T(8,128)S(1)}, f32[200,128]{1,0:T(8,128)S(1)}, u32[]{:S(2)}, u32[]{:S(2)}) collective-permute-start(f32[200,128]{1,0:T(8,128)S(1)} %get-tuple-element.24.own), channel_id=1, source_target_pairs={{4,8},{8,4},{12,16},{16,12},{20,24},{24,20},{28,32},{32,28},{36,40... | collective-permute-start | bytes 307208 | tf_op jit(solution)/shard_map/ppermute | solution.py:585
  50.9 1.9 %collective-permute-start.1 = (f32[200,128]{1,0:T(8,128)S(1)}, f32[200,128]{1,0:T(8,128)S(1)}, u32[]{:S(2)}, u32[]{:S(2)}) collective-permute-start(f32[200,128]{1,0:T(8,128)S(1)} %get-tuple-element.24.own), channel_id=1, source_target_pairs={{0,4},{4,0},{8,12},{12,8},{16,20},{20,16},{24,28},{28,24},{32,36},... | collective-permute-start | bytes 307208 | tf_op jit(solution)/shard_map/ppermute | solution.py:586
  52.8 2.8 %split_down.1 = (bf16[8,165,165]{2,1,0:T(8,128)(2,1)}, bf16[8,165,165]{2,1,0:T(8,128)(2,1)}) custom-call(f32[165,8,165]{2,1,0:T(8,128)} %bitcast.12), custom_call_target="tpu_custom_call" | custom-call | tf_op jit(solution)/shard_map/split_down/pallas_call | solution.py:141
  55.6 0.2 collective-permute-done.outer
  55.8 0.0 collective-permute-done.1.partner
  55.8 6.5 %near_terms.1 = (f32[165,128]{1,0:T(8,128)S(1)}, f32[165,128]{1,0:T(8,128)S(1)}, f32[47,24,165]{2,1,0:T(8,128)S(1)}) custom-call(s32[1]{0:T(128)} %bitcast.place, f32[200,128]{1,0:T(8,128)S(1)} %collective-permute-done.outer, f32[200,128]{1,0:T(8,128)S(1)} %get-tuple-element.24.own, f32[200,128]{1,0:T(8,128)S(1)} %collective-permute-done.1.partner, ...), custom_call_target="tpu_custom_call" | custom-call | tf_op jit(solution)/shard_map/near_terms/pallas_call | solution.py:318
  62.4 0.0 all-to-all-done.2
  62.4 0.0 copy-start.2
  62.4 0.0 copy-start.3
  62.4 0.0 copy-start.4
  62.4 7.3 %far_terms.1 = f32[4,165,128]{2,1,0:T(8,128)} custom-call(s32[1]{0:T(128)} %bitcast.place, s32[3,47]{1,0:T(4,128)S(1)} %get-tuple-element.19.listed_ref, f32[512,128]{1,0:T(8,128)S(1)} %bitcast.9, bf16[8,165,165]{2,1,0:T(8,128)(2,1)S(1)} %get-tuple-element.21.uph, bf16[8,165,165]{2,1,0:T(8,128)(2,1)S(1)} %get-tuple-element.22.upl, ...), custom_call_target="tpu_custom_call" | custom-call | tf_op jit(solution)/shard_map/far_terms/pallas_call | solution.py:457
  69.7 3.5 %all-to-all-start.3 = ((f32[4,165,128]{2,1,0:T(8,128)}), f32[4,165,128]{2,1,0:T(8,128)S(1)}, u32[]{:S(2)}, u32[]{:S(2)}) async-start(f32[4,165,128]{2,1,0:T(8,128)} %far_terms.1), calls=%async_computation.3 | async-start | bytes 688128 | tf_op jit(solution)/shard_map/all_to_all | solution.py:554
  73.2 0.0 copy-done.2
  73.2 0.0 copy-done.3
  73.2 2.4 %monomials.1 = (bf16[165,2048]{1,0:T(8,128)(2,1)}, bf16[165,2048]{1,0:T(8,128)(2,1)}) custom-call(s32[165,3]{1,0:T(8,128)S(1)} %copy-done.2, f32[3,2048]{1,0:T(4,128)S(1)} %copy-done.3), custom_call_target="tpu_custom_call" | custom-call | tf_op jit(solution)/shard_map/monomials/pallas_call | solution.py:510
  75.6 5.8 %all-to-all-done.3.parts = f32[4,165,128]{2,1,0:T(8,128)S(1)} async-done(((f32[4,165,128]{2,1,0:T(8,128)}), f32[4,165,128]{2,1,0:T(8,128)S(1)}, u32[]{:S(2)}, u32[]{:S(2)}) %all-to-all-start.3) | async-done | bytes 337952 | tf_op jit(solution)/shard_map/all_to_all | solution.py:554
  81.5 0.0 copy-done.4
  81.5 0.0 copy-start
  81.5 1.1 %copy-done = bf16[165,2048]{1,0:T(8,128)(2,1)S(1)} copy-done((bf16[165,2048]{1,0:T(8,128)(2,1)S(1)}, bf16[165,2048]{1,0:T(8,128)(2,1)}, u32[]{:S(2)}) %copy-start) | copy-done | bytes 675864
  82.6 0.0 copy-start.1
  82.6 1.1 %copy-done.1 = bf16[165,2048]{1,0:T(8,128)(2,1)S(1)} copy-done((bf16[165,2048]{1,0:T(8,128)(2,1)S(1)}, bf16[165,2048]{1,0:T(8,128)(2,1)}, u32[]{:S(2)}) %copy-start.1) | copy-done | bytes 675864
  83.7 1.2 %potentials.1 = (f32[165,128]{1,0:T(8,128)}, f32[1,2048]{1,0:T(1,128)}) custom-call(s32[1]{0:T(128)} %bitcast.place, f32[4,165,128]{2,1,0:T(8,128)S(1)} %all-to-all-done.3.parts, s32[1,2048]{1,0:T(1,128)S(1)} %bitcast.10, bf16[165,2048]{1,0:T(8,128)(2,1)S(1)} %copy-done, bf16[165,2048]{1,0:T(8,128)(2,1)S(1)} %copy-done.1), custom_call_target="tpu_custom_call" | custom-call | tf_op jit(solution)/shard_map/potentials/pallas_call | solution.py:538
Async XLA Ops:
  40.2 22.1 %all-to-all-start.2 = ((f32[8,64,128]{2,1,0:T(8,128)}), f32[8,64,128]{2,1,0:T(8,128)S(1)}, u32[]{:S(2)}, u32[]{:S(2)}) async-start(f32[8,64,128]{2,1,0:T(8,128)} %line_copies.1), calls=%async_computation.2 | async-start | bytes 524288 | tf_op jit(solution)/shard_map/all_to_all | solution.py:554
  47.7 8.1 %collective-permute-start = (f32[200,128]{1,0:T(8,128)S(1)}, f32[200,128]{1,0:T(8,128)S(1)}, u32[]{:S(2)}, u32[]{:S(2)}) collective-permute-start(f32[200,128]{1,0:T(8,128)S(1)} %get-tuple-element.24.own), channel_id=1, source_target_pairs={{4,8},{8,4},{12,16},{16,12},{20,24},{24,20},{28,32},{32,28},{36,40... | collective-permute-start | bytes 307208 | tf_op jit(solution)/shard_map/ppermute | solution.py:585
  50.9 5.0 %collective-permute-start.1 = (f32[200,128]{1,0:T(8,128)S(1)}, f32[200,128]{1,0:T(8,128)S(1)}, u32[]{:S(2)}, u32[]{:S(2)}) collective-permute-start(f32[200,128]{1,0:T(8,128)S(1)} %get-tuple-element.24.own), channel_id=1, source_target_pairs={{0,4},{4,0},{8,12},{12,8},{16,20},{20,16},{24,28},{28,24},{32,36},... | collective-permute-start | bytes 307208 | tf_op jit(solution)/shard_map/ppermute | solution.py:586
  62.4 10.9 %copy-start.2 = (s32[165,3]{1,0:T(8,128)S(1)}, s32[165,3]{1,0:T(8,128)}, u32[]{:S(2)}) copy-start(s32[165,3]{1,0:T(8,128)} %constant.14.clone.powers) | copy-start | bytes 5944
  62.4 10.9 %copy-start.3 = (f32[3,2048]{1,0:T(4,128)S(1)}, f32[3,2048]{1,0:T(4,128)}, u32[]{:S(2)}) copy-start(f32[3,2048]{1,0:T(4,128)} %coords.1) | copy-start | bytes 73732
  62.4 19.1 %copy-start.4 = (s32[2048]{0:T(1024)S(1)}, s32[2048]{0:T(1024)}, u32[]{:S(2)}) copy-start(s32[2048]{0:T(1024)} %param.20) | copy-start | bytes 24580
  69.7 11.7 %all-to-all-start.3 = ((f32[4,165,128]{2,1,0:T(8,128)}), f32[4,165,128]{2,1,0:T(8,128)S(1)}, u32[]{:S(2)}, u32[]{:S(2)}) async-start(f32[4,165,128]{2,1,0:T(8,128)} %far_terms.1), calls=%async_computation.3 | async-start | bytes 688128 | tf_op jit(solution)/shard_map/all_to_all | solution.py:554
  81.5 1.1 %copy-start = (bf16[165,2048]{1,0:T(8,128)(2,1)S(1)}, bf16[165,2048]{1,0:T(8,128)(2,1)}, u32[]{:S(2)}) copy-start(bf16[165,2048]{1,0:T(8,128)(2,1)} %get-tuple-element.32.high_ref) | copy-start | bytes 2027524
  82.6 1.1 %copy-start.1 = (bf16[165,2048]{1,0:T(8,128)(2,1)S(1)}, bf16[165,2048]{1,0:T(8,128)(2,1)}, u32[]{:S(2)}) copy-start(bf16[165,2048]{1,0:T(8,128)(2,1)} %get-tuple-element.33.low_ref) | copy-start | bytes 2027524

commit v7 on v6

--- a/solution.py
+++ b/solution.py
@@ -10,7 +10,7 @@
 ORDER = 8
 F32, BF16, I32 = jnp.float32, jnp.bfloat16, jnp.int32
 VMEM = pltpu.VMEM
-ORDER_0 = [6, 7, 5, 4, 3, 2, 1, 0]
+ORDER_0 = [6, 0, 1, 2, 3, 4, 5, 7]
 ORDER_1 = list(range(23, -1, -1))
 
 
@@ -219,7 +219,7 @@
 TALL = 24
 
 
-def near_kernel(place, outer, own, partner, fl, ml, ops_hbm, fine_out, mid_out, head, ops, full, rows, mids, mid_rows, xa, xb, acc_a, acc_b, sems):
+def near_kernel(place, outer, own, partner, fl, ml, ops_hbm, fine_out, mid_out, tails, ops, full, rows, mids, mid_rows, xa, xb, acc_a, acc_b, sems):
     slots, n = ops.shape[0], ops.shape[1]
     groups = -(-slots // GROUP)
     size = [min(GROUP, slots - k * GROUP) for k in range(groups)]
@@ -304,7 +304,10 @@
         if k + 1 < groups:
             load(k + 1, size[k + 1], bufs[(k + 1) % 2])
         use(k, size[k], bufs[k % 2])
-    head[...] = ops[:, pl.ds(0, TALL), :]
+    for k in range(tails.shape[0]):
+        parts = [ops[j, :, pl.ds(128, TAIL)] for j in range(3 * k, min(3 * k + 3, slots))]
+        parts.append(jnp.zeros((n, 128 - TAIL * len(parts)), F32))
+        tails[k] = jnp.concatenate(parts, axis=1)
     fine_out[...] = acc_a[:, pl.ds(0, 128)] + acc_b[...]
     folded = acc_a[:, pl.ds(128, 128)]
     for shift in (64, 32, 16):
@@ -317,7 +320,7 @@
     vm = pl.BlockSpec(memory_space=VMEM)
     return pl.pallas_call(
         near_kernel,
-        out_shape=(VMEM((n, 128), F32),) * 2 + (VMEM((slots, TALL, n), F32),),
+        out_shape=(VMEM((n, 128), F32),) * 2 + (VMEM((-(-slots // 3), n, 128), F32),),
         in_specs=[pl.BlockSpec(memory_space=pltpu.SMEM)] + [vm] * 5 + [pl.BlockSpec(memory_space=pltpu.HBM)],
         out_specs=(vm,) * 3,
         scratch_shapes=[
@@ -337,21 +340,22 @@
     )(place, outer, own, partner, fine_list, mid_list, in_hbm(ops))
 
 
-UNROLL = 8
+UNROLL = 1
 FIRST = (3, 2, 2)
 
 
 def far_kernel(
-    place, listed_ref, table, uph, upl, fine_term, mid_term, head, dnh_hbm, dnl_hbm, ops_hbm, out,
-    ops, dnh, dnl, tiles, rows, upper, chosen, top_col, upper_col, listed, sems, down_sems, list_sem,
+    place, listed_ref, table, uph, upl, fine_term, mid_term, tails, dnh_hbm, dnl_hbm, ops_hbm, out,
+    ops, dnh, dnl, tiles, rows, upper, tail_rows, chosen, chosen_tails, top_col, upper_col, listed, sems, down_sems, list_sem,
 ):
     slots, n = ops.shape[0], ops.shape[1]
+    triples = tails.shape[0]
     list_load = pltpu.make_async_copy(listed_ref, listed, list_sem)
     list_load.start()
     loads = []
-    for k, at in enumerate(range(TALL, n, TALL)):
-        where = (slice(None), pl.ds(at, min(TALL, n - at)))
-        loads.append(pltpu.make_async_copy(ops_hbm.at[where], ops.at[where], sems.at[k]))
+    for k, at in enumerate(range(0, n, TALL)):
+        where = (slice(None), pl.ds(at, min(TALL, n - at)), pl.ds(0, 128))
+        loads.append(pltpu.make_async_copy(ops_hbm.at[where], ops.at[where[:2]], sems.at[k]))
     down_loads = [
         pltpu.make_async_copy(source, target, down_sems.at[k])
         for k, (source, target) in enumerate(((dnh_hbm, dnh), (dnl_hbm, dnl)))
@@ -392,31 +396,50 @@
     upper[pl.ds(0, parents), :] = total
     begin(FIRST[2])
     list_load.wait()
-
-    def choose(j):
-        for t in range(2):
-            chosen[3 * j + t] = jnp.broadcast_to(rows[pl.ds(listed[t, j], 1), :], (8, n))
-        chosen[3 * j + 2] = jnp.broadcast_to(upper[pl.ds(listed[2, j], 1), :], (8, n))
+    lane = lax.broadcasted_iota(I32, (1, 128), 1)
+    for source, at in ((rows, 0), (upper, rows.shape[0])):
+        size = source.shape[0]
+        rest = jnp.concatenate([source[:, pl.ds(128, TAIL)], jnp.zeros((size, 128 - TAIL), F32)], axis=1)
+        for i in range(3):
+            tail_rows[i, pl.ds(at, size), :] = pltpu.roll(rest, TAIL * i, 1) if i else rest
+
+    def choose(k, count):
+        for t in range(3):
+            source, shift = (rows, 0) if t < 2 else (upper, rows.shape[0])
+            tail = None
+            for i in range(count):
+                index = listed[t, 3 * k + i]
+                chosen[9 * k + 3 * i + t] = jnp.broadcast_to(source[pl.ds(index, 1), :][:, :128], (8, 128))
+                part = tail_rows[i, pl.ds(index + shift, 1), :]
+                tail = part if tail is None else tail + part
+            chosen_tails[3 * k + t] = jnp.broadcast_to(tail, (8, 128))
 
     def some(i, carry):
         for k in range(UNROLL):
-            choose(i * UNROLL + k)
+            choose(i * UNROLL + k, 3)
         return carry
 
-    lax.fori_loop(0, slots // UNROLL, some, 0)
-    for j in range(slots // UNROLL * UNROLL, slots):
-        choose(j)
+    lax.fori_loop(0, slots // 3 // UNROLL, some, 0)
+    for k in range(slots // 3 // UNROLL * UNROLL, triples):
+        choose(k, min(3, slots - 3 * k))
     begin(len(queue))
 
-    def block(start, size, source=ops):
+    def block(start, size):
         edges = [(at, min(8, size - at)) for at in range(0, size, 8)]
-        sums = [[jnp.zeros((height, n), F32)] * 3 for _, height in edges]
-        for j in range(slots):
-            factors = [chosen[3 * j + t] for t in range(3)]
-            for part, (at, height) in zip(sums, edges, strict=True):
-                piece = source[j, pl.ds(start + at, height), :]
+        sums = [[jnp.zeros((height, 128), F32)] * 3 for _, height in edges]
+
+        def add(pieces, factors):
+            for part, piece, (_, height) in zip(sums, pieces, edges, strict=True):
                 for t in range(3):
                     part[t] = part[t] + piece * factors[t][:height]
+
+        for j in range(slots):
+            add([ops[j, pl.ds(start + at, height), :] for at, height in edges], [chosen[3 * j + t] for t in range(3)])
+        for k in range(triples):
+            add(
+                [tails[k, pl.ds(start + at, height), :] for at, height in edges],
+                [chosen_tails[3 * k + t] for t in range(3)],
+            )
         for part, (at, height) in zip(sums, edges, strict=True):
             s0, s1, s2 = [jnp.sum(s, axis=1, keepdims=True) for s in part]
             lane = lax.broadcasted_iota(I32, (height, 128), 1)
@@ -426,13 +449,12 @@
 
     def step(i, carry):
         at = pl.multiple_of(i * TALL, TALL)
-        where = (slice(None), pl.ds(at, TALL))
-        pltpu.make_async_copy(ops_hbm.at[where], ops.at[where], sems.at[i - 1]).wait()
+        where = (slice(None), pl.ds(at, TALL), pl.ds(0, 128))
+        pltpu.make_async_copy(ops_hbm.at[where], ops.at[where[:2]], sems.at[i]).wait()
         block(at, TALL)
         return carry
 
-    block(0, TALL, head)
-    lax.fori_loop(1, n // TALL, step, 0)
+    lax.fori_loop(0, n // TALL, step, 0)
     if n % TALL:
         loads[-1].wait()
         block(n // TALL * TALL, n % TALL)
@@ -450,7 +472,7 @@
         out[i] = local_fine
 
 
-def far_terms(place, listed, table, uph, upl, dnh, dnl, fine_term, mid_term, head, ops, copies):
+def far_terms(place, listed, table, uph, upl, dnh, dnl, fine_term, mid_term, tails, ops, copies):
     slots, n = ops.shape[0], ops.shape[1]
     parents = table.shape[0] // LINE_ROWS * 6
     vm, sm = pl.BlockSpec(memory_space=VMEM), pl.BlockSpec(memory_space=pltpu.SMEM)
@@ -460,13 +482,15 @@
         in_specs=[sm] + [vm] * 7 + [pl.BlockSpec(memory_space=pltpu.HBM)] * 3,
         out_specs=vm,
         scratch_shapes=[
-            pltpu.VMEM((slots, n, n), F32),
+            pltpu.VMEM((slots, n, 128), F32),
             pltpu.VMEM((8, n, n), BF16),
             pltpu.VMEM((8, n, n), BF16),
             pltpu.VMEM((4, 4 * parents, 128), F32),
             pltpu.VMEM((8 * PITCH, n), F32),
             pltpu.VMEM((parents + 8, n), F32),
-            pltpu.VMEM((3 * slots, 8, n), F32),
+            pltpu.VMEM((3, 8 * PITCH + parents + 8, 128), F32),
+            pltpu.VMEM((3 * slots, 8, 128), F32),
+            pltpu.VMEM((slots + 3, 8, 128), F32),
             pltpu.VMEM((n, 128), F32),
             pltpu.VMEM((n, 128), F32),
             pltpu.SMEM(listed.shape, I32),
@@ -477,7 +501,7 @@
         compiler_params=pltpu.CompilerParams(vmem_limit_bytes=20 << 20),
         name="far_terms",
     )(
-        place, listed, table, uph, upl, fine_term, mid_term, head,
+        place, listed, table, uph, upl, fine_term, mid_term, tails,
         in_hbm(dnh), in_hbm(dnl), in_hbm(ops),
     )
 

time: 85.5 us -> 85 us (level)
  no operation moved by 1% of the time
where the time goes in v7:
time: 85 us; the launch traced here: 84.4 us
  blocking collectives  35.1 us (41%)
  Pallas kernels  24.3 us (29%)
  starting transfers between devices  16 us (19%)
  waiting for transfers between devices  6.03 us (7%)
  local copies, waits for them, and re-layouts  2.22 us (3%)
    all_to_all x2, blocking collectives, exchanged(): lax.all_to_all(copies, axis, split_axis=0, concat_axis=0, tiled=True, axi...  35.1 us
    all_to_all x2, starting transfers between devices, exchanged(): lax.all_to_all(copies, axis, split_axis=0, concat_axis=0, tiled=True, axi...  11 us
    pallas_call x1, Pallas kernels, far_terms(): pl.pallas_call(far_kernel, out_shape=VMEM((copies, n, 128), F32), in_spec...  6.76 us
    pallas_call x1, Pallas kernels, near_terms(): pl.pallas_call(near_kernel, out_shape=(VMEM((n, 128), F32),) * 2 + (VMEM(...  6.67 us
    all_to_all x2, waiting for transfers between devices, exchanged(): lax.all_to_all(copies, axis, split_axis=0, concat_axis=0, tiled=True, axi...  5.78 us
    ppermute x1, starting transfers between devices, shards(): lax.ppermute(own, DOM, [(i, i + 2 * (i % 2) - 1) for i in range(1, slabs...  3.08 us
    pallas_call x1, Pallas kernels, split_down(): pl.pallas_call(split_kernel, out_shape=(pltpu.HBM((8, n, n), BF16),) * 2,...  2.81 us
    pallas_call x1, Pallas kernels, monomials(): pl.pallas_call(monomial_kernel, grid=(particles // width,), out_shape=(pl...  2.41 us
  transfers between devices with their start and end apart: 4, of which 2 were waited for; matrix products, arithmetic and copies ran while one was open for 0% of the time, Pallas kernels for 14%

profile of v7, /device:TPU:8, one launch (start us, length us, event | category | flops | bytes accessed | tf_op | source)
XLA Modules:
  0.0 84.4 jit_solution(7926995070809633800)
XLA Ops:
  0.6 1.8 %prepare.1 = (f32[4,165,1,128]{3,2,1,0:T(1,128)}, bf16[8,165,165]{2,1,0:T(8,128)(2,1)S(1)}, bf16[8,165,165]{2,1,0:T(8,128)(2,1)S(1)}, s32[3,47]{1,0:T(4,128)S(1)...) custom-call(s32[1]{0:T(128)} %bitcast.place, f32[165,1,128]{2,1,0:T(1,128)} %bitcast.13, f32[165,8,165]{2,1,0:T(8,128)} %bitcast.11, ...), custom_call_target="tpu_custom_call" | custom-call | tf_op jit(solution)/shard_map/prepare/pallas_call | solution.py:104
  2.5 11.8 %all_to_all.20.parts = f32[4,165,1,128]{3,2,1,0:T(1,128)S(1)} all-to-all(f32[4,165,1,128]{3,2,1,0:T(1,128)} %get-tuple-element.20), channel_id=1, replica_groups=mesh['dom_0'=8,'dom_1'=24,'sub'=4] {'sub'}, dimensions={0} | all-to-all | bytes 675840 | tf_op jit(solution)/shard_map/all_to_all | solution.py:578
  14.3 1.8 %own_moments.1 = (f32[200,128]{1,0:T(8,128)S(1)}, f32[24,1,384]{2,1,0:T(1,128)S(1)}) custom-call(f32[4,165,1,128]{3,2,1,0:T(1,128)S(1)} %all_to_all.20.parts, bf16[8,165,165]{2,1,0:T(8,128)(2,1)S(1)} %get-tuple-element.21.uph, bf16[8,165,165]{2,1,0:T(8,128)(2,1)S(1)} %get-tuple-element.22.upl), custom_call_target="tpu_custom_call" | custom-call | tf_op jit(solution)/shard_map/own_moments/pallas_call | solution.py:180
  16.1 23.3 %all_to_all.21.line = f32[24,1,384]{2,1,0:T(1,128)S(1)} all-to-all(f32[24,1,384]{2,1,0:T(1,128)S(1)} %get-tuple-element.23), channel_id=1, replica_groups={{92,88,84,80,76,72,68,64,60,56,52,48,44,40,36,32,28,24,20,16,12,8,4,0},..., dimensions={0} | all-to-all | bytes 73728 | tf_op jit(solution)/shard_map/all_to_all | solution.py:578
  39.4 0.8 line_copies.1
  40.2 7.5 %all-to-all-start.2 = ((f32[8,64,128]{2,1,0:T(8,128)}), f32[8,64,128]{2,1,0:T(8,128)S(1)}, u32[]{:S(2)}, u32[]{:S(2)}) async-start(f32[8,64,128]{2,1,0:T(8,128)} %line_copies.1), calls=%async_computation.2 | async-start | bytes 524288 | tf_op jit(solution)/shard_map/all_to_all | solution.py:578
  47.7 3.1 %collective-permute-start = (f32[200,128]{1,0:T(8,128)S(1)}, f32[200,128]{1,0:T(8,128)S(1)}, u32[]{:S(2)}, u32[]{:S(2)}) collective-permute-start(f32[200,128]{1,0:T(8,128)S(1)} %get-tuple-element.24.own), channel_id=1, source_target_pairs={{4,8},{8,4},{12,16},{16,12},{20,24},{24,20},{28,32},{32,28},{36,40... | collective-permute-start | bytes 307208 | tf_op jit(solution)/shard_map/ppermute | solution.py:609
  50.8 1.9 %collective-permute-start.1 = (f32[200,128]{1,0:T(8,128)S(1)}, f32[200,128]{1,0:T(8,128)S(1)}, u32[]{:S(2)}, u32[]{:S(2)}) collective-permute-start(f32[200,128]{1,0:T(8,128)S(1)} %get-tuple-element.24.own), channel_id=1, source_target_pairs={{0,4},{4,0},{8,12},{12,8},{16,20},{20,16},{24,28},{28,24},{32,36},... | collective-permute-start | bytes 307208 | tf_op jit(solution)/shard_map/ppermute | solution.py:610
  52.8 2.8 %split_down.1 = (bf16[8,165,165]{2,1,0:T(8,128)(2,1)}, bf16[8,165,165]{2,1,0:T(8,128)(2,1)}) custom-call(f32[165,8,165]{2,1,0:T(8,128)} %bitcast.12), custom_call_target="tpu_custom_call" | custom-call | tf_op jit(solution)/shard_map/split_down/pallas_call | solution.py:141
  55.6 0.2 collective-permute-done.outer
  55.8 0.0 collective-permute-done.1.partner
  55.8 6.7 %near_terms.1 = (f32[165,128]{1,0:T(8,128)S(1)}, f32[165,128]{1,0:T(8,128)S(1)}, f32[16,165,128]{2,1,0:T(8,128)S(1)}) custom-call(s32[1]{0:T(128)} %bitcast.place, f32[200,128]{1,0:T(8,128)S(1)} %collective-permute-done.outer, f32[200,128]{1,0:T(8,128)S(1)} %get-tuple-element.24.own, f32[200,128]{1,0:T(8,128)S(1)} %collective-permute-done.1.partner, ...), custom_call_target="tpu_custom_call" | custom-call | tf_op jit(solution)/shard_map/near_terms/pallas_call | solution.py:321
  62.5 0.0 all-to-all-done.2
  62.5 0.0 copy-start.2
  62.5 0.0 copy-start.3
  62.5 0.0 copy-start.4
  62.5 6.8 %far_terms.1 = f32[4,165,128]{2,1,0:T(8,128)} custom-call(s32[1]{0:T(128)} %bitcast.place, s32[3,47]{1,0:T(4,128)S(1)} %get-tuple-element.19.listed_ref, f32[512,128]{1,0:T(8,128)S(1)} %bitcast.9, bf16[8,165,165]{2,1,0:T(8,128)(2,1)S(1)} %get-tuple-element.21.uph, bf16[8,165,165]{2,1,0:T(8,128)(2,1)S(1)} %get-tuple-element.22.upl, ...), custom_call_target="tpu_custom_call" | custom-call | tf_op jit(solution)/shard_map/far_terms/pallas_call | solution.py:479
  69.3 3.5 %all-to-all-start.3 = ((f32[4,165,128]{2,1,0:T(8,128)}), f32[4,165,128]{2,1,0:T(8,128)S(1)}, u32[]{:S(2)}, u32[]{:S(2)}) async-start(f32[4,165,128]{2,1,0:T(8,128)} %far_terms.1), calls=%async_computation.3 | async-start | bytes 688128 | tf_op jit(solution)/shard_map/all_to_all | solution.py:578
  72.8 0.0 copy-done.2
  72.8 0.0 copy-done.3
  72.8 2.4 %monomials.1 = (bf16[165,2048]{1,0:T(8,128)(2,1)}, bf16[165,2048]{1,0:T(8,128)(2,1)}) custom-call(s32[165,3]{1,0:T(8,128)S(1)} %copy-done.2, f32[3,2048]{1,0:T(4,128)S(1)} %copy-done.3), custom_call_target="tpu_custom_call" | custom-call | tf_op jit(solution)/shard_map/monomials/pallas_call | solution.py:534
  75.2 5.8 %all-to-all-done.3.parts = f32[4,165,128]{2,1,0:T(8,128)S(1)} async-done(((f32[4,165,128]{2,1,0:T(8,128)}), f32[4,165,128]{2,1,0:T(8,128)S(1)}, u32[]{:S(2)}, u32[]{:S(2)}) %all-to-all-start.3) | async-done | bytes 337952 | tf_op jit(solution)/shard_map/all_to_all | solution.py:578
  81.0 0.0 copy-done.4
  81.0 0.0 copy-start
  81.0 1.1 %copy-done = bf16[165,2048]{1,0:T(8,128)(2,1)S(1)} copy-done((bf16[165,2048]{1,0:T(8,128)(2,1)S(1)}, bf16[165,2048]{1,0:T(8,128)(2,1)}, u32[]{:S(2)}) %copy-start) | copy-done | bytes 675864
  82.1 0.0 copy-start.1
  82.1 1.1 %copy-done.1 = bf16[165,2048]{1,0:T(8,128)(2,1)S(1)} copy-done((bf16[165,2048]{1,0:T(8,128)(2,1)S(1)}, bf16[165,2048]{1,0:T(8,128)(2,1)}, u32[]{:S(2)}) %copy-start.1) | copy-done | bytes 675864
  83.2 1.2 %potentials.1 = (f32[165,128]{1,0:T(8,128)}, f32[1,2048]{1,0:T(1,128)}) custom-call(s32[1]{0:T(128)} %bitcast.place, f32[4,165,128]{2,1,0:T(8,128)S(1)} %all-to-all-done.3.parts, s32[1,2048]{1,0:T(1,128)S(1)} %bitcast.10, bf16[165,2048]{1,0:T(8,128)(2,1)S(1)} %copy-done, bf16[165,2048]{1,0:T(8,128)(2,1)S(1)} %copy-done.1), custom_call_target="tpu_custom_call" | custom-call | tf_op jit(solution)/shard_map/potentials/pallas_call | solution.py:562
Async XLA Ops:
  40.2 22.3 %all-to-all-start.2 = ((f32[8,64,128]{2,1,0:T(8,128)}), f32[8,64,128]{2,1,0:T(8,128)S(1)}, u32[]{:S(2)}, u32[]{:S(2)}) async-start(f32[8,64,128]{2,1,0:T(8,128)} %line_copies.1), calls=%async_computation.2 | async-start | bytes 524288 | tf_op jit(solution)/shard_map/all_to_all | solution.py:578
  47.7 8.1 %collective-permute-start = (f32[200,128]{1,0:T(8,128)S(1)}, f32[200,128]{1,0:T(8,128)S(1)}, u32[]{:S(2)}, u32[]{:S(2)}) collective-permute-start(f32[200,128]{1,0:T(8,128)S(1)} %get-tuple-element.24.own), channel_id=1, source_target_pairs={{4,8},{8,4},{12,16},{16,12},{20,24},{24,20},{28,32},{32,28},{36,40... | collective-permute-start | bytes 307208 | tf_op jit(solution)/shard_map/ppermute | solution.py:609
  50.8 5.0 %collective-permute-start.1 = (f32[200,128]{1,0:T(8,128)S(1)}, f32[200,128]{1,0:T(8,128)S(1)}, u32[]{:S(2)}, u32[]{:S(2)}) collective-permute-start(f32[200,128]{1,0:T(8,128)S(1)} %get-tuple-element.24.own), channel_id=1, source_target_pairs={{0,4},{4,0},{8,12},{12,8},{16,20},{20,16},{24,28},{28,24},{32,36},... | collective-permute-start | bytes 307208 | tf_op jit(solution)/shard_map/ppermute | solution.py:610
  62.5 10.3 %copy-start.2 = (s32[165,3]{1,0:T(8,128)S(1)}, s32[165,3]{1,0:T(8,128)}, u32[]{:S(2)}) copy-start(s32[165,3]{1,0:T(8,128)} %constant.14.clone.powers) | copy-start | bytes 5944
  62.5 10.3 %copy-start.3 = (f32[3,2048]{1,0:T(4,128)S(1)}, f32[3,2048]{1,0:T(4,128)}, u32[]{:S(2)}) copy-start(f32[3,2048]{1,0:T(4,128)} %coords.1) | copy-start | bytes 73732
  62.5 18.5 %copy-start.4 = (s32[2048]{0:T(1024)S(1)}, s32[2048]{0:T(1024)}, u32[]{:S(2)}) copy-start(s32[2048]{0:T(1024)} %param.20) | copy-start | bytes 24580
  69.3 11.7 %all-to-all-start.3 = ((f32[4,165,128]{2,1,0:T(8,128)}), f32[4,165,128]{2,1,0:T(8,128)S(1)}, u32[]{:S(2)}, u32[]{:S(2)}) async-start(f32[4,165,128]{2,1,0:T(8,128)} %far_terms.1), calls=%async_computation.3 | async-start | bytes 688128 | tf_op jit(solution)/shard_map/all_to_all | solution.py:578
  81.0 1.1 %copy-start = (bf16[165,2048]{1,0:T(8,128)(2,1)S(1)}, bf16[165,2048]{1,0:T(8,128)(2,1)}, u32[]{:S(2)}) copy-start(bf16[165,2048]{1,0:T(8,128)(2,1)} %get-tuple-element.32.high_ref) | copy-start | bytes 2027524
  82.1 1.1 %copy-start.1 = (bf16[165,2048]{1,0:T(8,128)(2,1)S(1)}, bf16[165,2048]{1,0:T(8,128)(2,1)}, u32[]{:S(2)}) copy-start(bf16[165,2048]{1,0:T(8,128)(2,1)} %get-tuple-element.33.low_ref) | copy-start | bytes 2027524

commit v8 on v7

--- a/solution.py
+++ b/solution.py
@@ -170,8 +170,8 @@
     rows = jnp.transpose(mid)[:16]
     own_ref[pl.ds(MID_AT, 16), :] = rows[:, :128]
     own_ref[pl.ds(MID_AT + 16, 16), pl.ds(0, n - 128)] = rows[:, 128:]
-    rows = jnp.transpose(raised(mid, uph, upl))
-    row = packed(rows[:1], rows[1:2])
+    rows = jnp.transpose(octant_sum(uph, upl, jnp.concatenate(split(mid), axis=1)))
+    row = packed(*(jnp.sum(rows[8 * i : 8 * i + 8], axis=0, keepdims=True) for i in range(2)))
     for i in range(top_ref.shape[0]):
         top_ref[i] = row
 
@@ -216,7 +216,7 @@
 
 
 GROUP = 4
-TALL = 24
+TALL = 88
 
 
 def near_kernel(place, outer, own, partner, fl, ml, ops_hbm, fine_out, mid_out, tails, ops, full, rows, mids, mid_rows, xa, xb, acc_a, acc_b, sems):
@@ -341,7 +341,7 @@
 
 
 UNROLL = 1
-FIRST = (3, 2, 2)
+FIRST = (4, 0, 0)
 
 
 def far_kernel(

time: 85 us -> 84.2 us (level)
  no operation moved by 1% of the time
where the time goes in v8:
time: 84.2 us; the launch traced here: 83.6 us
  blocking collectives  35.1 us (42%)
  Pallas kernels  23.5 us (28%)
  starting transfers between devices  16 us (19%)
  waiting for transfers between devices  6.05 us (7%)
  local copies, waits for them, and re-layouts  2.22 us (3%)
    all_to_all x2, blocking collectives, exchanged(): lax.all_to_all(copies, axis, split_axis=0, concat_axis=0, tiled=True, axi...  35.1 us
    all_to_all x2, starting transfers between devices, exchanged(): lax.all_to_all(copies, axis, split_axis=0, concat_axis=0, tiled=True, axi...  11 us
    pallas_call x1, Pallas kernels, near_terms(): pl.pallas_call(near_kernel, out_shape=(VMEM((n, 128), F32),) * 2 + (VMEM(...  6.65 us
    pallas_call x1, Pallas kernels, far_terms(): pl.pallas_call(far_kernel, out_shape=VMEM((copies, n, 128), F32), in_spec...  6.05 us
    all_to_all x2, waiting for transfers between devices, exchanged(): lax.all_to_all(copies, axis, split_axis=0, concat_axis=0, tiled=True, axi...  5.79 us
    ppermute x1, starting transfers between devices, shards(): lax.ppermute(own, DOM, [(i, i + 2 * (i % 2) - 1) for i in range(1, slabs...  3.05 us
    pallas_call x1, Pallas kernels, split_down(): pl.pallas_call(split_kernel, out_shape=(pltpu.HBM((8, n, n), BF16),) * 2,...  2.81 us
    pallas_call x1, Pallas kernels, monomials(): pl.pallas_call(monomial_kernel, grid=(particles // width,), out_shape=(pl...  2.41 us
  transfers between devices with their start and end apart: 4, of which 2 were waited for; matrix products, arithmetic and copies ran while one was open for 0% of the time, Pallas kernels for 14%

profile of v8, /device:TPU:8, one launch (start us, length us, event | category | flops | bytes accessed | tf_op | source)
XLA Modules:
  0.0 83.6 jit_solution(16969517916632684706)
XLA Ops:
  0.6 1.8 %prepare.1 = (f32[4,165,1,128]{3,2,1,0:T(1,128)}, bf16[8,165,165]{2,1,0:T(8,128)(2,1)S(1)}, bf16[8,165,165]{2,1,0:T(8,128)(2,1)S(1)}, s32[3,47]{1,0:T(4,128)S(1)...) custom-call(s32[1]{0:T(128)} %bitcast.place, f32[165,1,128]{2,1,0:T(1,128)} %bitcast.13, f32[165,8,165]{2,1,0:T(8,128)} %bitcast.11, ...), custom_call_target="tpu_custom_call" | custom-call | tf_op jit(solution)/shard_map/prepare/pallas_call | solution.py:104
  2.5 11.8 %all_to_all.20.parts = f32[4,165,1,128]{3,2,1,0:T(1,128)S(1)} all-to-all(f32[4,165,1,128]{3,2,1,0:T(1,128)} %get-tuple-element.20), channel_id=1, replica_groups=mesh['dom_0'=8,'dom_1'=24,'sub'=4] {'sub'}, dimensions={0} | all-to-all | bytes 675840 | tf_op jit(solution)/shard_map/all_to_all | solution.py:578
  14.3 1.7 %own_moments.1 = (f32[200,128]{1,0:T(8,128)S(1)}, f32[24,1,384]{2,1,0:T(1,128)S(1)}) custom-call(f32[4,165,1,128]{3,2,1,0:T(1,128)S(1)} %all_to_all.20.parts, bf16[8,165,165]{2,1,0:T(8,128)(2,1)S(1)} %get-tuple-element.21.uph, bf16[8,165,165]{2,1,0:T(8,128)(2,1)S(1)} %get-tuple-element.22.upl), custom_call_target="tpu_custom_call" | custom-call | tf_op jit(solution)/shard_map/own_moments/pallas_call | solution.py:180
  16.0 23.3 %all_to_all.21.line = f32[24,1,384]{2,1,0:T(1,128)S(1)} all-to-all(f32[24,1,384]{2,1,0:T(1,128)S(1)} %get-tuple-element.23), channel_id=1, replica_groups={{92,88,84,80,76,72,68,64,60,56,52,48,44,40,36,32,28,24,20,16,12,8,4,0},..., dimensions={0} | all-to-all | bytes 73728 | tf_op jit(solution)/shard_map/all_to_all | solution.py:578
  39.3 0.8 line_copies.1
  40.1 7.5 %all-to-all-start.2 = ((f32[8,64,128]{2,1,0:T(8,128)}), f32[8,64,128]{2,1,0:T(8,128)S(1)}, u32[]{:S(2)}, u32[]{:S(2)}) async-start(f32[8,64,128]{2,1,0:T(8,128)} %line_copies.1), calls=%async_computation.2 | async-start | bytes 524288 | tf_op jit(solution)/shard_map/all_to_all | solution.py:578
  47.7 3.1 %collective-permute-start = (f32[200,128]{1,0:T(8,128)S(1)}, f32[200,128]{1,0:T(8,128)S(1)}, u32[]{:S(2)}, u32[]{:S(2)}) collective-permute-start(f32[200,128]{1,0:T(8,128)S(1)} %get-tuple-element.24.own), channel_id=1, source_target_pairs={{4,8},{8,4},{12,16},{16,12},{20,24},{24,20},{28,32},{32,28},{36,40... | collective-permute-start | bytes 307208 | tf_op jit(solution)/shard_map/ppermute | solution.py:609
  50.7 1.9 %collective-permute-start.1 = (f32[200,128]{1,0:T(8,128)S(1)}, f32[200,128]{1,0:T(8,128)S(1)}, u32[]{:S(2)}, u32[]{:S(2)}) collective-permute-start(f32[200,128]{1,0:T(8,128)S(1)} %get-tuple-element.24.own), channel_id=1, source_target_pairs={{0,4},{4,0},{8,12},{12,8},{16,20},{20,16},{24,28},{28,24},{32,36},... | collective-permute-start | bytes 307208 | tf_op jit(solution)/shard_map/ppermute | solution.py:610
  52.6 2.8 %split_down.1 = (bf16[8,165,165]{2,1,0:T(8,128)(2,1)}, bf16[8,165,165]{2,1,0:T(8,128)(2,1)}) custom-call(f32[165,8,165]{2,1,0:T(8,128)} %bitcast.12), custom_call_target="tpu_custom_call" | custom-call | tf_op jit(solution)/shard_map/split_down/pallas_call | solution.py:141
  55.5 0.3 collective-permute-done.outer
  55.7 0.0 collective-permute-done.1.partner
  55.7 6.7 %near_terms.1 = (f32[165,128]{1,0:T(8,128)S(1)}, f32[165,128]{1,0:T(8,128)S(1)}, f32[16,165,128]{2,1,0:T(8,128)S(1)}) custom-call(s32[1]{0:T(128)} %bitcast.place, f32[200,128]{1,0:T(8,128)S(1)} %collective-permute-done.outer, f32[200,128]{1,0:T(8,128)S(1)} %get-tuple-element.24.own, f32[200,128]{1,0:T(8,128)S(1)} %collective-permute-done.1.partner, ...), custom_call_target="tpu_custom_call" | custom-call | tf_op jit(solution)/shard_map/near_terms/pallas_call | solution.py:321
  62.4 0.0 all-to-all-done.2
  62.4 0.0 copy-start.2
  62.4 0.0 copy-start.3
  62.4 0.0 copy-start.4
  62.4 6.0 %far_terms.1 = f32[4,165,128]{2,1,0:T(8,128)} custom-call(s32[1]{0:T(128)} %bitcast.place, s32[3,47]{1,0:T(4,128)S(1)} %get-tuple-element.19.listed_ref, f32[512,128]{1,0:T(8,128)S(1)} %bitcast.9, bf16[8,165,165]{2,1,0:T(8,128)(2,1)S(1)} %get-tuple-element.21.uph, bf16[8,165,165]{2,1,0:T(8,128)(2,1)S(1)} %get-tuple-element.22.upl, ...), custom_call_target="tpu_custom_call" | custom-call | tf_op jit(solution)/shard_map/far_terms/pallas_call | solution.py:479
  68.5 3.5 %all-to-all-start.3 = ((f32[4,165,128]{2,1,0:T(8,128)}), f32[4,165,128]{2,1,0:T(8,128)S(1)}, u32[]{:S(2)}, u32[]{:S(2)}) async-start(f32[4,165,128]{2,1,0:T(8,128)} %far_terms.1), calls=%async_computation.3 | async-start | bytes 688128 | tf_op jit(solution)/shard_map/all_to_all | solution.py:578
  72.0 0.0 copy-done.2
  72.0 0.0 copy-done.3
  72.0 2.4 %monomials.1 = (bf16[165,2048]{1,0:T(8,128)(2,1)}, bf16[165,2048]{1,0:T(8,128)(2,1)}) custom-call(s32[165,3]{1,0:T(8,128)S(1)} %copy-done.2, f32[3,2048]{1,0:T(4,128)S(1)} %copy-done.3), custom_call_target="tpu_custom_call" | custom-call | tf_op jit(solution)/shard_map/monomials/pallas_call | solution.py:534
  74.4 5.8 %all-to-all-done.3.parts = f32[4,165,128]{2,1,0:T(8,128)S(1)} async-done(((f32[4,165,128]{2,1,0:T(8,128)}), f32[4,165,128]{2,1,0:T(8,128)S(1)}, u32[]{:S(2)}, u32[]{:S(2)}) %all-to-all-start.3) | async-done | bytes 337952 | tf_op jit(solution)/shard_map/all_to_all | solution.py:578
  80.2 0.0 copy-done.4
  80.2 0.0 copy-start
  80.2 1.1 %copy-done = bf16[165,2048]{1,0:T(8,128)(2,1)S(1)} copy-done((bf16[165,2048]{1,0:T(8,128)(2,1)S(1)}, bf16[165,2048]{1,0:T(8,128)(2,1)}, u32[]{:S(2)}) %copy-start) | copy-done | bytes 675864
  81.3 0.0 copy-start.1
  81.3 1.1 %copy-done.1 = bf16[165,2048]{1,0:T(8,128)(2,1)S(1)} copy-done((bf16[165,2048]{1,0:T(8,128)(2,1)S(1)}, bf16[165,2048]{1,0:T(8,128)(2,1)}, u32[]{:S(2)}) %copy-start.1) | copy-done | bytes 675864
  82.4 1.2 %potentials.1 = (f32[165,128]{1,0:T(8,128)}, f32[1,2048]{1,0:T(1,128)}) custom-call(s32[1]{0:T(128)} %bitcast.place, f32[4,165,128]{2,1,0:T(8,128)S(1)} %all-to-all-done.3.parts, s32[1,2048]{1,0:T(1,128)S(1)} %bitcast.10, bf16[165,2048]{1,0:T(8,128)(2,1)S(1)} %copy-done, bf16[165,2048]{1,0:T(8,128)(2,1)S(1)} %copy-done.1), custom_call_target="tpu_custom_call" | custom-call | tf_op jit(solution)/shard_map/potentials/pallas_call | solution.py:562
Async XLA Ops:
  40.1 22.3 %all-to-all-start.2 = ((f32[8,64,128]{2,1,0:T(8,128)}), f32[8,64,128]{2,1,0:T(8,128)S(1)}, u32[]{:S(2)}, u32[]{:S(2)}) async-start(f32[8,64,128]{2,1,0:T(8,128)} %line_copies.1), calls=%async_computation.2 | async-start | bytes 524288 | tf_op jit(solution)/shard_map/all_to_all | solution.py:578
  47.7 8.1 %collective-permute-start = (f32[200,128]{1,0:T(8,128)S(1)}, f32[200,128]{1,0:T(8,128)S(1)}, u32[]{:S(2)}, u32[]{:S(2)}) collective-permute-start(f32[200,128]{1,0:T(8,128)S(1)} %get-tuple-element.24.own), channel_id=1, source_target_pairs={{4,8},{8,4},{12,16},{16,12},{20,24},{24,20},{28,32},{32,28},{36,40... | collective-permute-start | bytes 307208 | tf_op jit(solution)/shard_map/ppermute | solution.py:609
  50.7 5.0 %collective-permute-start.1 = (f32[200,128]{1,0:T(8,128)S(1)}, f32[200,128]{1,0:T(8,128)S(1)}, u32[]{:S(2)}, u32[]{:S(2)}) collective-permute-start(f32[200,128]{1,0:T(8,128)S(1)} %get-tuple-element.24.own), channel_id=1, source_target_pairs={{0,4},{4,0},{8,12},{12,8},{16,20},{20,16},{24,28},{28,24},{32,36},... | collective-permute-start | bytes 307208 | tf_op jit(solution)/shard_map/ppermute | solution.py:610
  62.4 9.6 %copy-start.2 = (s32[165,3]{1,0:T(8,128)S(1)}, s32[165,3]{1,0:T(8,128)}, u32[]{:S(2)}) copy-start(s32[165,3]{1,0:T(8,128)} %constant.14.clone.powers) | copy-start | bytes 5944
  62.4 9.6 %copy-start.3 = (f32[3,2048]{1,0:T(4,128)S(1)}, f32[3,2048]{1,0:T(4,128)}, u32[]{:S(2)}) copy-start(f32[3,2048]{1,0:T(4,128)} %coords.1) | copy-start | bytes 73732
  62.4 17.8 %copy-start.4 = (s32[2048]{0:T(1024)S(1)}, s32[2048]{0:T(1024)}, u32[]{:S(2)}) copy-start(s32[2048]{0:T(1024)} %param.20) | copy-start | bytes 24580
  68.5 11.7 %all-to-all-start.3 = ((f32[4,165,128]{2,1,0:T(8,128)}), f32[4,165,128]{2,1,0:T(8,128)S(1)}, u32[]{:S(2)}, u32[]{:S(2)}) async-start(f32[4,165,128]{2,1,0:T(8,128)} %far_terms.1), calls=%async_computation.3 | async-start | bytes 688128 | tf_op jit(solution)/shard_map/all_to_all | solution.py:578
  80.2 1.1 %copy-start = (bf16[165,2048]{1,0:T(8,128)(2,1)S(1)}, bf16[165,2048]{1,0:T(8,128)(2,1)}, u32[]{:S(2)}) copy-start(bf16[165,2048]{1,0:T(8,128)(2,1)} %get-tuple-element.32.high_ref) | copy-start | bytes 2027524
  81.3 1.1 %copy-start.1 = (bf16[165,2048]{1,0:T(8,128)(2,1)S(1)}, bf16[165,2048]{1,0:T(8,128)(2,1)}, u32[]{:S(2)}) copy-start(bf16[165,2048]{1,0:T(8,128)(2,1)} %get-tuple-element.33.low_ref) | copy-start | bytes 2027524
